TPU v7x, 256 devices: a 2x2x32 block of a 4x8x32 slice. The times are simulated.
256 devices in a mesh: shots: 4 (over y, x), gx: 32 (over z), gy: 2 (over core).
Axes of the slice: x: 2, y: 2, z: 32, core: 2. Of those that a mesh axis runs over, the one named last changes fastest.
The devices are a block of a 4x8x32 slice.
Arguments:
- pressure: float32 [128, 1024, 256], P(None, ('shots', 'gx'), 'gy'), parts along dimension 1, may hold values from -6 to 6
- pressure_prior: float32 [128, 1024, 256], P(None, ('shots', 'gx'), 'gy'), parts along dimension 1, may hold values from -6 to 6
- courant_square: bfloat16 [128, 256, 256], P(None, 'gx', 'gy'), may hold values from 0.049804688 to 0.1796875
- wavelet: float32 [64], P('shots'), parts along dimension 0, may hold values from -4 to 4
- delay_steps: int32 [1024, 256], P(('shots', 'gx'), 'gy'), parts along dimension 0, may hold values from 0 to 7
- source_depth: int32 [1024, 256], P(('shots', 'gx'), 'gy'), parts along dimension 0, may hold values from 4 to 31
- receiver_depth: int32 [1024, 256], P(('shots', 'gx'), 'gy'), parts along dimension 0, may hold values from 0 to 31
- receiver_field: float32 [128, 1024, 256], P(None, ('shots', 'gx'), 'gy'), parts along dimension 1, may hold values from -6 to 6
Outputs:
- pressure_final: float32 [128, 1024, 256], P(None, ('shots', 'gx'), 'gy'), parts along dimension 1
- image: float32 [128, 1024, 256], P('gx', 'shots', 'gy'), parts along dimension 1
There are 4 independent parts, one for each index of `shots`. A program takes and returns all parts, laid end to end along the dimension named above; an argument that names none is the same for every part. Nothing has to cross between parts.
All inputs are finite; a program needn't handle non-finite values.
Results may differ from a plain program's by a relative error of at most 0.00035.
Values sent between devices are 32-bit elements; how exact they have to be, the bound alone decides.
No kernel may reach another device: no remote copies, remote signals or barrier semaphores. Data moves between devices by JAX's collectives and lax.ppermute only.
A program may use at most 64 MiB of HBM per device.

v0:
```python
import jax
import jax.numpy as jnp
from jax import lax
from jax.sharding import PartitionSpec as P

STEPS = 8


CENTER = -205.0 / 72.0
COEFS = (1.6, -0.2, 8.0 / 315.0, -1.0 / 560.0)


def padded_2(shard, sides, width):
    edges = {}
    for axis, dim in sides:
        size, length = (lax.axis_size(axis), shard.shape[dim])
        up = [(i, (i + 1) % size) for i in range(size - 1)]
        last = lax.slice_in_dim(shard, length - width, length, axis=dim)
        leading = lax.slice_in_dim(shard, 0, width, axis=dim)
        edges[dim] = (
            lax.ppermute(last, axis, up),
            lax.ppermute(leading, axis, [(b, a) for a, b in up]),
        )
    done = []
    for _, dim in sides:
        low, high = edges[dim]
        around = [(width, width) if d in done else (0, 0) for d in range(shard.ndim)]
        shard = jnp.concatenate([jnp.pad(low, around), shard, jnp.pad(high, around)], axis=dim)
        done.append(dim)
    return shard


def laplacian(field):
    depth, width, length = field.shape
    sides = padded_2(field, (("gx", 1), ("gy", 2)), 4)
    deep = jnp.pad(field, ((4, 4), (0, 0), (0, 0)))
    total = 3.0 * CENTER * field
    for k in range(1, 5):
        near = deep[4 + k : 4 + k + depth] + deep[4 - k : 4 - k + depth]
        near = (
            near
            + sides[:, 4 + k : 4 + k + width, 4 : 4 + length]
            + sides[:, 4 - k : 4 - k + width, 4 : 4 + length]
        )
        near = (
            near
            + sides[:, 4 : 4 + width, 4 + k : 4 + k + length]
            + sides[:, 4 : 4 + width, 4 - k : 4 - k + length]
        )
        total = total + COEFS[k - 1] * near
    return total


def injection(step, wavelet, delay_steps, source_depth, depth):
    picks = jnp.arange(wavelet.shape[0], dtype=jnp.int32)
    onehot = (picks[:, None, None] == (delay_steps + step)[None]).astype(jnp.float32)
    amplitude = jnp.sum(onehot * wavelet[:, None, None], axis=0)
    levels = jnp.arange(depth, dtype=jnp.int32)[:, None, None]
    return jnp.where(levels == source_depth[None], amplitude[None], jnp.zeros_like(amplitude)[None])


def depth_filter(product, padded):
    return 2.0 * product - padded[:-2] - padded[2:]


def shards(
    pressure,
    pressure_prior,
    courant_square,
    wavelet,
    delay_steps,
    source_depth,
    receiver_depth,
    receiver_field,
):
    depth = pressure.shape[0]
    coefficient = courant_square.astype(jnp.float32)
    current, prior = (pressure, pressure_prior)
    for step in range(STEPS):
        nxt = (
            2.0 * current
            - prior
            + coefficient * laplacian(current)
            + injection(step, wavelet, delay_steps, source_depth, depth)
        )
        prior, current = (current, nxt)
    levels = jnp.arange(depth, dtype=jnp.int32)[:, None, None]
    masked = jnp.where(
        levels >= receiver_depth[None], receiver_field, jnp.zeros_like(receiver_field)
    )
    product = current * masked
    rimmed = jnp.pad(product, ((1, 1), (0, 0), (0, 0)))
    filtered = depth_filter(product, rimmed)
    image = lax.all_to_all(filtered, "gx", split_axis=0, concat_axis=1, tiled=True)
    return (current, image)


def solution(mesh):
    in_specs = (
        P(None, ("shots", "gx"), "gy"),
        P(None, ("shots", "gx"), "gy"),
        P(None, "gx", "gy"),
        P("shots"),
        P(("shots", "gx"), "gy"),
        P(("shots", "gx"), "gy"),
        P(("shots", "gx"), "gy"),
        P(None, ("shots", "gx"), "gy"),
    )
    out_specs = (P(None, ("shots", "gx"), "gy"), P("gx", "shots", "gy"))
    return jax.shard_map(shards, mesh=mesh, in_specs=in_specs, out_specs=out_specs, check_vma=False)
```

profile of v0, /device:TPU:46, one launch (start us, length us, event | category | flops | bytes accessed | tf_op | source)
XLA Modules:
  0.0 235.6 jit_solution(14520718467578617591)
XLA Ops:
  0.7 1.3 fusion.273
  3.3 4.7 %collective-permute-start.1 = (f32[128,4,128]{2,1,0:T(4,128)S(1)}, f32[128,4,128]{2,1,0:T(4,128)S(1)}, u32[]{:S(2)}, u32[]{:S(2)}) collective-permute-start(f32[128,4,128]{2,1,0:T(4,128)S(1)} %get-tuple-element.59), channel_id=1, source_target_pairs={{0,2},{2,4},{4,6},{6,8},{8,10},{10,12},{12,14},{14,16},{16,18},{18... | collective-permute-start | bytes 786440 | tf_op jit(solution)/shard_map/ppermute | solution.py:21
  8.0 1.4 fusion.272
  10.8 3.1 %collective-permute-start.3 = (f32[128,8,4]{2,1,0:T(8,128)S(1)}, f32[128,8,4]{2,1,0:T(8,128)S(1)}, u32[]{:S(2)}, u32[]{:S(2)}) collective-permute-start(f32[128,8,4]{2,1,0:T(8,128)S(1)} %get-tuple-element.57), channel_id=1, source_target_pairs={{0,1},{2,3},{4,5},{6,7},{8,9},{10,11},{12,13},{14,15},{16,17},{18,... | collective-permute-start | bytes 49160 | tf_op jit(solution)/shard_map/ppermute | solution.py:21
  15.4 1.4 select_maximum_fusion.15
  16.9 1.6 fusion.1
  18.5 1.3 collective-permute-start.4
  19.8 4.7 %collective-permute-start.5 = (f32[128,4,128]{2,1,0:T(4,128)S(1)}, f32[128,4,128]{2,1,0:T(4,128)S(1)}, u32[]{:S(2)}, u32[]{:S(2)}) collective-permute-start(f32[128,4,128]{2,1,0:T(4,128)S(1)} %get-tuple-element.55), channel_id=1, source_target_pairs={{0,2},{2,4},{4,6},{6,8},{8,10},{10,12},{12,14},{14,16},{16,18},{18... | collective-permute-start | bytes 786440 | tf_op jit(solution)/shard_map/ppermute | solution.py:21
  26.1 3.1 %collective-permute-start.7 = (f32[128,8,4]{2,1,0:T(8,128)S(1)}, f32[128,8,4]{2,1,0:T(8,128)S(1)}, u32[]{:S(2)}, u32[]{:S(2)}) collective-permute-start(f32[128,8,4]{2,1,0:T(8,128)S(1)} %get-tuple-element.53), channel_id=1, source_target_pairs={{0,1},{2,3},{4,5},{6,7},{8,9},{10,11},{12,13},{14,15},{16,17},{18,... | collective-permute-start | bytes 49160 | tf_op jit(solution)/shard_map/ppermute | solution.py:21
  29.2 1.5 collective-permute-done.7
  30.7 1.5 select_maximum_fusion.13
  32.2 1.8 fusion.3
  34.0 1.3 collective-permute-start.8
  35.4 5.0 %collective-permute-start.9 = (f32[128,4,128]{2,1,0:T(4,128)S(1)}, f32[128,4,128]{2,1,0:T(4,128)S(1)}, u32[]{:S(2)}, u32[]{:S(2)}) collective-permute-start(f32[128,4,128]{2,1,0:T(4,128)S(1)} %get-tuple-element.51), channel_id=1, source_target_pairs={{0,2},{2,4},{4,6},{6,8},{8,10},{10,12},{12,14},{14,16},{16,18},{18... | collective-permute-start | bytes 786440 | tf_op jit(solution)/shard_map/ppermute | solution.py:21
  41.9 3.1 %collective-permute-start.11 = (f32[128,8,4]{2,1,0:T(8,128)S(1)}, f32[128,8,4]{2,1,0:T(8,128)S(1)}, u32[]{:S(2)}, u32[]{:S(2)}) collective-permute-start(f32[128,8,4]{2,1,0:T(8,128)S(1)} %get-tuple-element.49), channel_id=1, source_target_pairs={{0,1},{2,3},{4,5},{6,7},{8,9},{10,11},{12,13},{14,15},{16,17},{18,... | collective-permute-start | bytes 49160 | tf_op jit(solution)/shard_map/ppermute | solution.py:21
  45.0 1.5 collective-permute-done.11
  46.5 1.4 select_maximum_fusion.11
  47.9 1.8 fusion.5
  49.8 1.3 collective-permute-start.12
  51.2 5.6 %collective-permute-start.13 = (f32[128,4,128]{2,1,0:T(4,128)S(1)}, f32[128,4,128]{2,1,0:T(4,128)S(1)}, u32[]{:S(2)}, u32[]{:S(2)}) collective-permute-start(f32[128,4,128]{2,1,0:T(4,128)S(1)} %get-tuple-element.47), channel_id=1, source_target_pairs={{0,2},{2,4},{4,6},{6,8},{8,10},{10,12},{12,14},{14,16},{16,18},{18... | collective-permute-start | bytes 786440 | tf_op jit(solution)/shard_map/ppermute | solution.py:21
  58.3 3.3 %collective-permute-start.15 = (f32[128,8,4]{2,1,0:T(8,128)S(1)}, f32[128,8,4]{2,1,0:T(8,128)S(1)}, u32[]{:S(2)}, u32[]{:S(2)}) collective-permute-start(f32[128,8,4]{2,1,0:T(8,128)S(1)} %get-tuple-element.45), channel_id=1, source_target_pairs={{0,1},{2,3},{4,5},{6,7},{8,9},{10,11},{12,13},{14,15},{16,17},{18,... | collective-permute-start | bytes 49160 | tf_op jit(solution)/shard_map/ppermute | solution.py:21
  62.9 1.4 select_maximum_fusion.9
  64.4 1.8 fusion.7
  66.3 1.3 collective-permute-start.16
  67.6 5.8 %collective-permute-start.17 = (f32[128,4,128]{2,1,0:T(4,128)S(1)}, f32[128,4,128]{2,1,0:T(4,128)S(1)}, u32[]{:S(2)}, u32[]{:S(2)}) collective-permute-start(f32[128,4,128]{2,1,0:T(4,128)S(1)} %get-tuple-element.43), channel_id=1, source_target_pairs={{0,2},{2,4},{4,6},{6,8},{8,10},{10,12},{12,14},{14,16},{16,18},{18... | collective-permute-start | bytes 786440 | tf_op jit(solution)/shard_map/ppermute | solution.py:21
  74.9 3.1 %collective-permute-start.19 = (f32[128,8,4]{2,1,0:T(8,128)S(1)}, f32[128,8,4]{2,1,0:T(8,128)S(1)}, u32[]{:S(2)}, u32[]{:S(2)}) collective-permute-start(f32[128,8,4]{2,1,0:T(8,128)S(1)} %get-tuple-element.41), channel_id=1, source_target_pairs={{0,1},{2,3},{4,5},{6,7},{8,9},{10,11},{12,13},{14,15},{16,17},{18,... | collective-permute-start | bytes 49160 | tf_op jit(solution)/shard_map/ppermute | solution.py:21
  78.1 1.5 collective-permute-done.19
  79.6 1.4 select_maximum_fusion.7
  81.0 1.8 fusion.9
  82.9 1.3 collective-permute-start.20
  84.2 5.9 %collective-permute-start.21 = (f32[128,4,128]{2,1,0:T(4,128)S(1)}, f32[128,4,128]{2,1,0:T(4,128)S(1)}, u32[]{:S(2)}, u32[]{:S(2)}) collective-permute-start(f32[128,4,128]{2,1,0:T(4,128)S(1)} %get-tuple-element.39), channel_id=1, source_target_pairs={{0,2},{2,4},{4,6},{6,8},{8,10},{10,12},{12,14},{14,16},{16,18},{18... | collective-permute-start | bytes 786440 | tf_op jit(solution)/shard_map/ppermute | solution.py:21
  91.7 3.1 %collective-permute-start.23 = (f32[128,8,4]{2,1,0:T(8,128)S(1)}, f32[128,8,4]{2,1,0:T(8,128)S(1)}, u32[]{:S(2)}, u32[]{:S(2)}) collective-permute-start(f32[128,8,4]{2,1,0:T(8,128)S(1)} %get-tuple-element.37), channel_id=1, source_target_pairs={{0,1},{2,3},{4,5},{6,7},{8,9},{10,11},{12,13},{14,15},{16,17},{18,... | collective-permute-start | bytes 49160 | tf_op jit(solution)/shard_map/ppermute | solution.py:21
  94.8 1.5 collective-permute-done.23
  96.3 1.4 select_maximum_fusion.5
  97.7 1.8 fusion.11
  100.9 5.8 %collective-permute-start.25 = (f32[128,4,128]{2,1,0:T(4,128)S(1)}, f32[128,4,128]{2,1,0:T(4,128)S(1)}, u32[]{:S(2)}, u32[]{:S(2)}) collective-permute-start(f32[128,4,128]{2,1,0:T(4,128)S(1)} %get-tuple-element.35), channel_id=1, source_target_pairs={{0,2},{2,4},{4,6},{6,8},{8,10},{10,12},{12,14},{14,16},{16,18},{18... | collective-permute-start | bytes 786440 | tf_op jit(solution)/shard_map/ppermute | solution.py:21
  108.3 3.1 %collective-permute-start.27 = (f32[128,8,4]{2,1,0:T(8,128)S(1)}, f32[128,8,4]{2,1,0:T(8,128)S(1)}, u32[]{:S(2)}, u32[]{:S(2)}) collective-permute-start(f32[128,8,4]{2,1,0:T(8,128)S(1)} %get-tuple-element.33), channel_id=1, source_target_pairs={{0,1},{2,3},{4,5},{6,7},{8,9},{10,11},{12,13},{14,15},{16,17},{18,... | collective-permute-start | bytes 49160 | tf_op jit(solution)/shard_map/ppermute | solution.py:21
  111.4 1.5 collective-permute-done.27
  112.9 1.5 select_maximum_fusion.3
  114.4 1.8 fusion.13
  116.3 5.3 %collective-permute-start.29 = (f32[128,4,128]{2,1,0:T(4,128)S(1)}, f32[128,4,128]{2,1,0:T(4,128)S(1)}, u32[]{:S(2)}, u32[]{:S(2)}) collective-permute-start(f32[128,4,128]{2,1,0:T(4,128)S(1)} %get-tuple-element.30), channel_id=1, source_target_pairs={{0,2},{2,4},{4,6},{6,8},{8,10},{10,12},{12,14},{14,16},{16,18},{18... | collective-permute-start | bytes 786440 | tf_op jit(solution)/shard_map/ppermute | solution.py:21
  121.5 1.5 collective-permute-start.28
  124.6 3.3 %collective-permute-start.31 = (f32[128,8,4]{2,1,0:T(8,128)S(1)}, f32[128,8,4]{2,1,0:T(8,128)S(1)}, u32[]{:S(2)}, u32[]{:S(2)}) collective-permute-start(f32[128,8,4]{2,1,0:T(8,128)S(1)} %get-tuple-element.29), channel_id=1, source_target_pairs={{0,1},{2,3},{4,5},{6,7},{8,9},{10,11},{12,13},{14,15},{16,17},{18,... | collective-permute-start | bytes 49160 | tf_op jit(solution)/shard_map/ppermute | solution.py:21
  127.9 1.5 collective-permute-done.31
  129.4 3.9 %collective-permute-done.28 = f32[128,4,128]{2,1,0:T(4,128)S(1)} collective-permute-done((f32[128,4,128]{2,1,0:T(4,128)S(1)}, f32[128,4,128]{2,1,0:T(4,128)S(1)}, u32[]{:S(2)}, u32[]{:S(2)}) %collective-permute-start.28) | collective-permute-done | bytes 262176 | tf_op jit(solution)/shard_map/ppermute | solution.py:22
  133.2 1.4 select_maximum_fusion.1
  134.7 2.6 %select_multiply_fusion = (f32[128,8,128]{2,1,0:T(8,128)S(1)}, f32[128,8,128]{2,1,0:T(8,128)}) fusion(f32[128,8,128]{2,1,0:T(8,128)S(1)} %copy-done.3, s32[8,128]{1,0:T(8,128)S(1)} %copy-done.6, f32[8,128]{1,0:T(8,128)S(1)} %get-tuple-element.2, s32[8,128]{1,0:T(8,128)S(1)} %copy-done.4, f32[128,16,132]{2,1,0:T(8,128)S(1)} %get-tuple-element.13, ...), kind=kLoop, calls=%fused_computation.386 | loop fusion | flops 6291456 | bytes 7614464 | tf_op jit(solution)/shard_map/mul | solution.py:91
  137.3 97.4 %all_to_all.18 = f32[128,8,128]{2,1,0:T(8,128)S(1)} all-to-all(f32[128,8,128]{2,1,0:T(8,128)S(1)} %slice_subtract_fusion), channel_id=1, replica_groups=mesh['shots'=4,'gx'=32,'gy'=2] {'gx'}, dimensions={0} | all-to-all | bytes 1048576 | tf_op jit(solution)/shard_map/all_to_all | solution.py:94
  (71 shorter events, 18.7 us)
Async XLA Ops:
  0.6 13.3 %copy-start = (f32[128,8,128]{2,1,0:T(8,128)S(1)}, f32[128,8,128]{2,1,0:T(8,128)}, u32[]{:S(2)}) copy-start(f32[128,8,128]{2,1,0:T(8,128)} %param.8) | copy-start | bytes 1572868
  0.6 13.3 %copy-start.5 = (s32[8,128]{1,0:T(8,128)S(1)}, s32[8,128]{1,0:T(8,128)}, u32[]{:S(2)}) copy-start(s32[8,128]{1,0:T(8,128)} %param.12) | copy-start | bytes 12292
  0.7 13.3 %copy-start.7 = (f32[16]{0:T(128)S(1)}, f32[16]{0:T(128)}, u32[]{:S(2)}) copy-start(f32[16]{0:T(128)} %param.11) | copy-start | bytes 196
  2.0 12.1 %collective-permute-start = (f32[128,4,128]{2,1,0:T(4,128)S(1)}, f32[128,4,128]{2,1,0:T(4,128)S(1)}, u32[]{:S(2)}, u32[]{:S(2)}) collective-permute-start(f32[128,4,128]{2,1,0:T(4,128)S(1)} %get-tuple-element.58), channel_id=1, source_target_pairs={{2,0},{4,2},{6,4},{8,6},{10,8},{12,10},{14,12},{16,14},{18,16},{20... | collective-permute-start | bytes 786440 | tf_op jit(solution)/shard_map/ppermute | solution.py:22
  3.3 12.1 %collective-permute-start.1 = (f32[128,4,128]{2,1,0:T(4,128)S(1)}, f32[128,4,128]{2,1,0:T(4,128)S(1)}, u32[]{:S(2)}, u32[]{:S(2)}) collective-permute-start(f32[128,4,128]{2,1,0:T(4,128)S(1)} %get-tuple-element.59), channel_id=1, source_target_pairs={{0,2},{2,4},{4,6},{6,8},{8,10},{10,12},{12,14},{14,16},{16,18},{18... | collective-permute-start | bytes 786440 | tf_op jit(solution)/shard_map/ppermute | solution.py:21
  9.4 4.8 %collective-permute-start.2 = (f32[128,8,4]{2,1,0:T(8,128)S(1)}, f32[128,8,4]{2,1,0:T(8,128)S(1)}, u32[]{:S(2)}, u32[]{:S(2)}) collective-permute-start(f32[128,8,4]{2,1,0:T(8,128)S(1)} %get-tuple-element.56), channel_id=1, source_target_pairs={{1,0},{3,2},{5,4},{7,6},{9,8},{11,10},{13,12},{15,14},{17,16},{19,... | collective-permute-start | bytes 49160 | tf_op jit(solution)/shard_map/ppermute | solution.py:22
  10.8 4.6 %collective-permute-start.3 = (f32[128,8,4]{2,1,0:T(8,128)S(1)}, f32[128,8,4]{2,1,0:T(8,128)S(1)}, u32[]{:S(2)}, u32[]{:S(2)}) collective-permute-start(f32[128,8,4]{2,1,0:T(8,128)S(1)} %get-tuple-element.57), channel_id=1, source_target_pairs={{0,1},{2,3},{4,5},{6,7},{8,9},{10,11},{12,13},{14,15},{16,17},{18,... | collective-permute-start | bytes 49160 | tf_op jit(solution)/shard_map/ppermute | solution.py:21
  14.2 2.6 %copy-start.1 = (bf16[128,8,128]{2,1,0:T(8,128)(2,1)S(1)}, bf16[128,8,128]{2,1,0:T(8,128)(2,1)}, u32[]{:S(2)}) copy-start(bf16[128,8,128]{2,1,0:T(8,128)(2,1)} %param.10) | copy-start | bytes 786436
  14.2 2.6 %copy-start.2 = (f32[128,8,128]{2,1,0:T(8,128)S(1)}, f32[128,8,128]{2,1,0:T(8,128)}, u32[]{:S(2)}) copy-start(f32[128,8,128]{2,1,0:T(8,128)} %param.9) | copy-start | bytes 1572868
  14.2 2.6 %copy-start.4 = (s32[8,128]{1,0:T(8,128)S(1)}, s32[8,128]{1,0:T(8,128)}, u32[]{:S(2)}) copy-start(s32[8,128]{1,0:T(8,128)} %param.13) | copy-start | bytes 12292
  18.5 12.2 %collective-permute-start.4 = (f32[128,4,128]{2,1,0:T(4,128)S(1)}, f32[128,4,128]{2,1,0:T(4,128)S(1)}, u32[]{:S(2)}, u32[]{:S(2)}) collective-permute-start(f32[128,4,128]{2,1,0:T(4,128)S(1)} %get-tuple-element.54), channel_id=1, source_target_pairs={{2,0},{4,2},{6,4},{8,6},{10,8},{12,10},{14,12},{16,14},{18,16},{20... | collective-permute-start | bytes 786440 | tf_op jit(solution)/shard_map/ppermute | solution.py:22
  19.8 10.9 %collective-permute-start.5 = (f32[128,4,128]{2,1,0:T(4,128)S(1)}, f32[128,4,128]{2,1,0:T(4,128)S(1)}, u32[]{:S(2)}, u32[]{:S(2)}) collective-permute-start(f32[128,4,128]{2,1,0:T(4,128)S(1)} %get-tuple-element.55), channel_id=1, source_target_pairs={{0,2},{2,4},{4,6},{6,8},{8,10},{10,12},{12,14},{14,16},{16,18},{18... | collective-permute-start | bytes 786440 | tf_op jit(solution)/shard_map/ppermute | solution.py:21
  24.8 4.5 %collective-permute-start.6 = (f32[128,8,4]{2,1,0:T(8,128)S(1)}, f32[128,8,4]{2,1,0:T(8,128)S(1)}, u32[]{:S(2)}, u32[]{:S(2)}) collective-permute-start(f32[128,8,4]{2,1,0:T(8,128)S(1)} %get-tuple-element.52), channel_id=1, source_target_pairs={{1,0},{3,2},{5,4},{7,6},{9,8},{11,10},{13,12},{15,14},{17,16},{19,... | collective-permute-start | bytes 49160 | tf_op jit(solution)/shard_map/ppermute | solution.py:22
  26.1 4.6 %collective-permute-start.7 = (f32[128,8,4]{2,1,0:T(8,128)S(1)}, f32[128,8,4]{2,1,0:T(8,128)S(1)}, u32[]{:S(2)}, u32[]{:S(2)}) collective-permute-start(f32[128,8,4]{2,1,0:T(8,128)S(1)} %get-tuple-element.53), channel_id=1, source_target_pairs={{0,1},{2,3},{4,5},{6,7},{8,9},{10,11},{12,13},{14,15},{16,17},{18,... | collective-permute-start | bytes 49160 | tf_op jit(solution)/shard_map/ppermute | solution.py:21
  34.0 12.5 %collective-permute-start.8 = (f32[128,4,128]{2,1,0:T(4,128)S(1)}, f32[128,4,128]{2,1,0:T(4,128)S(1)}, u32[]{:S(2)}, u32[]{:S(2)}) collective-permute-start(f32[128,4,128]{2,1,0:T(4,128)S(1)} %get-tuple-element.50), channel_id=1, source_target_pairs={{2,0},{4,2},{6,4},{8,6},{10,8},{12,10},{14,12},{16,14},{18,16},{20... | collective-permute-start | bytes 786440 | tf_op jit(solution)/shard_map/ppermute | solution.py:22
  35.4 11.2 %collective-permute-start.9 = (f32[128,4,128]{2,1,0:T(4,128)S(1)}, f32[128,4,128]{2,1,0:T(4,128)S(1)}, u32[]{:S(2)}, u32[]{:S(2)}) collective-permute-start(f32[128,4,128]{2,1,0:T(4,128)S(1)} %get-tuple-element.51), channel_id=1, source_target_pairs={{0,2},{2,4},{4,6},{6,8},{8,10},{10,12},{12,14},{14,16},{16,18},{18... | collective-permute-start | bytes 786440 | tf_op jit(solution)/shard_map/ppermute | solution.py:21
  40.6 4.5 %collective-permute-start.10 = (f32[128,8,4]{2,1,0:T(8,128)S(1)}, f32[128,8,4]{2,1,0:T(8,128)S(1)}, u32[]{:S(2)}, u32[]{:S(2)}) collective-permute-start(f32[128,8,4]{2,1,0:T(8,128)S(1)} %get-tuple-element.48), channel_id=1, source_target_pairs={{1,0},{3,2},{5,4},{7,6},{9,8},{11,10},{13,12},{15,14},{17,16},{19,... | collective-permute-start | bytes 49160 | tf_op jit(solution)/shard_map/ppermute | solution.py:22
  41.9 4.6 %collective-permute-start.11 = (f32[128,8,4]{2,1,0:T(8,128)S(1)}, f32[128,8,4]{2,1,0:T(8,128)S(1)}, u32[]{:S(2)}, u32[]{:S(2)}) collective-permute-start(f32[128,8,4]{2,1,0:T(8,128)S(1)} %get-tuple-element.49), channel_id=1, source_target_pairs={{0,1},{2,3},{4,5},{6,7},{8,9},{10,11},{12,13},{14,15},{16,17},{18,... | collective-permute-start | bytes 49160 | tf_op jit(solution)/shard_map/ppermute | solution.py:21
  49.8 13.1 %collective-permute-start.12 = (f32[128,4,128]{2,1,0:T(4,128)S(1)}, f32[128,4,128]{2,1,0:T(4,128)S(1)}, u32[]{:S(2)}, u32[]{:S(2)}) collective-permute-start(f32[128,4,128]{2,1,0:T(4,128)S(1)} %get-tuple-element.46), channel_id=1, source_target_pairs={{2,0},{4,2},{6,4},{8,6},{10,8},{12,10},{14,12},{16,14},{18,16},{20... | collective-permute-start | bytes 786440 | tf_op jit(solution)/shard_map/ppermute | solution.py:22
  51.2 11.8 %collective-permute-start.13 = (f32[128,4,128]{2,1,0:T(4,128)S(1)}, f32[128,4,128]{2,1,0:T(4,128)S(1)}, u32[]{:S(2)}, u32[]{:S(2)}) collective-permute-start(f32[128,4,128]{2,1,0:T(4,128)S(1)} %get-tuple-element.47), channel_id=1, source_target_pairs={{0,2},{2,4},{4,6},{6,8},{8,10},{10,12},{12,14},{14,16},{16,18},{18... | collective-permute-start | bytes 786440 | tf_op jit(solution)/shard_map/ppermute | solution.py:21
  57.0 4.6 %collective-permute-start.14 = (f32[128,8,4]{2,1,0:T(8,128)S(1)}, f32[128,8,4]{2,1,0:T(8,128)S(1)}, u32[]{:S(2)}, u32[]{:S(2)}) collective-permute-start(f32[128,8,4]{2,1,0:T(8,128)S(1)} %get-tuple-element.44), channel_id=1, source_target_pairs={{1,0},{3,2},{5,4},{7,6},{9,8},{11,10},{13,12},{15,14},{17,16},{19,... | collective-permute-start | bytes 49160 | tf_op jit(solution)/shard_map/ppermute | solution.py:22
  58.3 4.6 %collective-permute-start.15 = (f32[128,8,4]{2,1,0:T(8,128)S(1)}, f32[128,8,4]{2,1,0:T(8,128)S(1)}, u32[]{:S(2)}, u32[]{:S(2)}) collective-permute-start(f32[128,8,4]{2,1,0:T(8,128)S(1)} %get-tuple-element.45), channel_id=1, source_target_pairs={{0,1},{2,3},{4,5},{6,7},{8,9},{10,11},{12,13},{14,15},{16,17},{18,... | collective-permute-start | bytes 49160 | tf_op jit(solution)/shard_map/ppermute | solution.py:21
  66.3 13.3 %collective-permute-start.16 = (f32[128,4,128]{2,1,0:T(4,128)S(1)}, f32[128,4,128]{2,1,0:T(4,128)S(1)}, u32[]{:S(2)}, u32[]{:S(2)}) collective-permute-start(f32[128,4,128]{2,1,0:T(4,128)S(1)} %get-tuple-element.42), channel_id=1, source_target_pairs={{2,0},{4,2},{6,4},{8,6},{10,8},{12,10},{14,12},{16,14},{18,16},{20... | collective-permute-start | bytes 786440 | tf_op jit(solution)/shard_map/ppermute | solution.py:22
  67.6 12.0 %collective-permute-start.17 = (f32[128,4,128]{2,1,0:T(4,128)S(1)}, f32[128,4,128]{2,1,0:T(4,128)S(1)}, u32[]{:S(2)}, u32[]{:S(2)}) collective-permute-start(f32[128,4,128]{2,1,0:T(4,128)S(1)} %get-tuple-element.43), channel_id=1, source_target_pairs={{0,2},{2,4},{4,6},{6,8},{8,10},{10,12},{12,14},{14,16},{16,18},{18... | collective-permute-start | bytes 786440 | tf_op jit(solution)/shard_map/ppermute | solution.py:21
  73.6 4.5 %collective-permute-start.18 = (f32[128,8,4]{2,1,0:T(8,128)S(1)}, f32[128,8,4]{2,1,0:T(8,128)S(1)}, u32[]{:S(2)}, u32[]{:S(2)}) collective-permute-start(f32[128,8,4]{2,1,0:T(8,128)S(1)} %get-tuple-element.40), channel_id=1, source_target_pairs={{1,0},{3,2},{5,4},{7,6},{9,8},{11,10},{13,12},{15,14},{17,16},{19,... | collective-permute-start | bytes 49160 | tf_op jit(solution)/shard_map/ppermute | solution.py:22
  74.9 4.6 %collective-permute-start.19 = (f32[128,8,4]{2,1,0:T(8,128)S(1)}, f32[128,8,4]{2,1,0:T(8,128)S(1)}, u32[]{:S(2)}, u32[]{:S(2)}) collective-permute-start(f32[128,8,4]{2,1,0:T(8,128)S(1)} %get-tuple-element.41), channel_id=1, source_target_pairs={{0,1},{2,3},{4,5},{6,7},{8,9},{10,11},{12,13},{14,15},{16,17},{18,... | collective-permute-start | bytes 49160 | tf_op jit(solution)/shard_map/ppermute | solution.py:21
  82.9 13.4 %collective-permute-start.20 = (f32[128,4,128]{2,1,0:T(4,128)S(1)}, f32[128,4,128]{2,1,0:T(4,128)S(1)}, u32[]{:S(2)}, u32[]{:S(2)}) collective-permute-start(f32[128,4,128]{2,1,0:T(4,128)S(1)} %get-tuple-element.38), channel_id=1, source_target_pairs={{2,0},{4,2},{6,4},{8,6},{10,8},{12,10},{14,12},{16,14},{18,16},{20... | collective-permute-start | bytes 786440 | tf_op jit(solution)/shard_map/ppermute | solution.py:22
  84.2 12.1 %collective-permute-start.21 = (f32[128,4,128]{2,1,0:T(4,128)S(1)}, f32[128,4,128]{2,1,0:T(4,128)S(1)}, u32[]{:S(2)}, u32[]{:S(2)}) collective-permute-start(f32[128,4,128]{2,1,0:T(4,128)S(1)} %get-tuple-element.39), channel_id=1, source_target_pairs={{0,2},{2,4},{4,6},{6,8},{8,10},{10,12},{12,14},{14,16},{16,18},{18... | collective-permute-start | bytes 786440 | tf_op jit(solution)/shard_map/ppermute | solution.py:21
  90.3 4.5 %collective-permute-start.22 = (f32[128,8,4]{2,1,0:T(8,128)S(1)}, f32[128,8,4]{2,1,0:T(8,128)S(1)}, u32[]{:S(2)}, u32[]{:S(2)}) collective-permute-start(f32[128,8,4]{2,1,0:T(8,128)S(1)} %get-tuple-element.36), channel_id=1, source_target_pairs={{1,0},{3,2},{5,4},{7,6},{9,8},{11,10},{13,12},{15,14},{17,16},{19,... | collective-permute-start | bytes 49160 | tf_op jit(solution)/shard_map/ppermute | solution.py:22
  91.7 4.6 %collective-permute-start.23 = (f32[128,8,4]{2,1,0:T(8,128)S(1)}, f32[128,8,4]{2,1,0:T(8,128)S(1)}, u32[]{:S(2)}, u32[]{:S(2)}) collective-permute-start(f32[128,8,4]{2,1,0:T(8,128)S(1)} %get-tuple-element.37), channel_id=1, source_target_pairs={{0,1},{2,3},{4,5},{6,7},{8,9},{10,11},{12,13},{14,15},{16,17},{18,... | collective-permute-start | bytes 49160 | tf_op jit(solution)/shard_map/ppermute | solution.py:21
  99.6 13.3 %collective-permute-start.24 = (f32[128,4,128]{2,1,0:T(4,128)S(1)}, f32[128,4,128]{2,1,0:T(4,128)S(1)}, u32[]{:S(2)}, u32[]{:S(2)}) collective-permute-start(f32[128,4,128]{2,1,0:T(4,128)S(1)} %get-tuple-element.34), channel_id=1, source_target_pairs={{2,0},{4,2},{6,4},{8,6},{10,8},{12,10},{14,12},{16,14},{18,16},{20... | collective-permute-start | bytes 786440 | tf_op jit(solution)/shard_map/ppermute | solution.py:22
  100.9 12.0 %collective-permute-start.25 = (f32[128,4,128]{2,1,0:T(4,128)S(1)}, f32[128,4,128]{2,1,0:T(4,128)S(1)}, u32[]{:S(2)}, u32[]{:S(2)}) collective-permute-start(f32[128,4,128]{2,1,0:T(4,128)S(1)} %get-tuple-element.35), channel_id=1, source_target_pairs={{0,2},{2,4},{4,6},{6,8},{8,10},{10,12},{12,14},{14,16},{16,18},{18... | collective-permute-start | bytes 786440 | tf_op jit(solution)/shard_map/ppermute | solution.py:21
  107.0 4.5 %collective-permute-start.26 = (f32[128,8,4]{2,1,0:T(8,128)S(1)}, f32[128,8,4]{2,1,0:T(8,128)S(1)}, u32[]{:S(2)}, u32[]{:S(2)}) collective-permute-start(f32[128,8,4]{2,1,0:T(8,128)S(1)} %get-tuple-element.32), channel_id=1, source_target_pairs={{1,0},{3,2},{5,4},{7,6},{9,8},{11,10},{13,12},{15,14},{17,16},{19,... | collective-permute-start | bytes 49160 | tf_op jit(solution)/shard_map/ppermute | solution.py:22
  108.3 4.6 %collective-permute-start.27 = (f32[128,8,4]{2,1,0:T(8,128)S(1)}, f32[128,8,4]{2,1,0:T(8,128)S(1)}, u32[]{:S(2)}, u32[]{:S(2)}) collective-permute-start(f32[128,8,4]{2,1,0:T(8,128)S(1)} %get-tuple-element.33), channel_id=1, source_target_pairs={{0,1},{2,3},{4,5},{6,7},{8,9},{10,11},{12,13},{14,15},{16,17},{18,... | collective-permute-start | bytes 49160 | tf_op jit(solution)/shard_map/ppermute | solution.py:21
  116.3 13.1 %collective-permute-start.29 = (f32[128,4,128]{2,1,0:T(4,128)S(1)}, f32[128,4,128]{2,1,0:T(4,128)S(1)}, u32[]{:S(2)}, u32[]{:S(2)}) collective-permute-start(f32[128,4,128]{2,1,0:T(4,128)S(1)} %get-tuple-element.30), channel_id=1, source_target_pairs={{0,2},{2,4},{4,6},{6,8},{8,10},{10,12},{12,14},{14,16},{16,18},{18... | collective-permute-start | bytes 786440 | tf_op jit(solution)/shard_map/ppermute | solution.py:21
  121.5 11.7 %collective-permute-start.28 = (f32[128,4,128]{2,1,0:T(4,128)S(1)}, f32[128,4,128]{2,1,0:T(4,128)S(1)}, u32[]{:S(2)}, u32[]{:S(2)}) collective-permute-start(f32[128,4,128]{2,1,0:T(4,128)S(1)} %get-tuple-element.31), channel_id=1, source_target_pairs={{2,0},{4,2},{6,4},{8,6},{10,8},{12,10},{14,12},{16,14},{18,16},{20... | collective-permute-start | bytes 786440 | tf_op jit(solution)/shard_map/ppermute | solution.py:22
  123.3 4.6 %collective-permute-start.30 = (f32[128,8,4]{2,1,0:T(8,128)S(1)}, f32[128,8,4]{2,1,0:T(8,128)S(1)}, u32[]{:S(2)}, u32[]{:S(2)}) collective-permute-start(f32[128,8,4]{2,1,0:T(8,128)S(1)} %get-tuple-element.28), channel_id=1, source_target_pairs={{1,0},{3,2},{5,4},{7,6},{9,8},{11,10},{13,12},{15,14},{17,16},{19,... | collective-permute-start | bytes 49160 | tf_op jit(solution)/shard_map/ppermute | solution.py:22
  124.6 10.1 %copy-start.3 = (f32[128,8,128]{2,1,0:T(8,128)S(1)}, f32[128,8,128]{2,1,0:T(8,128)}, u32[]{:S(2)}) copy-start(f32[128,8,128]{2,1,0:T(8,128)} %param.15) | copy-start | bytes 1572868
  124.6 10.1 %copy-start.6 = (s32[8,128]{1,0:T(8,128)S(1)}, s32[8,128]{1,0:T(8,128)}, u32[]{:S(2)}) copy-start(s32[8,128]{1,0:T(8,128)} %param.14) | copy-start | bytes 12292
  124.6 4.8 %collective-permute-start.31 = (f32[128,8,4]{2,1,0:T(8,128)S(1)}, f32[128,8,4]{2,1,0:T(8,128)S(1)}, u32[]{:S(2)}, u32[]{:S(2)}) collective-permute-start(f32[128,8,4]{2,1,0:T(8,128)S(1)} %get-tuple-element.29), channel_id=1, source_target_pairs={{0,1},{2,3},{4,5},{6,7},{8,9},{10,11},{12,13},{14,15},{16,17},{18,... | collective-permute-start | bytes 49160 | tf_op jit(solution)/shard_map/ppermute | solution.py:21
where the time goes:
time: 236 us
  blocking collectives  97.4 us (41%)
  starting transfers between devices  89.4 us (38%)
  other arithmetic  26.6 us (11%)
  waiting for transfers between devices  15.2 us (6%)
  local copies, waits for them, and re-layouts  5.7 us (2%)
    all_to_all x1, blocking collectives, shards(): lax.all_to_all(filtered, 'gx', split_axis=0, concat_axis=1, tiled=True)  97.4 us
    ppermute x16, starting transfers between devices, padded_2(): lax.ppermute(last, axis, up)  68.2 us
    ppermute x16, starting transfers between devices, padded_2(): lax.ppermute(leading, axis, [(b, a) for a, b in up])  21.1 us
    add x7, other arithmetic, shards(): 2.0 * current - prior + coefficient * laplacian(current)  12.4 us
    concatenate x8, other arithmetic, padded_2(): jnp.concatenate([jnp.pad(low, around), shard, jnp.pad(high, around)], axi...  11.4 us
    ppermute x16, waiting for transfers between devices, padded_2(): lax.ppermute(last, axis, up)  11.3 us
  transfers between devices with their start and end apart: 32, of which 9 were waited for; matrix products, arithmetic and copies ran while one was open for 1% of the time, Pallas kernels for 0%

commit v1 on v0

v1 whole, which is shorter than its diff:
```python
import functools

import jax
import jax.numpy as jnp
from jax import lax
from jax.experimental import pallas as pl
from jax.experimental.pallas import tpu as pltpu
from jax.sharding import PartitionSpec as P

STEPS = 8

CENTER = -205.0 / 72.0
COEFS = (1.6, -0.2, 8.0 / 315.0, -1.0 / 560.0)
REACH = len(COEFS)
CHUNK = 32

VM = pl.BlockSpec(memory_space=pltpu.VMEM)
SM = pl.BlockSpec(memory_space=pltpu.SMEM)
F32 = jnp.float32


def split_planes(src_ref, odd, put):
    depth = src_ref.shape[0] // (2 * REACH)
    for i in range(REACH):
        right = src_ref[pl.ds(REACH + i, depth, stride=2 * REACH), :].T
        left = src_ref[pl.ds(REACH - 1 - i, depth, stride=2 * REACH), :].T
        put(i, jnp.where(odd, left, right), jnp.where(odd, right, left))


def rim(plane_ref, i, first):
    length = plane_ref.shape[1]
    return jnp.where(first, plane_ref[i, length - REACH : length, :], plane_ref[i, 0:REACH, :])


def open_kernel(flags_ref, p_ref, near_ref, far_ref, rim_ref):
    odd = flags_ref[0] == 1
    first = flags_ref[1] == 0

    def put(i, near, far):
        near_ref[i] = near
        far_ref[i] = far

    split_planes(p_ref, odd, put)
    for i in range(REACH):
        rim_ref[i] = rim(near_ref, i, first)
        rim_ref[REACH + i] = rim(far_ref, i, first)


def tables_kernel(
    flags_ref, wavelet_ref, prior_ref, coef_ref, delay_ref, depth_ref,
    prior_near, prior_far, coef_near, coef_far, mark_near, mark_far, amp_ref,
):
    odd = flags_ref[0] == 1
    length, depth = prior_near.shape[1:]

    def put_prior(i, near, far):
        prior_near[i] = near
        prior_far[i] = far

    def put_coef(i, near, far):
        coef_near[i] = near
        coef_far[i] = far

    split_planes(prior_ref, odd, put_prior)
    split_planes(coef_ref, odd, put_coef)
    delay = delay_ref[...]
    rows = []
    for step in range(STEPS):
        amplitude = jnp.zeros(delay.shape, F32)
        for w in range(wavelet_ref.shape[0]):
            amplitude = jnp.where(delay + step == w, wavelet_ref[w], amplitude)
        rows.append(amplitude)
    rows.append(depth_ref[...].astype(F32))
    fill = jnp.zeros((length - len(rows) * 2 * REACH, length), F32)
    columns = jnp.concatenate(rows + [fill], axis=0).T
    amp_ref[...] = columns
    levels = lax.broadcasted_iota(jnp.int32, (length, depth), 1).astype(F32)
    base = STEPS * 2 * REACH
    for i in range(REACH):
        right = columns[:, base + REACH + i : base + REACH + i + 1]
        left = columns[:, base + REACH - 1 - i : base + REACH - i]
        near = jnp.where(odd, left, right)
        far = jnp.where(odd, right, left)
        mark_near[i] = jnp.where(levels == near, 1.0, 0.0)
        mark_far[i] = jnp.where(levels == far, 1.0, 0.0)


def advance_kernel(
    step, half, flags_ref, self_ref, other_ref, halo_ref, rim_in_ref, prior_ref, coef_ref, mark_ref, amp_ref, *rest
):
    if half:
        near_new_ref, out_ref, rim_ref, pad_ref, deep_ref = rest
    else:
        out_ref, pad_ref, deep_ref = rest
    odd = flags_ref[0] == 1
    first = flags_ref[1] == 0
    planes, length, depth = self_ref.shape
    for i in range(planes):
        edge = rim_in_ref[half * REACH + i]
        none = jnp.zeros_like(edge)
        pad_ref[i, 8 : 8 + length, :] = self_ref[i]
        pad_ref[i, 8 - REACH : 8, :] = jnp.where(first, none, edge)
        pad_ref[i, 8 + length : 8 + length + REACH, :] = jnp.where(first, edge, none)
    apart = jnp.abs(
        lax.broadcasted_iota(jnp.int32, (depth, depth), 0) - lax.broadcasted_iota(jnp.int32, (depth, depth), 1)
    )
    band = jnp.where(apart == 0, F32(3.0 * CENTER), F32(0.0))
    for k in range(1, REACH + 1):
        band = jnp.where(apart == k, F32(COEFS[k - 1]), band)
    line = [(other_ref, REACH - 1 - i) for i in range(REACH)]
    line += [(self_ref, i) for i in range(REACH)]
    line += [(halo_ref, REACH - 1 - i) for i in range(REACH)]
    for i in range(planes):
        deep_ref[...] = jnp.dot(self_ref[i], band, precision=lax.Precision.HIGHEST, preferred_element_type=F32)
        right, left = REACH + i, REACH - 1 - i
        even_col, odd_col = (left, right) if half else (right, left)
        for row in range(0, length, CHUNK):
            at = slice(row, row + CHUNK)
            total = deep_ref[at, :]
            for k in range(1, REACH + 1):
                low_ref, low = line[REACH + i - k]
                high_ref, high = line[REACH + i + k]
                around = low_ref[low, at, :] + high_ref[high, at, :]
                around = around + pad_ref[i, 8 + row - k : 8 + row - k + CHUNK, :]
                around = around + pad_ref[i, 8 + row + k : 8 + row + k + CHUNK, :]
                total = total + COEFS[k - 1] * around
            column = step * 2 * REACH
            amplitude = jnp.where(
                odd,
                amp_ref[at, column + odd_col : column + odd_col + 1],
                amp_ref[at, column + even_col : column + even_col + 1],
            )
            out_ref[i, at, :] = (
                2.0 * self_ref[i, at, :]
                - prior_ref[i, at, :]
                + coef_ref[i, at, :] * total
                + mark_ref[i, at, :] * amplitude
            )
    if half:
        for i in range(planes):
            rim_ref[i] = rim(near_new_ref, i, first)
            rim_ref[REACH + i] = rim(out_ref, i, first)


def close_kernel(flags_ref, near_ref, far_ref, receiver_ref, receiver_depth_ref, p_ref, image_ref, product_ref):
    odd = flags_ref[0] == 1
    width = 2 * REACH
    depth = p_ref.shape[0] // width
    for i in range(REACH):
        near, far = near_ref[i], far_ref[i]
        p_ref[pl.ds(REACH + i, depth, stride=width), :] = jnp.where(odd, far, near).T
        p_ref[pl.ds(REACH - 1 - i, depth, stride=width), :] = jnp.where(odd, near, far).T
    start = receiver_depth_ref[...]
    for z in range(depth):
        at = slice(z * width, (z + 1) * width)
        field = receiver_ref[at, :]
        product_ref[at, :] = p_ref[at, :] * jnp.where(start <= z, field, jnp.zeros_like(field))
    for z in range(depth):
        at = slice(z * width, (z + 1) * width)
        value = 2.0 * product_ref[at, :]
        if z > 0:
            value = value - product_ref[(z - 1) * width : z * width, :]
        if z < depth - 1:
            value = value - product_ref[(z + 1) * width : (z + 2) * width, :]
        image_ref[at, :] = value


def pairs(size, first):
    left = [(i, i + 1) for i in range(first, size - 1, 2)]
    return left + [(b, a) for a, b in left]


def shards(
    pressure,
    pressure_prior,
    courant_square,
    wavelet,
    delay_steps,
    source_depth,
    receiver_depth,
    receiver_field,
):
    depth, width, length = pressure.shape
    size = lax.axis_size("gx")
    even, uneven = pairs(size, 0), pairs(size, 1)
    swap = pairs(lax.axis_size("gy"), 0)
    flags = jnp.stack([lax.axis_index("gx") % 2, lax.axis_index("gy")]).astype(jnp.int32)
    flat = (depth * width, length)
    half = jax.ShapeDtypeStruct((REACH, length, depth), F32)
    rims = jax.ShapeDtypeStruct((2 * REACH, REACH, depth), F32)
    square = jax.ShapeDtypeStruct((length, length), F32)

    near, far, edge = pl.pallas_call(
        open_kernel, out_shape=(half, half, rims), in_specs=[SM, VM], out_specs=(VM, VM, VM), name="open"
    )(flags, pressure.reshape(flat))
    near_prior, far_prior, near_coef, far_coef, near_mark, far_mark, amp = pl.pallas_call(
        tables_kernel,
        out_shape=(half,) * 6 + (square,),
        in_specs=[SM, SM] + [VM] * 4,
        out_specs=(VM,) * 7,
        name="tables",
    )(
        flags,
        wavelet,
        pressure_prior.reshape(flat),
        courant_square.astype(F32).reshape(flat),
        delay_steps,
        source_depth,
    )
    scratch = [pltpu.VMEM((REACH, length + 16, depth), F32), pltpu.VMEM((length, depth), F32)]
    for step in range(STEPS):
        near_halo = lax.ppermute(near, "gx", even)
        far_halo = lax.ppermute(far, "gx", uneven)
        edge_in = lax.ppermute(edge, "gy", swap)
        near_next = pl.pallas_call(
            functools.partial(advance_kernel, step, 0),
            out_shape=half,
            in_specs=[SM] + [VM] * 8,
            out_specs=VM,
            scratch_shapes=scratch,
            name=f"near{step}",
        )(flags, near, far, near_halo, edge_in, near_prior, near_coef, near_mark, amp)
        far_next, edge = pl.pallas_call(
            functools.partial(advance_kernel, step, 1),
            out_shape=(half, rims),
            in_specs=[SM] + [VM] * 9,
            out_specs=(VM, VM),
            scratch_shapes=scratch,
            name=f"far{step}",
        )(flags, far, near, far_halo, edge_in, far_prior, far_coef, far_mark, amp, near_next)
        near_prior, far_prior = near, far
        near, far = near_next, far_next
    final, filtered = pl.pallas_call(
        close_kernel,
        out_shape=(jax.ShapeDtypeStruct(flat, F32), jax.ShapeDtypeStruct(flat, F32)),
        in_specs=[SM] + [VM] * 4,
        out_specs=(VM, VM),
        scratch_shapes=[pltpu.VMEM(flat, F32)],
        name="close",
    )(flags, near, far, receiver_field.reshape(flat), receiver_depth)
    image = lax.all_to_all(filtered.reshape(depth, width, length), "gx", split_axis=0, concat_axis=1, tiled=True)
    return final.reshape(depth, width, length), image


def solution(mesh):
    in_specs = (
        P(None, ("shots", "gx"), "gy"),
        P(None, ("shots", "gx"), "gy"),
        P(None, "gx", "gy"),
        P("shots"),
        P(("shots", "gx"), "gy"),
        P(("shots", "gx"), "gy"),
        P(("shots", "gx"), "gy"),
        P(None, ("shots", "gx"), "gy"),
    )
    out_specs = (P(None, ("shots", "gx"), "gy"), P("gx", "shots", "gy"))
    return jax.shard_map(shards, mesh=mesh, in_specs=in_specs, out_specs=out_specs, check_vma=False)
```

time: 236 us -> 218 us (0.924)
  Pallas kernels: 0 us -> 50.5 us
  starting transfers between devices: 89.4 us -> 45.3 us
  other arithmetic: 26.6 us -> 1.49 us
  blocking collectives: 97.4 us -> 87.2 us
  local copies, waits for them, and re-layouts: 5.7 us -> 12.1 us
  waiting for transfers between devices: 15.2 us -> 19.9 us
    pallas_call x0 -> x19, Pallas kernels: none -> 50.5 us  [the longest x8 22 us: shards(): pl.pallas_call(functools.partial(advance_kernel, step, 1), out_shape=(hal...]
    ppermute x32 -> x24, starting transfers between devices: 89.4 us -> 45.3 us  [the longest x8 38.5 us: shards(): near_halo = lax.ppermute(near, 'gx', even)]
    add x8 -> x0, other arithmetic: 12.4 us -> none  [the longest x7 12.4 us: shards(): 2.0 * current - prior + coefficient * laplacian(current)]
    concatenate x8 -> x0, other arithmetic: 11.4 us -> none  [padded_2(): jnp.concatenate([jnp.pad(low, around), shard, jnp.pad(high, around)], axi...]
    unnamed x17 -> x50, local copies, waits for them, and re-layouts: 0.08 us -> 11.3 us
    all_to_all x1, blocking collectives: 97.4 us -> 87.2 us  [shards(): lax.all_to_all(filtered.reshape(depth, width, length), 'gx', split_axis=0...]
    slice x16 -> x0, local copies, waits for them, and re-layouts: 4.73 us -> none  [the longest x15 4.64 us: padded_2(): leading = lax.slice_in_dim(shard, 0, width, axis=dim)]
    ppermute x32 -> x24, waiting for transfers between devices: 15.2 us -> 19.9 us  [the longest x8 10.5 us: shards(): near_halo = lax.ppermute(near, 'gx', even)]
  transfers between devices with their start and end apart: 32 -> 24, of which waited for: 9 -> 15; matrix products, arithmetic and copies ran while one was open for 1% -> 0% of each run, Pallas kernels for 0% -> 20%
where the time goes in v1:
time: 218 us; the launch traced here: 217 us
  blocking collectives  87.2 us (40%)
  Pallas kernels  50.5 us (23%)
  starting transfers between devices  45.3 us (21%)
  waiting for transfers between devices  19.9 us (9%)
  local copies, waits for them, and re-layouts  12.1 us (6%)
    all_to_all x1, blocking collectives, shards(): lax.all_to_all(filtered.reshape(depth, width, length), 'gx', split_axis=0...  87.2 us
    ppermute x8, starting transfers between devices, shards(): near_halo = lax.ppermute(near, 'gx', even)  38.5 us
    pallas_call x8, Pallas kernels, shards(): pl.pallas_call(functools.partial(advance_kernel, step, 1), out_shape=(hal...  22 us
    pallas_call x8, Pallas kernels, shards(): pl.pallas_call(functools.partial(advance_kernel, step, 0), out_shape=half...  21.1 us
    unnamed x50, local copies, waits for them, and re-layouts  11.3 us
    ppermute x8, waiting for transfers between devices, shards(): near_halo = lax.ppermute(near, 'gx', even)  10.5 us
    ppermute x8, waiting for transfers between devices, shards(): edge_in = lax.ppermute(edge, 'gy', swap)  9.41 us
    ppermute x8, starting transfers between devices, shards(): far_halo = lax.ppermute(far, 'gx', uneven)  5.33 us
  transfers between devices with their start and end apart: 24, of which 15 were waited for; matrix products, arithmetic and copies ran while one was open for 0% of the time, Pallas kernels for 20%

profile of v1, /device:TPU:46, one launch (start us, length us, event | category | flops | bytes accessed | tf_op | source)
XLA Modules:
  0.0 217.3 jit_solution(1724547257516661683)
XLA Ops:
  1.3 2.1 open.1
  3.4 2.1 collective-permute-start
  6.3 0.8 bitcast_convert_fusion.coef_ref
  7.2 2.9 %tables.1 = (f32[4,128,128]{2,1,0:T(8,128)}, f32[4,128,128]{2,1,0:T(8,128)}, f32[4,128,128]{2,1,0:T(8,128)}, f32[4,128,128]{2,1,0:T(8,128)}, f32[4,128,128]{2,1,...) custom-call(s32[2]{0:T(128)} %pad_add_fusion.flags_ref, f32[16]{0:T(128)} %wavelet_ref.1, f32[1024,128]{1,0:T(8,128)} %bitcast.17, ...), custom_call_target="tpu_custom_call" | custom-call | tf_op jit(solution)/shard_map/tables/pallas_call | solution.py:196
  10.1 2.0 collective-permute-done.halo_ref
  12.8 2.6 %near0.1.rest_0_.self_ref.other_ref.prior_ref = f32[4,128,128]{2,1,0:T(8,128)} custom-call(s32[2]{0:T(128)} %pad_add_fusion.flags_ref, f32[4,128,128]{2,1,0:T(8,128)} %get-tuple-element.29.self_ref.other_ref.prior_ref, f32[4,128,128]{2,1,0:T(8,128)} %get-tuple-element.30.other_ref.self_ref.prior_ref, f32[4,128,128]{2,1,0:T(8,128)} %copy-done.5, ...), custom_call_target="tpu_custom_call" | custom-call | tf_op jit(solution)/shard_map/near0/pallas_call | solution.py:215
  15.4 3.5 %collective-permute-start.3 = (f32[4,128,128]{2,1,0:T(8,128)}, f32[4,128,128]{2,1,0:T(8,128)S(1)}, u32[]{:S(2)}, u32[]{:S(2)}) collective-permute-start(f32[4,128,128]{2,1,0:T(8,128)} %near0.1.rest_0_.self_ref.other_ref.prior_ref), channel_id=1, source_target_pairs={{0,2},{4,6},{8,10},{12,14},{16,18},{20,22},{24,26},{28,30},{32,34}... | collective-permute-start | bytes 786440 | tf_op jit(solution)/shard_map/ppermute | solution.py:212
  19.7 2.7 %far0.1 = (f32[4,128,128]{2,1,0:T(8,128)}, f32[8,4,128]{2,1,0:T(4,128)}) custom-call(s32[2]{0:T(128)} %pad_add_fusion.flags_ref, f32[4,128,128]{2,1,0:T(8,128)} %get-tuple-element.30.other_ref.self_ref.prior_ref, f32[4,128,128]{2,1,0:T(8,128)} %get-tuple-element.29.self_ref.other_ref.prior_ref, f32[4,128,128]{2,1,0:T(8,128)} %copy-done.1, ...), custom_call_target="tpu_custom_call" | custom-call | tf_op jit(solution)/shard_map/far0/pallas_call | solution.py:223
  23.4 1.2 collective-permute-done.4.rim_in_ref
  24.6 1.5 collective-permute-done.3.halo_ref
  26.1 0.7 copy-done.4
  26.8 2.6 %near1.1.rest_0_.self_ref.other_ref.prior_ref = f32[4,128,128]{2,1,0:T(8,128)} custom-call(s32[2]{0:T(128)} %pad_add_fusion.flags_ref, f32[4,128,128]{2,1,0:T(8,128)} %near0.1.rest_0_.self_ref.other_ref.prior_ref, f32[4,128,128]{2,1,0:T(8,128)} %get-tuple-element.39.other_ref.self_ref.prior_ref, f32[4,128,128]{2,1,0:T(8,128)} %copy-done.4, ...), custom_call_target="tpu_custom_call" | custom-call | tf_op jit(solution)/shard_map/near1/pallas_call | solution.py:215
  29.5 5.8 %collective-permute-start.6 = (f32[4,128,128]{2,1,0:T(8,128)}, f32[4,128,128]{2,1,0:T(8,128)S(1)}, u32[]{:S(2)}, u32[]{:S(2)}) collective-permute-start(f32[4,128,128]{2,1,0:T(8,128)} %near1.1.rest_0_.self_ref.other_ref.prior_ref), channel_id=1, source_target_pairs={{0,2},{4,6},{8,10},{12,14},{16,18},{20,22},{24,26},{28,30},{32,34}... | collective-permute-start | bytes 786440 | tf_op jit(solution)/shard_map/ppermute | solution.py:212
  35.2 0.7 copy-done.11
  35.9 2.7 %far1.1 = (f32[4,128,128]{2,1,0:T(8,128)}, f32[8,4,128]{2,1,0:T(4,128)}) custom-call(s32[2]{0:T(128)} %pad_add_fusion.flags_ref, f32[4,128,128]{2,1,0:T(8,128)} %get-tuple-element.39.other_ref.self_ref.prior_ref, f32[4,128,128]{2,1,0:T(8,128)} %near0.1.rest_0_.self_ref.other_ref.prior_ref, f32[4,128,128]{2,1,0:T(8,128)} %copy-done.11, ...), custom_call_target="tpu_custom_call" | custom-call | tf_op jit(solution)/shard_map/far1/pallas_call | solution.py:223
  39.5 1.4 collective-permute-done.7.rim_in_ref
  40.9 1.2 collective-permute-done.6.halo_ref
  42.1 0.7 copy-done.6
  42.8 2.6 %near2.1.rest_0_.self_ref.other_ref.prior_ref = f32[4,128,128]{2,1,0:T(8,128)} custom-call(s32[2]{0:T(128)} %pad_add_fusion.flags_ref, f32[4,128,128]{2,1,0:T(8,128)} %near1.1.rest_0_.self_ref.other_ref.prior_ref, f32[4,128,128]{2,1,0:T(8,128)} %get-tuple-element.41.other_ref.self_ref.prior_ref, f32[4,128,128]{2,1,0:T(8,128)} %copy-done.6, ...), custom_call_target="tpu_custom_call" | custom-call | tf_op jit(solution)/shard_map/near2/pallas_call | solution.py:215
  45.4 4.9 %collective-permute-start.9 = (f32[4,128,128]{2,1,0:T(8,128)}, f32[4,128,128]{2,1,0:T(8,128)S(1)}, u32[]{:S(2)}, u32[]{:S(2)}) collective-permute-start(f32[4,128,128]{2,1,0:T(8,128)} %near2.1.rest_0_.self_ref.other_ref.prior_ref), channel_id=1, source_target_pairs={{0,2},{4,6},{8,10},{12,14},{16,18},{20,22},{24,26},{28,30},{32,34}... | collective-permute-start | bytes 786440 | tf_op jit(solution)/shard_map/ppermute | solution.py:212
  51.0 2.7 %far2.1 = (f32[4,128,128]{2,1,0:T(8,128)}, f32[8,4,128]{2,1,0:T(4,128)}) custom-call(s32[2]{0:T(128)} %pad_add_fusion.flags_ref, f32[4,128,128]{2,1,0:T(8,128)} %get-tuple-element.41.other_ref.self_ref.prior_ref, f32[4,128,128]{2,1,0:T(8,128)} %near1.1.rest_0_.self_ref.other_ref.prior_ref, f32[4,128,128]{2,1,0:T(8,128)} %copy-done.12, ...), custom_call_target="tpu_custom_call" | custom-call | tf_op jit(solution)/shard_map/far2/pallas_call | solution.py:223
  54.6 1.4 collective-permute-done.10.rim_in_ref
  56.0 1.2 collective-permute-done.9.halo_ref
  57.9 2.6 %near3.1.rest_0_.self_ref.other_ref.prior_ref = f32[4,128,128]{2,1,0:T(8,128)} custom-call(s32[2]{0:T(128)} %pad_add_fusion.flags_ref, f32[4,128,128]{2,1,0:T(8,128)} %near2.1.rest_0_.self_ref.other_ref.prior_ref, f32[4,128,128]{2,1,0:T(8,128)} %get-tuple-element.43.other_ref.self_ref.prior_ref, f32[4,128,128]{2,1,0:T(8,128)} %copy-done.7, ...), custom_call_target="tpu_custom_call" | custom-call | tf_op jit(solution)/shard_map/near3/pallas_call | solution.py:215
  60.5 6.1 %collective-permute-start.12 = (f32[4,128,128]{2,1,0:T(8,128)}, f32[4,128,128]{2,1,0:T(8,128)S(1)}, u32[]{:S(2)}, u32[]{:S(2)}) collective-permute-start(f32[4,128,128]{2,1,0:T(8,128)} %near3.1.rest_0_.self_ref.other_ref.prior_ref), channel_id=1, source_target_pairs={{0,2},{4,6},{8,10},{12,14},{16,18},{20,22},{24,26},{28,30},{32,34}... | collective-permute-start | bytes 786440 | tf_op jit(solution)/shard_map/ppermute | solution.py:212
  67.3 2.7 %far3.1 = (f32[4,128,128]{2,1,0:T(8,128)}, f32[8,4,128]{2,1,0:T(4,128)}) custom-call(s32[2]{0:T(128)} %pad_add_fusion.flags_ref, f32[4,128,128]{2,1,0:T(8,128)} %get-tuple-element.43.other_ref.self_ref.prior_ref, f32[4,128,128]{2,1,0:T(8,128)} %near2.1.rest_0_.self_ref.other_ref.prior_ref, f32[4,128,128]{2,1,0:T(8,128)} %copy-done.13, ...), custom_call_target="tpu_custom_call" | custom-call | tf_op jit(solution)/shard_map/far3/pallas_call | solution.py:223
  71.1 1.4 collective-permute-done.13.rim_in_ref
  72.4 1.0 collective-permute-done.12.halo_ref
  74.2 2.6 %near4.1.rest_0_.self_ref.other_ref.prior_ref = f32[4,128,128]{2,1,0:T(8,128)} custom-call(s32[2]{0:T(128)} %pad_add_fusion.flags_ref, f32[4,128,128]{2,1,0:T(8,128)} %near3.1.rest_0_.self_ref.other_ref.prior_ref, f32[4,128,128]{2,1,0:T(8,128)} %get-tuple-element.45.other_ref.self_ref.prior_ref, f32[4,128,128]{2,1,0:T(8,128)} %copy-done.8, ...), custom_call_target="tpu_custom_call" | custom-call | tf_op jit(solution)/shard_map/near4/pallas_call | solution.py:215
  76.8 5.1 %collective-permute-start.15 = (f32[4,128,128]{2,1,0:T(8,128)}, f32[4,128,128]{2,1,0:T(8,128)S(1)}, u32[]{:S(2)}, u32[]{:S(2)}) collective-permute-start(f32[4,128,128]{2,1,0:T(8,128)} %near4.1.rest_0_.self_ref.other_ref.prior_ref), channel_id=1, source_target_pairs={{0,2},{4,6},{8,10},{12,14},{16,18},{20,22},{24,26},{28,30},{32,34}... | collective-permute-start | bytes 786440 | tf_op jit(solution)/shard_map/ppermute | solution.py:212
  82.6 2.8 %far4.1 = (f32[4,128,128]{2,1,0:T(8,128)}, f32[8,4,128]{2,1,0:T(4,128)}) custom-call(s32[2]{0:T(128)} %pad_add_fusion.flags_ref, f32[4,128,128]{2,1,0:T(8,128)} %get-tuple-element.45.other_ref.self_ref.prior_ref, f32[4,128,128]{2,1,0:T(8,128)} %near3.1.rest_0_.self_ref.other_ref.prior_ref, f32[4,128,128]{2,1,0:T(8,128)} %copy-done.14, ...), custom_call_target="tpu_custom_call" | custom-call | tf_op jit(solution)/shard_map/far4/pallas_call | solution.py:223
  86.2 1.4 collective-permute-done.16.rim_in_ref
  87.5 1.2 collective-permute-done.15.halo_ref
  89.4 2.6 %near5.1.rest_0_.self_ref.other_ref.prior_ref = f32[4,128,128]{2,1,0:T(8,128)} custom-call(s32[2]{0:T(128)} %pad_add_fusion.flags_ref, f32[4,128,128]{2,1,0:T(8,128)} %near4.1.rest_0_.self_ref.other_ref.prior_ref, f32[4,128,128]{2,1,0:T(8,128)} %get-tuple-element.47.other_ref.self_ref.prior_ref, f32[4,128,128]{2,1,0:T(8,128)} %copy-done.9, ...), custom_call_target="tpu_custom_call" | custom-call | tf_op jit(solution)/shard_map/near5/pallas_call | solution.py:215
  92.1 6.1 %collective-permute-start.18 = (f32[4,128,128]{2,1,0:T(8,128)}, f32[4,128,128]{2,1,0:T(8,128)S(1)}, u32[]{:S(2)}, u32[]{:S(2)}) collective-permute-start(f32[4,128,128]{2,1,0:T(8,128)} %near5.1.rest_0_.self_ref.other_ref.prior_ref), channel_id=1, source_target_pairs={{0,2},{4,6},{8,10},{12,14},{16,18},{20,22},{24,26},{28,30},{32,34}... | collective-permute-start | bytes 786440 | tf_op jit(solution)/shard_map/ppermute | solution.py:212
  98.9 2.8 %far5.1 = (f32[4,128,128]{2,1,0:T(8,128)}, f32[8,4,128]{2,1,0:T(4,128)}) custom-call(s32[2]{0:T(128)} %pad_add_fusion.flags_ref, f32[4,128,128]{2,1,0:T(8,128)} %get-tuple-element.47.other_ref.self_ref.prior_ref, f32[4,128,128]{2,1,0:T(8,128)} %near4.1.rest_0_.self_ref.other_ref.prior_ref, f32[4,128,128]{2,1,0:T(8,128)} %copy-done.15, ...), custom_call_target="tpu_custom_call" | custom-call | tf_op jit(solution)/shard_map/far5/pallas_call | solution.py:223
  102.5 1.4 collective-permute-done.19.rim_in_ref
  103.8 1.2 collective-permute-done.18.halo_ref
  105.7 2.6 %near6.1.rest_0_.self_ref.other_ref = f32[4,128,128]{2,1,0:T(8,128)} custom-call(s32[2]{0:T(128)} %pad_add_fusion.flags_ref, f32[4,128,128]{2,1,0:T(8,128)} %near5.1.rest_0_.self_ref.other_ref.prior_ref, f32[4,128,128]{2,1,0:T(8,128)} %get-tuple-element.49.other_ref.self_ref.prior_ref, f32[4,128,128]{2,1,0:T(8,128)} %copy-done.10, f32[8,4,128]{2,1,0:T(4,128)} %copy-done.24, ...), custom_call_target="tpu_custom_call" | custom-call | tf_op jit(solution)/shard_map/near6/pallas_call | solution.py:215
  108.4 4.9 %collective-permute-start.21 = (f32[4,128,128]{2,1,0:T(8,128)}, f32[4,128,128]{2,1,0:T(8,128)S(1)}, u32[]{:S(2)}, u32[]{:S(2)}) collective-permute-start(f32[4,128,128]{2,1,0:T(8,128)} %near6.1.rest_0_.self_ref.other_ref), channel_id=1, source_target_pairs={{0,2},{4,6},{8,10},{12,14},{16,18},{20,22},{24,26},{28,30},{32,34}... | collective-permute-start | bytes 786440 | tf_op jit(solution)/shard_map/ppermute | solution.py:212
  114.0 2.7 %far6.1 = (f32[4,128,128]{2,1,0:T(8,128)}, f32[8,4,128]{2,1,0:T(4,128)}) custom-call(s32[2]{0:T(128)} %pad_add_fusion.flags_ref, f32[4,128,128]{2,1,0:T(8,128)} %get-tuple-element.49.other_ref.self_ref.prior_ref, f32[4,128,128]{2,1,0:T(8,128)} %near5.1.rest_0_.self_ref.other_ref.prior_ref, f32[4,128,128]{2,1,0:T(8,128)} %copy-done.16, ...), custom_call_target="tpu_custom_call" | custom-call | tf_op jit(solution)/shard_map/far6/pallas_call | solution.py:223
  117.5 1.4 collective-permute-done.22.rim_in_ref
  118.9 1.2 collective-permute-done.21.halo_ref
  120.8 2.6 %near7.1.rest_0_.near_ref = f32[4,128,128]{2,1,0:T(8,128)} custom-call(s32[2]{0:T(128)} %pad_add_fusion.flags_ref, f32[4,128,128]{2,1,0:T(8,128)} %near6.1.rest_0_.self_ref.other_ref, f32[4,128,128]{2,1,0:T(8,128)} %get-tuple-element.51.other_ref.self_ref, f32[4,128,128]{2,1,0:T(8,128)} %copy-done.2, f32[8,4,128]{2,1,0:T(4,128)} %copy-done.18, ...), custom_call_target="tpu_custom_call" | custom-call | tf_op jit(solution)/shard_map/near7/pallas_call | solution.py:215
  124.2 2.7 %far7.1 = (f32[4,128,128]{2,1,0:T(8,128)}, f32[8,4,128]{2,1,0:T(4,128)}) custom-call(s32[2]{0:T(128)} %pad_add_fusion.flags_ref, f32[4,128,128]{2,1,0:T(8,128)} %get-tuple-element.51.other_ref.self_ref, f32[4,128,128]{2,1,0:T(8,128)} %near6.1.rest_0_.self_ref.other_ref, f32[4,128,128]{2,1,0:T(8,128)} %copy-done.3, f32[8,4,128]{2,1,0:T(4,128)} %copy-done.18, ...), custom_call_target="tpu_custom_call" | custom-call | tf_op jit(solution)/shard_map/far7/pallas_call | solution.py:223
  126.9 2.4 %close.1 = (f32[1024,128]{1,0:T(8,128)}, f32[1024,128]{1,0:T(8,128)}) custom-call(s32[2]{0:T(128)} %pad_add_fusion.flags_ref, f32[4,128,128]{2,1,0:T(8,128)} %near7.1.rest_0_.near_ref, f32[4,128,128]{2,1,0:T(8,128)} %get-tuple-element.53.far_ref, f32[1024,128]{1,0:T(8,128)} %bitcast.21, s32[8,128]{1,0:T(8,128)} %receiver_depth_ref.1), custom_call_target="tpu_custom_call" | custom-call | tf_op jit(solution)/shard_map/close/pallas_call | solution.py:233
  129.3 87.2 %all_to_all.18 = f32[128,8,128]{2,1,0:T(8,128)S(1)} all-to-all(f32[128,8,128]{2,1,0:T(8,128)} %bitcast.20), channel_id=1, replica_groups=mesh['shots'=4,'gx'=32,'gy'=2] {'gx'}, dimensions={0} | all-to-all | bytes 1048576 | tf_op jit(solution)/shard_map/all_to_all | solution.py:241
  216.5 0.8 copy.12
  (73 shorter events, 16.7 us)
Async XLA Ops:
  1.3 5.0 %copy-start = (bf16[128,8,128]{2,1,0:T(8,128)(2,1)S(1)}, bf16[128,8,128]{2,1,0:T(8,128)(2,1)}, u32[]{:S(2)}) copy-start(bf16[128,8,128]{2,1,0:T(8,128)(2,1)} %param.10) | copy-start | bytes 786436
  3.4 8.7 %collective-permute-start = (f32[4,128,128]{2,1,0:T(8,128)}, f32[4,128,128]{2,1,0:T(8,128)S(1)}, u32[]{:S(2)}, u32[]{:S(2)}) collective-permute-start(f32[4,128,128]{2,1,0:T(8,128)} %get-tuple-element.29.self_ref.other_ref.prior_ref), channel_id=1, source_target_pairs={{0,2},{4,6},{8,10},{12,14},{16,18},{20,22},{24,26},{28,30},{32,34}... | collective-permute-start | bytes 786440 | tf_op jit(solution)/shard_map/ppermute | solution.py:212
  5.5 13.4 %collective-permute-start.2 = (f32[4,128,128]{2,1,0:T(8,128)}, f32[4,128,128]{2,1,0:T(8,128)S(1)}, u32[]{:S(2)}, u32[]{:S(2)}) collective-permute-start(f32[4,128,128]{2,1,0:T(8,128)} %get-tuple-element.30.other_ref.self_ref.prior_ref), channel_id=1, source_target_pairs={{2,4},{6,8},{10,12},{14,16},{18,20},{22,24},{26,28},{30,32},{34,36... | collective-permute-start | bytes 786440 | tf_op jit(solution)/shard_map/ppermute | solution.py:213
  6.2 3.9 %collective-permute-start.1 = (f32[8,4,128]{2,1,0:T(4,128)}, f32[8,4,128]{2,1,0:T(4,128)S(1)}, u32[]{:S(2)}, u32[]{:S(2)}) collective-permute-start(f32[8,4,128]{2,1,0:T(4,128)} %get-tuple-element.31), channel_id=1, source_target_pairs={{0,1},{1,0},{2,3},{3,2},{4,5},{5,4},{6,7},{7,6},{8,9},{9,8},{10,11... | collective-permute-start | bytes 49160 | tf_op jit(solution)/shard_map/ppermute | solution.py:214
  10.1 2.0 copy-start.17
  15.4 10.7 %collective-permute-start.3 = (f32[4,128,128]{2,1,0:T(8,128)}, f32[4,128,128]{2,1,0:T(8,128)S(1)}, u32[]{:S(2)}, u32[]{:S(2)}) collective-permute-start(f32[4,128,128]{2,1,0:T(8,128)} %near0.1.rest_0_.self_ref.other_ref.prior_ref), channel_id=1, source_target_pairs={{0,2},{4,6},{8,10},{12,14},{16,18},{20,22},{24,26},{28,30},{32,34}... | collective-permute-start | bytes 786440 | tf_op jit(solution)/shard_map/ppermute | solution.py:212
  19.0 0.7 copy-start.1
  22.4 12.8 %collective-permute-start.5 = (f32[4,128,128]{2,1,0:T(8,128)}, f32[4,128,128]{2,1,0:T(8,128)S(1)}, u32[]{:S(2)}, u32[]{:S(2)}) collective-permute-start(f32[4,128,128]{2,1,0:T(8,128)} %get-tuple-element.39.other_ref.self_ref.prior_ref), channel_id=1, source_target_pairs={{2,4},{6,8},{10,12},{14,16},{18,20},{22,24},{26,28},{30,32},{34,36... | collective-permute-start | bytes 786440 | tf_op jit(solution)/shard_map/ppermute | solution.py:213
  23.1 1.5 collective-permute-start.4
  24.6 1.5 copy-start.19
  26.1 0.7 copy-start.4
  29.5 12.6 %collective-permute-start.6 = (f32[4,128,128]{2,1,0:T(8,128)}, f32[4,128,128]{2,1,0:T(8,128)S(1)}, u32[]{:S(2)}, u32[]{:S(2)}) collective-permute-start(f32[4,128,128]{2,1,0:T(8,128)} %near1.1.rest_0_.self_ref.other_ref.prior_ref), channel_id=1, source_target_pairs={{0,2},{4,6},{8,10},{12,14},{16,18},{20,22},{24,26},{28,30},{32,34}... | collective-permute-start | bytes 786440 | tf_op jit(solution)/shard_map/ppermute | solution.py:212
  35.2 0.7 copy-start.11
  38.7 11.6 %collective-permute-start.8 = (f32[4,128,128]{2,1,0:T(8,128)}, f32[4,128,128]{2,1,0:T(8,128)S(1)}, u32[]{:S(2)}, u32[]{:S(2)}) collective-permute-start(f32[4,128,128]{2,1,0:T(8,128)} %get-tuple-element.41.other_ref.self_ref.prior_ref), channel_id=1, source_target_pairs={{2,4},{6,8},{10,12},{14,16},{18,20},{22,24},{26,28},{30,32},{34,36... | collective-permute-start | bytes 786440 | tf_op jit(solution)/shard_map/ppermute | solution.py:213
  39.4 1.5 collective-permute-start.7
  40.9 1.2 copy-start.20
  42.1 0.7 copy-start.6
  45.4 11.7 %collective-permute-start.9 = (f32[4,128,128]{2,1,0:T(8,128)}, f32[4,128,128]{2,1,0:T(8,128)S(1)}, u32[]{:S(2)}, u32[]{:S(2)}) collective-permute-start(f32[4,128,128]{2,1,0:T(8,128)} %near2.1.rest_0_.self_ref.other_ref.prior_ref), channel_id=1, source_target_pairs={{0,2},{4,6},{8,10},{12,14},{16,18},{20,22},{24,26},{28,30},{32,34}... | collective-permute-start | bytes 786440 | tf_op jit(solution)/shard_map/ppermute | solution.py:212
  50.3 0.7 copy-start.12
  53.8 12.8 %collective-permute-start.11 = (f32[4,128,128]{2,1,0:T(8,128)}, f32[4,128,128]{2,1,0:T(8,128)S(1)}, u32[]{:S(2)}, u32[]{:S(2)}) collective-permute-start(f32[4,128,128]{2,1,0:T(8,128)} %get-tuple-element.43.other_ref.self_ref.prior_ref), channel_id=1, source_target_pairs={{2,4},{6,8},{10,12},{14,16},{18,20},{22,24},{26,28},{30,32},{34,36... | collective-permute-start | bytes 786440 | tf_op jit(solution)/shard_map/ppermute | solution.py:213
  54.5 1.5 collective-permute-start.10
  56.0 1.2 copy-start.21
  57.2 0.7 copy-start.7
  60.5 12.9 %collective-permute-start.12 = (f32[4,128,128]{2,1,0:T(8,128)}, f32[4,128,128]{2,1,0:T(8,128)S(1)}, u32[]{:S(2)}, u32[]{:S(2)}) collective-permute-start(f32[4,128,128]{2,1,0:T(8,128)} %near3.1.rest_0_.self_ref.other_ref.prior_ref), channel_id=1, source_target_pairs={{0,2},{4,6},{8,10},{12,14},{16,18},{20,22},{24,26},{28,30},{32,34}... | collective-permute-start | bytes 786440 | tf_op jit(solution)/shard_map/ppermute | solution.py:212
  66.6 0.7 copy-start.13
  70.1 11.8 %collective-permute-start.14 = (f32[4,128,128]{2,1,0:T(8,128)}, f32[4,128,128]{2,1,0:T(8,128)S(1)}, u32[]{:S(2)}, u32[]{:S(2)}) collective-permute-start(f32[4,128,128]{2,1,0:T(8,128)} %get-tuple-element.45.other_ref.self_ref.prior_ref), channel_id=1, source_target_pairs={{2,4},{6,8},{10,12},{14,16},{18,20},{22,24},{26,28},{30,32},{34,36... | collective-permute-start | bytes 786440 | tf_op jit(solution)/shard_map/ppermute | solution.py:213
  70.7 1.7 collective-permute-start.13
  72.4 1.0 copy-start.22
  73.5 0.7 copy-start.8
  76.8 11.9 %collective-permute-start.15 = (f32[4,128,128]{2,1,0:T(8,128)}, f32[4,128,128]{2,1,0:T(8,128)S(1)}, u32[]{:S(2)}, u32[]{:S(2)}) collective-permute-start(f32[4,128,128]{2,1,0:T(8,128)} %near4.1.rest_0_.self_ref.other_ref.prior_ref), channel_id=1, source_target_pairs={{0,2},{4,6},{8,10},{12,14},{16,18},{20,22},{24,26},{28,30},{32,34}... | collective-permute-start | bytes 786440 | tf_op jit(solution)/shard_map/ppermute | solution.py:212
  81.9 0.7 copy-start.14
  85.3 12.8 %collective-permute-start.17 = (f32[4,128,128]{2,1,0:T(8,128)}, f32[4,128,128]{2,1,0:T(8,128)S(1)}, u32[]{:S(2)}, u32[]{:S(2)}) collective-permute-start(f32[4,128,128]{2,1,0:T(8,128)} %get-tuple-element.47.other_ref.self_ref.prior_ref), channel_id=1, source_target_pairs={{2,4},{6,8},{10,12},{14,16},{18,20},{22,24},{26,28},{30,32},{34,36... | collective-permute-start | bytes 786440 | tf_op jit(solution)/shard_map/ppermute | solution.py:213
  86.0 1.5 collective-permute-start.16
  87.5 1.2 copy-start.23
  88.7 0.7 copy-start.9
  92.1 13.0 %collective-permute-start.18 = (f32[4,128,128]{2,1,0:T(8,128)}, f32[4,128,128]{2,1,0:T(8,128)S(1)}, u32[]{:S(2)}, u32[]{:S(2)}) collective-permute-start(f32[4,128,128]{2,1,0:T(8,128)} %near5.1.rest_0_.self_ref.other_ref.prior_ref), channel_id=1, source_target_pairs={{0,2},{4,6},{8,10},{12,14},{16,18},{20,22},{24,26},{28,30},{32,34}... | collective-permute-start | bytes 786440 | tf_op jit(solution)/shard_map/ppermute | solution.py:212
  98.2 0.7 copy-start.15
  101.7 11.6 %collective-permute-start.20 = (f32[4,128,128]{2,1,0:T(8,128)}, f32[4,128,128]{2,1,0:T(8,128)S(1)}, u32[]{:S(2)}, u32[]{:S(2)}) collective-permute-start(f32[4,128,128]{2,1,0:T(8,128)} %get-tuple-element.49.other_ref.self_ref.prior_ref), channel_id=1, source_target_pairs={{2,4},{6,8},{10,12},{14,16},{18,20},{22,24},{26,28},{30,32},{34,36... | collective-permute-start | bytes 786440 | tf_op jit(solution)/shard_map/ppermute | solution.py:213
  102.3 1.5 collective-permute-start.19
  103.8 1.2 copy-start.24
  105.0 0.7 copy-start.10
  108.4 11.8 %collective-permute-start.21 = (f32[4,128,128]{2,1,0:T(8,128)}, f32[4,128,128]{2,1,0:T(8,128)S(1)}, u32[]{:S(2)}, u32[]{:S(2)}) collective-permute-start(f32[4,128,128]{2,1,0:T(8,128)} %near6.1.rest_0_.self_ref.other_ref), channel_id=1, source_target_pairs={{0,2},{4,6},{8,10},{12,14},{16,18},{20,22},{24,26},{28,30},{32,34}... | collective-permute-start | bytes 786440 | tf_op jit(solution)/shard_map/ppermute | solution.py:212
  113.3 0.7 copy-start.16
  116.7 6.7 %collective-permute-start.23 = (f32[4,128,128]{2,1,0:T(8,128)}, f32[4,128,128]{2,1,0:T(8,128)S(1)}, u32[]{:S(2)}, u32[]{:S(2)}) collective-permute-start(f32[4,128,128]{2,1,0:T(8,128)} %get-tuple-element.51.other_ref.self_ref), channel_id=1, source_target_pairs={{2,4},{6,8},{10,12},{14,16},{18,20},{22,24},{26,28},{30,32},{34,36... | collective-permute-start | bytes 786440 | tf_op jit(solution)/shard_map/ppermute | solution.py:213
  117.4 1.5 collective-permute-start.22
  118.9 1.2 copy-start.18
  120.1 0.7 copy-start.2
  123.5 0.7 copy-start.3
  (1 other events, 0.7 us)

commit v2 on v1

--- a/solution.py
+++ b/solution.py
@@ -17,6 +17,7 @@
 VM = pl.BlockSpec(memory_space=pltpu.VMEM)
 SM = pl.BlockSpec(memory_space=pltpu.SMEM)
 F32 = jnp.float32
+PARAMS = pltpu.CompilerParams(vmem_limit_bytes=8 * 2**20)
 
 
 def split_planes(src_ref, odd, put):
@@ -191,14 +192,14 @@
     square = jax.ShapeDtypeStruct((length, length), F32)
 
     near, far, edge = pl.pallas_call(
-        open_kernel, out_shape=(half, half, rims), in_specs=[SM, VM], out_specs=(VM, VM, VM), name="open"
+        open_kernel, out_shape=(half, half, rims), in_specs=[SM, VM], out_specs=(VM, VM, VM), compiler_params=PARAMS, name="open"
     )(flags, pressure.reshape(flat))
     near_prior, far_prior, near_coef, far_coef, near_mark, far_mark, amp = pl.pallas_call(
         tables_kernel,
         out_shape=(half,) * 6 + (square,),
         in_specs=[SM, SM] + [VM] * 4,
         out_specs=(VM,) * 7,
-        name="tables",
+        compiler_params=PARAMS, name="tables",
     )(
         flags,
         wavelet,
@@ -218,7 +219,7 @@
             in_specs=[SM] + [VM] * 8,
             out_specs=VM,
             scratch_shapes=scratch,
-            name=f"near{step}",
+            compiler_params=PARAMS, name=f"near{step}",
         )(flags, near, far, near_halo, edge_in, near_prior, near_coef, near_mark, amp)
         far_next, edge = pl.pallas_call(
             functools.partial(advance_kernel, step, 1),
@@ -226,7 +227,7 @@
             in_specs=[SM] + [VM] * 9,
             out_specs=(VM, VM),
             scratch_shapes=scratch,
-            name=f"far{step}",
+            compiler_params=PARAMS, name=f"far{step}",
         )(flags, far, near, far_halo, edge_in, far_prior, far_coef, far_mark, amp, near_next)
         near_prior, far_prior = near, far
         near, far = near_next, far_next
@@ -236,7 +237,7 @@
         in_specs=[SM] + [VM] * 4,
         out_specs=(VM, VM),
         scratch_shapes=[pltpu.VMEM(flat, F32)],
-        name="close",
+        compiler_params=PARAMS, name="close",
     )(flags, near, far, receiver_field.reshape(flat), receiver_depth)
     image = lax.all_to_all(filtered.reshape(depth, width, length), "gx", split_axis=0, concat_axis=1, tiled=True)
     return final.reshape(depth, width, length), image

time: 218 us -> 188 us (0.86)
  Pallas kernels: 50.5 us -> 23.2 us
  waiting for transfers between devices: 19.9 us -> 35.9 us
  starting transfers between devices: 45.3 us -> 31.5 us
  local copies, waits for them, and re-layouts: 12.1 us -> 2.54 us
  blocking collectives: 87.2 us -> 93.1 us
    ppermute x8, waiting for transfers between devices: 10.5 us -> 28 us  [shards(): near_halo = lax.ppermute(near, 'gx', even)]
    ppermute x8, starting transfers between devices: 38.5 us -> 24.6 us  [shards(): near_halo = lax.ppermute(near, 'gx', even)]
    pallas_call x8, Pallas kernels: 22 us -> 9.83 us  [shards(): pl.pallas_call(functools.partial(advance_kernel, step, 1), out_shape=(hal...]
    pallas_call x8, Pallas kernels: 21.1 us -> 9.7 us  [shards(): pl.pallas_call(functools.partial(advance_kernel, step, 0), out_shape=half...]
    unnamed x50 -> x16, local copies, waits for them, and re-layouts: 11.3 us -> 1.71 us
    all_to_all x1, blocking collectives: 87.2 us -> 93.1 us  [shards(): lax.all_to_all(filtered.reshape(depth, width, length), 'gx', split_axis=0...]
  transfers between devices with their start and end apart: 24 -> 24, of which waited for: 15 -> 15; matrix products, arithmetic and copies ran while one was open for 0% -> 0% of each run, Pallas kernels for 20% -> 10%
where the time goes in v2:
time: 188 us; the launch traced here: 187 us
  blocking collectives  93.1 us (50%)
  waiting for transfers between devices  35.9 us (19%)
  starting transfers between devices  31.5 us (17%)
  Pallas kernels  23.2 us (12%)
  local copies, waits for them, and re-layouts  2.54 us (1%)
    all_to_all x1, blocking collectives, shards(): lax.all_to_all(filtered.reshape(depth, width, length), 'gx', split_axis=0...  93.1 us
    ppermute x8, waiting for transfers between devices, shards(): near_halo = lax.ppermute(near, 'gx', even)  28 us
    ppermute x8, starting transfers between devices, shards(): near_halo = lax.ppermute(near, 'gx', even)  24.6 us
    pallas_call x8, Pallas kernels, shards(): pl.pallas_call(functools.partial(advance_kernel, step, 1), out_shape=(hal...  9.83 us
    pallas_call x8, Pallas kernels, shards(): pl.pallas_call(functools.partial(advance_kernel, step, 0), out_shape=half...  9.7 us
    ppermute x8, waiting for transfers between devices, shards(): edge_in = lax.ppermute(edge, 'gy', swap)  7.96 us
    ppermute x8, starting transfers between devices, shards(): far_halo = lax.ppermute(far, 'gx', uneven)  5.41 us
  transfers between devices with their start and end apart: 24, of which 15 were waited for; matrix products, arithmetic and copies ran while one was open for 0% of the time, Pallas kernels for 10%

profile of v2, /device:TPU:46, one launch (start us, length us, event | category | flops | bytes accessed | tf_op | source)
XLA Modules:
  0.0 187.4 jit_solution(17522848196729755911)
XLA Ops:
  0.7 1.0 copy-done.1
  1.8 0.7 open.1
  2.5 2.2 %collective-permute-start = (f32[4,128,128]{2,1,0:T(8,128)S(1)}, f32[4,128,128]{2,1,0:T(8,128)S(1)}, u32[]{:S(2)}, u32[]{:S(2)}) collective-permute-start(f32[4,128,128]{2,1,0:T(8,128)S(1)} %get-tuple-element.29.self_ref.other_ref.prior_ref), channel_id=1, source_target_pairs={{0,2},{4,6},{8,10},{12,14},{16,18},{20,22},{24,26},{28,30},{32,34}... | collective-permute-start | bytes 786440 | tf_op jit(solution)/shard_map/ppermute | solution.py:213
  6.3 1.4 tables.1
  7.7 3.4 %collective-permute-done.halo_ref = f32[4,128,128]{2,1,0:T(8,128)S(1)} collective-permute-done((f32[4,128,128]{2,1,0:T(8,128)S(1)}, f32[4,128,128]{2,1,0:T(8,128)S(1)}, u32[]{:S(2)}, u32[]{:S(2)}) %collective-permute-start) | collective-permute-done | bytes 262176 | tf_op jit(solution)/shard_map/ppermute | solution.py:213
  11.2 1.2 near0.1.rest_0_.self_ref.other_ref.prior_ref
  12.3 2.2 %collective-permute-start.3 = (f32[4,128,128]{2,1,0:T(8,128)S(1)}, f32[4,128,128]{2,1,0:T(8,128)S(1)}, u32[]{:S(2)}, u32[]{:S(2)}) collective-permute-start(f32[4,128,128]{2,1,0:T(8,128)S(1)} %near0.1.rest_0_.self_ref.other_ref.prior_ref), channel_id=1, source_target_pairs={{0,2},{4,6},{8,10},{12,14},{16,18},{20,22},{24,26},{28,30},{32,34}... | collective-permute-start | bytes 786440 | tf_op jit(solution)/shard_map/ppermute | solution.py:213
  14.6 1.1 far0.1
  15.7 0.7 collective-permute-start.5
  16.7 1.0 collective-permute-done.4.rim_in_ref
  17.7 3.8 %collective-permute-done.3.halo_ref = f32[4,128,128]{2,1,0:T(8,128)S(1)} collective-permute-done((f32[4,128,128]{2,1,0:T(8,128)S(1)}, f32[4,128,128]{2,1,0:T(8,128)S(1)}, u32[]{:S(2)}, u32[]{:S(2)}) %collective-permute-start.3) | collective-permute-done | bytes 262176 | tf_op jit(solution)/shard_map/ppermute | solution.py:213
  21.5 1.2 near1.1.rest_0_.self_ref.other_ref.prior_ref
  22.7 3.0 %collective-permute-start.6 = (f32[4,128,128]{2,1,0:T(8,128)S(1)}, f32[4,128,128]{2,1,0:T(8,128)S(1)}, u32[]{:S(2)}, u32[]{:S(2)}) collective-permute-start(f32[4,128,128]{2,1,0:T(8,128)S(1)} %near1.1.rest_0_.self_ref.other_ref.prior_ref), channel_id=1, source_target_pairs={{0,2},{4,6},{8,10},{12,14},{16,18},{20,22},{24,26},{28,30},{32,34}... | collective-permute-start | bytes 786440 | tf_op jit(solution)/shard_map/ppermute | solution.py:213
  25.7 1.2 far1.1
  27.7 1.2 collective-permute-done.7.rim_in_ref
  28.9 3.5 %collective-permute-done.6.halo_ref = f32[4,128,128]{2,1,0:T(8,128)S(1)} collective-permute-done((f32[4,128,128]{2,1,0:T(8,128)S(1)}, f32[4,128,128]{2,1,0:T(8,128)S(1)}, u32[]{:S(2)}, u32[]{:S(2)}) %collective-permute-start.6) | collective-permute-done | bytes 262176 | tf_op jit(solution)/shard_map/ppermute | solution.py:213
  32.4 1.2 near2.1.rest_0_.self_ref.other_ref.prior_ref
  33.6 3.6 %collective-permute-start.9 = (f32[4,128,128]{2,1,0:T(8,128)S(1)}, f32[4,128,128]{2,1,0:T(8,128)S(1)}, u32[]{:S(2)}, u32[]{:S(2)}) collective-permute-start(f32[4,128,128]{2,1,0:T(8,128)S(1)} %near2.1.rest_0_.self_ref.other_ref.prior_ref), channel_id=1, source_target_pairs={{0,2},{4,6},{8,10},{12,14},{16,18},{20,22},{24,26},{28,30},{32,34}... | collective-permute-start | bytes 786440 | tf_op jit(solution)/shard_map/ppermute | solution.py:213
  37.2 1.2 far2.1
  39.2 1.2 collective-permute-done.10.rim_in_ref
  40.4 3.5 %collective-permute-done.9.halo_ref = f32[4,128,128]{2,1,0:T(8,128)S(1)} collective-permute-done((f32[4,128,128]{2,1,0:T(8,128)S(1)}, f32[4,128,128]{2,1,0:T(8,128)S(1)}, u32[]{:S(2)}, u32[]{:S(2)}) %collective-permute-start.9) | collective-permute-done | bytes 262176 | tf_op jit(solution)/shard_map/ppermute | solution.py:213
  43.9 1.2 near3.1.rest_0_.self_ref.other_ref.prior_ref
  45.1 3.4 %collective-permute-start.12 = (f32[4,128,128]{2,1,0:T(8,128)S(1)}, f32[4,128,128]{2,1,0:T(8,128)S(1)}, u32[]{:S(2)}, u32[]{:S(2)}) collective-permute-start(f32[4,128,128]{2,1,0:T(8,128)S(1)} %near3.1.rest_0_.self_ref.other_ref.prior_ref), channel_id=1, source_target_pairs={{0,2},{4,6},{8,10},{12,14},{16,18},{20,22},{24,26},{28,30},{32,34}... | collective-permute-start | bytes 786440 | tf_op jit(solution)/shard_map/ppermute | solution.py:213
  48.5 1.2 far3.1
  49.6 0.7 collective-permute-start.14
  50.6 1.2 collective-permute-done.13.rim_in_ref
  51.8 3.3 %collective-permute-done.12.halo_ref = f32[4,128,128]{2,1,0:T(8,128)S(1)} collective-permute-done((f32[4,128,128]{2,1,0:T(8,128)S(1)}, f32[4,128,128]{2,1,0:T(8,128)S(1)}, u32[]{:S(2)}, u32[]{:S(2)}) %collective-permute-start.12) | collective-permute-done | bytes 262176 | tf_op jit(solution)/shard_map/ppermute | solution.py:213
  55.1 1.2 near4.1.rest_0_.self_ref.other_ref.prior_ref
  56.3 3.5 %collective-permute-start.15 = (f32[4,128,128]{2,1,0:T(8,128)S(1)}, f32[4,128,128]{2,1,0:T(8,128)S(1)}, u32[]{:S(2)}, u32[]{:S(2)}) collective-permute-start(f32[4,128,128]{2,1,0:T(8,128)S(1)} %near4.1.rest_0_.self_ref.other_ref.prior_ref), channel_id=1, source_target_pairs={{0,2},{4,6},{8,10},{12,14},{16,18},{20,22},{24,26},{28,30},{32,34}... | collective-permute-start | bytes 786440 | tf_op jit(solution)/shard_map/ppermute | solution.py:213
  59.8 1.1 far4.1
  60.9 0.7 collective-permute-start.17
  61.8 1.2 collective-permute-done.16.rim_in_ref
  62.9 3.5 %collective-permute-done.15.halo_ref = f32[4,128,128]{2,1,0:T(8,128)S(1)} collective-permute-done((f32[4,128,128]{2,1,0:T(8,128)S(1)}, f32[4,128,128]{2,1,0:T(8,128)S(1)}, u32[]{:S(2)}, u32[]{:S(2)}) %collective-permute-start.15) | collective-permute-done | bytes 262176 | tf_op jit(solution)/shard_map/ppermute | solution.py:213
  66.4 1.2 near5.1.rest_0_.self_ref.other_ref.prior_ref
  67.7 3.3 %collective-permute-start.18 = (f32[4,128,128]{2,1,0:T(8,128)S(1)}, f32[4,128,128]{2,1,0:T(8,128)S(1)}, u32[]{:S(2)}, u32[]{:S(2)}) collective-permute-start(f32[4,128,128]{2,1,0:T(8,128)S(1)} %near5.1.rest_0_.self_ref.other_ref.prior_ref), channel_id=1, source_target_pairs={{0,2},{4,6},{8,10},{12,14},{16,18},{20,22},{24,26},{28,30},{32,34}... | collective-permute-start | bytes 786440 | tf_op jit(solution)/shard_map/ppermute | solution.py:213
  71.0 1.1 far5.1
  73.0 1.2 collective-permute-done.19.rim_in_ref
  74.1 3.5 %collective-permute-done.18.halo_ref = f32[4,128,128]{2,1,0:T(8,128)S(1)} collective-permute-done((f32[4,128,128]{2,1,0:T(8,128)S(1)}, f32[4,128,128]{2,1,0:T(8,128)S(1)}, u32[]{:S(2)}, u32[]{:S(2)}) %collective-permute-start.18) | collective-permute-done | bytes 262176 | tf_op jit(solution)/shard_map/ppermute | solution.py:213
  77.6 1.2 near6.1.rest_0_.self_ref.other_ref
  78.9 3.3 %collective-permute-start.21 = (f32[4,128,128]{2,1,0:T(8,128)S(1)}, f32[4,128,128]{2,1,0:T(8,128)S(1)}, u32[]{:S(2)}, u32[]{:S(2)}) collective-permute-start(f32[4,128,128]{2,1,0:T(8,128)S(1)} %near6.1.rest_0_.self_ref.other_ref), channel_id=1, source_target_pairs={{0,2},{4,6},{8,10},{12,14},{16,18},{20,22},{24,26},{28,30},{32,34}... | collective-permute-start | bytes 786440 | tf_op jit(solution)/shard_map/ppermute | solution.py:213
  82.2 1.2 far6.1
  84.2 1.2 collective-permute-done.22.rim_in_ref
  85.4 3.5 %collective-permute-done.21.halo_ref = f32[4,128,128]{2,1,0:T(8,128)S(1)} collective-permute-done((f32[4,128,128]{2,1,0:T(8,128)S(1)}, f32[4,128,128]{2,1,0:T(8,128)S(1)}, u32[]{:S(2)}, u32[]{:S(2)}) %collective-permute-start.21) | collective-permute-done | bytes 262176 | tf_op jit(solution)/shard_map/ppermute | solution.py:213
  88.8 1.2 near7.1.rest_0_.near_ref
  90.1 1.8 far7.1
  91.9 1.6 close.1
  93.4 93.1 %all_to_all.18 = f32[128,8,128]{2,1,0:T(8,128)S(1)} all-to-all(f32[128,8,128]{2,1,0:T(8,128)S(1)} %bitcast.18), channel_id=1, replica_groups=mesh['shots'=4,'gx'=32,'gy'=2] {'gx'}, dimensions={0} | all-to-all | bytes 1048576 | tf_op jit(solution)/shard_map/all_to_all | solution.py:242
  186.5 0.8 copy.12
  (39 shorter events, 5.7 us)
Async XLA Ops:
  0.7 1.0 copy-start.1
  1.8 3.8 %copy-start.7 = (bf16[128,8,128]{2,1,0:T(8,128)(2,1)S(1)}, bf16[128,8,128]{2,1,0:T(8,128)(2,1)}, u32[]{:S(2)}) copy-start(bf16[128,8,128]{2,1,0:T(8,128)(2,1)} %param.10) | copy-start | bytes 786436
  2.5 3.2 %copy-start = (f32[128,8,128]{2,1,0:T(8,128)S(1)}, f32[128,8,128]{2,1,0:T(8,128)}, u32[]{:S(2)}) copy-start(f32[128,8,128]{2,1,0:T(8,128)} %param.9) | copy-start | bytes 1572868
  2.5 8.6 %collective-permute-start = (f32[4,128,128]{2,1,0:T(8,128)S(1)}, f32[4,128,128]{2,1,0:T(8,128)S(1)}, u32[]{:S(2)}, u32[]{:S(2)}) collective-permute-start(f32[4,128,128]{2,1,0:T(8,128)S(1)} %get-tuple-element.29.self_ref.other_ref.prior_ref), channel_id=1, source_target_pairs={{0,2},{4,6},{8,10},{12,14},{16,18},{20,22},{24,26},{28,30},{32,34}... | collective-permute-start | bytes 786440 | tf_op jit(solution)/shard_map/ppermute | solution.py:213
  4.8 9.8 %collective-permute-start.2 = (f32[4,128,128]{2,1,0:T(8,128)S(1)}, f32[4,128,128]{2,1,0:T(8,128)S(1)}, u32[]{:S(2)}, u32[]{:S(2)}) collective-permute-start(f32[4,128,128]{2,1,0:T(8,128)S(1)} %get-tuple-element.30.other_ref.self_ref.prior_ref), channel_id=1, source_target_pairs={{2,4},{6,8},{10,12},{14,16},{18,20},{22,24},{26,28},{30,32},{34,36... | collective-permute-start | bytes 786440 | tf_op jit(solution)/shard_map/ppermute | solution.py:214
  5.4 2.3 %collective-permute-start.1 = (f32[8,4,128]{2,1,0:T(4,128)S(1)}, f32[8,4,128]{2,1,0:T(4,128)S(1)}, u32[]{:S(2)}, u32[]{:S(2)}) collective-permute-start(f32[8,4,128]{2,1,0:T(4,128)S(1)} %get-tuple-element.31), channel_id=1, source_target_pairs={{0,1},{1,0},{2,3},{3,2},{4,5},{5,4},{6,7},{7,6},{8,9},{9,8},{10,11... | collective-permute-start | bytes 49160 | tf_op jit(solution)/shard_map/ppermute | solution.py:215
  5.6 0.7 copy-start.3
  5.6 0.7 copy-start.4
  5.7 0.7 copy-start.6
  12.3 9.2 %collective-permute-start.3 = (f32[4,128,128]{2,1,0:T(8,128)S(1)}, f32[4,128,128]{2,1,0:T(8,128)S(1)}, u32[]{:S(2)}, u32[]{:S(2)}) collective-permute-start(f32[4,128,128]{2,1,0:T(8,128)S(1)} %near0.1.rest_0_.self_ref.other_ref.prior_ref), channel_id=1, source_target_pairs={{0,2},{4,6},{8,10},{12,14},{16,18},{20,22},{24,26},{28,30},{32,34}... | collective-permute-start | bytes 786440 | tf_op jit(solution)/shard_map/ppermute | solution.py:213
  15.7 10.1 %collective-permute-start.5 = (f32[4,128,128]{2,1,0:T(8,128)S(1)}, f32[4,128,128]{2,1,0:T(8,128)S(1)}, u32[]{:S(2)}, u32[]{:S(2)}) collective-permute-start(f32[4,128,128]{2,1,0:T(8,128)S(1)} %get-tuple-element.39.other_ref.self_ref.prior_ref), channel_id=1, source_target_pairs={{2,4},{6,8},{10,12},{14,16},{18,20},{22,24},{26,28},{30,32},{34,36... | collective-permute-start | bytes 786440 | tf_op jit(solution)/shard_map/ppermute | solution.py:214
  16.4 1.3 collective-permute-start.4
  22.7 9.7 %collective-permute-start.6 = (f32[4,128,128]{2,1,0:T(8,128)S(1)}, f32[4,128,128]{2,1,0:T(8,128)S(1)}, u32[]{:S(2)}, u32[]{:S(2)}) collective-permute-start(f32[4,128,128]{2,1,0:T(8,128)S(1)} %near1.1.rest_0_.self_ref.other_ref.prior_ref), channel_id=1, source_target_pairs={{0,2},{4,6},{8,10},{12,14},{16,18},{20,22},{24,26},{28,30},{32,34}... | collective-permute-start | bytes 786440 | tf_op jit(solution)/shard_map/ppermute | solution.py:213
  26.9 10.3 %collective-permute-start.8 = (f32[4,128,128]{2,1,0:T(8,128)S(1)}, f32[4,128,128]{2,1,0:T(8,128)S(1)}, u32[]{:S(2)}, u32[]{:S(2)}) collective-permute-start(f32[4,128,128]{2,1,0:T(8,128)S(1)} %get-tuple-element.41.other_ref.self_ref.prior_ref), channel_id=1, source_target_pairs={{2,4},{6,8},{10,12},{14,16},{18,20},{22,24},{26,28},{30,32},{34,36... | collective-permute-start | bytes 786440 | tf_op jit(solution)/shard_map/ppermute | solution.py:214
  27.6 1.3 collective-permute-start.7
  33.6 10.3 %collective-permute-start.9 = (f32[4,128,128]{2,1,0:T(8,128)S(1)}, f32[4,128,128]{2,1,0:T(8,128)S(1)}, u32[]{:S(2)}, u32[]{:S(2)}) collective-permute-start(f32[4,128,128]{2,1,0:T(8,128)S(1)} %near2.1.rest_0_.self_ref.other_ref.prior_ref), channel_id=1, source_target_pairs={{0,2},{4,6},{8,10},{12,14},{16,18},{20,22},{24,26},{28,30},{32,34}... | collective-permute-start | bytes 786440 | tf_op jit(solution)/shard_map/ppermute | solution.py:213
  38.4 10.1 %collective-permute-start.11 = (f32[4,128,128]{2,1,0:T(8,128)S(1)}, f32[4,128,128]{2,1,0:T(8,128)S(1)}, u32[]{:S(2)}, u32[]{:S(2)}) collective-permute-start(f32[4,128,128]{2,1,0:T(8,128)S(1)} %get-tuple-element.43.other_ref.self_ref.prior_ref), channel_id=1, source_target_pairs={{2,4},{6,8},{10,12},{14,16},{18,20},{22,24},{26,28},{30,32},{34,36... | collective-permute-start | bytes 786440 | tf_op jit(solution)/shard_map/ppermute | solution.py:214
  39.1 1.3 collective-permute-start.10
  45.1 10.0 %collective-permute-start.12 = (f32[4,128,128]{2,1,0:T(8,128)S(1)}, f32[4,128,128]{2,1,0:T(8,128)S(1)}, u32[]{:S(2)}, u32[]{:S(2)}) collective-permute-start(f32[4,128,128]{2,1,0:T(8,128)S(1)} %near3.1.rest_0_.self_ref.other_ref.prior_ref), channel_id=1, source_target_pairs={{0,2},{4,6},{8,10},{12,14},{16,18},{20,22},{24,26},{28,30},{32,34}... | collective-permute-start | bytes 786440 | tf_op jit(solution)/shard_map/ppermute | solution.py:213
  49.6 10.2 %collective-permute-start.14 = (f32[4,128,128]{2,1,0:T(8,128)S(1)}, f32[4,128,128]{2,1,0:T(8,128)S(1)}, u32[]{:S(2)}, u32[]{:S(2)}) collective-permute-start(f32[4,128,128]{2,1,0:T(8,128)S(1)} %get-tuple-element.45.other_ref.self_ref.prior_ref), channel_id=1, source_target_pairs={{2,4},{6,8},{10,12},{14,16},{18,20},{22,24},{26,28},{30,32},{34,36... | collective-permute-start | bytes 786440 | tf_op jit(solution)/shard_map/ppermute | solution.py:214
  50.3 1.5 collective-permute-start.13
  56.3 10.1 %collective-permute-start.15 = (f32[4,128,128]{2,1,0:T(8,128)S(1)}, f32[4,128,128]{2,1,0:T(8,128)S(1)}, u32[]{:S(2)}, u32[]{:S(2)}) collective-permute-start(f32[4,128,128]{2,1,0:T(8,128)S(1)} %near4.1.rest_0_.self_ref.other_ref.prior_ref), channel_id=1, source_target_pairs={{0,2},{4,6},{8,10},{12,14},{16,18},{20,22},{24,26},{28,30},{32,34}... | collective-permute-start | bytes 786440 | tf_op jit(solution)/shard_map/ppermute | solution.py:213
  60.9 10.1 %collective-permute-start.17 = (f32[4,128,128]{2,1,0:T(8,128)S(1)}, f32[4,128,128]{2,1,0:T(8,128)S(1)}, u32[]{:S(2)}, u32[]{:S(2)}) collective-permute-start(f32[4,128,128]{2,1,0:T(8,128)S(1)} %get-tuple-element.47.other_ref.self_ref.prior_ref), channel_id=1, source_target_pairs={{2,4},{6,8},{10,12},{14,16},{18,20},{22,24},{26,28},{30,32},{34,36... | collective-permute-start | bytes 786440 | tf_op jit(solution)/shard_map/ppermute | solution.py:214
  61.6 1.3 collective-permute-start.16
  67.7 10.0 %collective-permute-start.18 = (f32[4,128,128]{2,1,0:T(8,128)S(1)}, f32[4,128,128]{2,1,0:T(8,128)S(1)}, u32[]{:S(2)}, u32[]{:S(2)}) collective-permute-start(f32[4,128,128]{2,1,0:T(8,128)S(1)} %near5.1.rest_0_.self_ref.other_ref.prior_ref), channel_id=1, source_target_pairs={{0,2},{4,6},{8,10},{12,14},{16,18},{20,22},{24,26},{28,30},{32,34}... | collective-permute-start | bytes 786440 | tf_op jit(solution)/shard_map/ppermute | solution.py:213
  72.1 10.0 %collective-permute-start.20 = (f32[4,128,128]{2,1,0:T(8,128)S(1)}, f32[4,128,128]{2,1,0:T(8,128)S(1)}, u32[]{:S(2)}, u32[]{:S(2)}) collective-permute-start(f32[4,128,128]{2,1,0:T(8,128)S(1)} %get-tuple-element.49.other_ref.self_ref.prior_ref), channel_id=1, source_target_pairs={{2,4},{6,8},{10,12},{14,16},{18,20},{22,24},{26,28},{30,32},{34,36... | collective-permute-start | bytes 786440 | tf_op jit(solution)/shard_map/ppermute | solution.py:214
  72.8 1.3 collective-permute-start.19
  78.9 9.9 %collective-permute-start.21 = (f32[4,128,128]{2,1,0:T(8,128)S(1)}, f32[4,128,128]{2,1,0:T(8,128)S(1)}, u32[]{:S(2)}, u32[]{:S(2)}) collective-permute-start(f32[4,128,128]{2,1,0:T(8,128)S(1)} %near6.1.rest_0_.self_ref.other_ref), channel_id=1, source_target_pairs={{0,2},{4,6},{8,10},{12,14},{16,18},{20,22},{24,26},{28,30},{32,34}... | collective-permute-start | bytes 786440 | tf_op jit(solution)/shard_map/ppermute | solution.py:213
  83.4 6.7 %collective-permute-start.23 = (f32[4,128,128]{2,1,0:T(8,128)S(1)}, f32[4,128,128]{2,1,0:T(8,128)S(1)}, u32[]{:S(2)}, u32[]{:S(2)}) collective-permute-start(f32[4,128,128]{2,1,0:T(8,128)S(1)} %get-tuple-element.51.other_ref.self_ref), channel_id=1, source_target_pairs={{2,4},{6,8},{10,12},{14,16},{18,20},{22,24},{26,28},{30,32},{34,36... | collective-permute-start | bytes 786440 | tf_op jit(solution)/shard_map/ppermute | solution.py:214
  84.1 1.3 collective-permute-start.22
  90.1 1.8 copy-start.2
  90.1 1.8 copy-start.5

commit v3 on v1

v3 whole, which is shorter than its diff:
```python
import functools

import jax
import jax.numpy as jnp
from jax import lax
from jax.experimental import pallas as pl
from jax.experimental.pallas import tpu as pltpu
from jax.sharding import PartitionSpec as P

STEPS = 8

CENTER = -205.0 / 72.0
COEFS = (1.6, -0.2, 8.0 / 315.0, -1.0 / 560.0)
REACH = len(COEFS)
CHUNK = 32

VM = pl.BlockSpec(memory_space=pltpu.VMEM)
F32 = jnp.float32
BF16 = jnp.bfloat16
PARAMS = pltpu.CompilerParams(vmem_limit_bytes=8 * 2**20)


def choose(flag, shape, yes, no):
    return jnp.where(jnp.broadcast_to(flag, shape) > 0.5, yes, no)


def split_planes(src_ref, odd, put):
    depth = src_ref.shape[0] // (2 * REACH)
    for i in range(REACH):
        right = src_ref[pl.ds(REACH + i, depth, stride=2 * REACH), :].T
        left = src_ref[pl.ds(REACH - 1 - i, depth, stride=2 * REACH), :].T
        put(i, choose(odd, right.shape, left, right), choose(odd, right.shape, right, left))


def rim(plane_ref, i, first):
    length, depth = plane_ref.shape[1:]
    return choose(first, (REACH, depth), plane_ref[i, length - REACH : length, :], plane_ref[i, 0:REACH, :])


def open_kernel(sides_ref, p_ref, near_ref, far_ref, rim_ref):
    odd = sides_ref[0:1, :]
    first = sides_ref[1:2, :]

    def put(i, near, far):
        near_ref[i] = near
        far_ref[i] = far

    split_planes(p_ref, odd, put)
    for i in range(REACH):
        rim_ref[i] = rim(near_ref, i, first)
        rim_ref[REACH + i] = rim(far_ref, i, first)


def tables_kernel(
    sides_ref, wavelet_ref, prior_ref, coef_ref, delay_ref, depth_ref,
    prior_near, prior_far, coef_near, coef_far, mark_near, mark_far, amp_ref,
):
    odd = sides_ref[0:1, :]
    length, depth = prior_near.shape[1:]

    def put_prior(i, near, far):
        prior_near[i] = near
        prior_far[i] = far

    def put_coef(i, near, far):
        coef_near[i] = near
        coef_far[i] = far

    split_planes(prior_ref, odd, put_prior)
    split_planes(coef_ref, odd, put_coef)

    def arrange(rows):
        right = [rows[REACH + i : REACH + i + 1, :] for i in range(REACH)]
        left = [rows[REACH - 1 - i : REACH - i, :] for i in range(REACH)]
        return choose(odd, rows.shape, jnp.concatenate(left + right, axis=0), jnp.concatenate(right + left, axis=0))

    delay = delay_ref[...]
    rows = []
    for step in range(STEPS):
        amplitude = jnp.zeros(delay.shape, F32)
        for w in range(wavelet_ref.shape[0]):
            wave = jnp.broadcast_to(wavelet_ref[w : w + 1, :], delay.shape)
            amplitude = jnp.where(delay + step == w, wave, amplitude)
        rows.append(arrange(amplitude))
    rows.append(arrange(depth_ref[...].astype(F32)))
    fill = jnp.zeros((length - len(rows) * 2 * REACH, length), F32)
    columns = jnp.concatenate(rows + [fill], axis=0).T
    amp_ref[...] = columns
    levels = lax.broadcasted_iota(jnp.int32, (length, depth), 1).astype(F32)
    base = STEPS * 2 * REACH
    for i in range(REACH):
        mark_near[i] = jnp.where(levels == columns[:, base + i : base + i + 1], 1.0, 0.0)
        mark_far[i] = jnp.where(levels == columns[:, base + REACH + i : base + REACH + i + 1], 1.0, 0.0)


def advance_kernel(
    step, half, sides_ref, self_ref, other_ref, halo_ref, rim_in_ref, prior_ref, coef_ref, mark_ref, amp_ref, *rest
):
    pad_ref, deep_ref = rest[-2:]
    first = sides_ref[1:2, :]
    planes, length, depth = self_ref.shape
    if half:
        near_new_ref, out_ref, rim_ref = rest[:3]
    else:
        out_ref = rest[0]
    for i in range(planes):
        edge = rim_in_ref[half * REACH + i]
        none = jnp.zeros_like(edge)
        pad_ref[i, 8 : 8 + length, :] = self_ref[i]
        pad_ref[i, 8 - REACH : 8, :] = choose(first, edge.shape, none, edge)
        pad_ref[i, 8 + length : 8 + length + REACH, :] = choose(first, edge.shape, edge, none)
    apart = jnp.abs(
        lax.broadcasted_iota(jnp.int32, (depth, depth), 0) - lax.broadcasted_iota(jnp.int32, (depth, depth), 1)
    )
    band = jnp.where(apart == 0, F32(3.0 * CENTER), F32(0.0))
    for k in range(1, REACH + 1):
        band = jnp.where(apart == k, F32(COEFS[k - 1]), band)
    band_high = band.astype(BF16)
    band_low = (band - band_high.astype(F32)).astype(BF16)
    flat = self_ref[...].reshape(planes * length, depth)
    high = flat.astype(BF16)
    low = (flat - high.astype(F32)).astype(BF16)
    dot = functools.partial(jnp.dot, preferred_element_type=F32)
    deep_ref[...] = dot(high, band_high) + (dot(low, band_high) + dot(high, band_low))
    for row in range(0, length, CHUNK):
        at = slice(row, row + CHUNK)
        line = [other_ref[REACH - 1 - i, at, :] for i in range(REACH)]
        line += [self_ref[i, at, :] for i in range(REACH)]
        line += [halo_ref[REACH - 1 - i, at, :] for i in range(REACH)]
        for i in range(planes):
            total = deep_ref[i * length + row : i * length + row + CHUNK, :]
            for k in range(1, REACH + 1):
                around = line[REACH + i - k] + line[REACH + i + k]
                around = around + pad_ref[i, 8 + row - k : 8 + row - k + CHUNK, :]
                around = around + pad_ref[i, 8 + row + k : 8 + row + k + CHUNK, :]
                total = total + COEFS[k - 1] * around
            column = (step * 2 + half) * REACH + i
            out_ref[i, at, :] = (
                2.0 * line[REACH + i]
                - prior_ref[i, at, :]
                + coef_ref[i, at, :] * total
                + mark_ref[i, at, :] * amp_ref[at, column : column + 1]
            )
    if half:
        for i in range(planes):
            rim_ref[i] = rim(near_new_ref, i, first)
            rim_ref[REACH + i] = rim(out_ref, i, first)


def close_kernel(sides_ref, near_ref, far_ref, receiver_ref, receiver_depth_ref, p_ref, image_ref, product_ref):
    odd = sides_ref[0:1, :]
    width = 2 * REACH
    depth = p_ref.shape[0] // width
    for i in range(REACH):
        near, far = near_ref[i], far_ref[i]
        p_ref[pl.ds(REACH + i, depth, stride=width), :] = choose(odd, near.shape, far, near).T
        p_ref[pl.ds(REACH - 1 - i, depth, stride=width), :] = choose(odd, near.shape, near, far).T
    start = receiver_depth_ref[...]
    for z in range(depth):
        at = slice(z * width, (z + 1) * width)
        field = receiver_ref[at, :]
        product_ref[at, :] = p_ref[at, :] * jnp.where(start <= z, field, jnp.zeros_like(field))
    for z in range(depth):
        at = slice(z * width, (z + 1) * width)
        value = 2.0 * product_ref[at, :]
        if z > 0:
            value = value - product_ref[(z - 1) * width : z * width, :]
        if z < depth - 1:
            value = value - product_ref[(z + 1) * width : (z + 2) * width, :]
        image_ref[at, :] = value


def pairs(size, first):
    left = [(i, i + 1) for i in range(first, size - 1, 2)]
    return left + [(b, a) for a, b in left]


def shards(
    pressure,
    pressure_prior,
    courant_square,
    wavelet,
    delay_steps,
    source_depth,
    receiver_depth,
    receiver_field,
):
    depth, width, length = pressure.shape
    size, cores = lax.axis_size("gx"), lax.axis_size("gy")
    near_pairs, far_pairs = pairs(size, 0), pairs(size, 1)
    rim_pairs = pairs(cores, 0)
    odd = lax.axis_index("gx") % 2
    first = jnp.where(lax.axis_index("gy") == 0, 1, 0)
    rows = lax.broadcasted_iota(jnp.int32, (8, length), 0)
    sides = jnp.where(rows == 0, odd, first).astype(F32)
    flat = (depth * width, length)
    half = jax.ShapeDtypeStruct((REACH, length, depth), F32)
    rims = jax.ShapeDtypeStruct((2 * REACH, REACH, depth), F32)
    square = jax.ShapeDtypeStruct((length, length), F32)
    wave = jnp.broadcast_to(wavelet[:, None], (wavelet.shape[0], length))

    def kernel(body, outs, inputs, scratch=(), name=None):
        return pl.pallas_call(
            body,
            out_shape=outs,
            in_specs=[VM] * len(inputs),
            out_specs=jax.tree.map(lambda _: VM, outs),
            scratch_shapes=list(scratch),
            compiler_params=PARAMS,
            name=name,
        )(*inputs)

    near, far, edge = kernel(open_kernel, (half, half, rims), (sides, pressure.reshape(flat)), name="open")
    near_prior, far_prior, near_coef, far_coef, near_mark, far_mark, amp = kernel(
        tables_kernel,
        (half,) * 6 + (square,),
        (
            sides,
            wave,
            pressure_prior.reshape(flat),
            courant_square.astype(F32).reshape(flat),
            delay_steps,
            source_depth,
        ),
        name="tables",
    )
    scratch = (pltpu.VMEM((REACH, length + 16, depth), F32), pltpu.VMEM((REACH * length, depth), F32))
    for step in range(STEPS):
        near_halo = lax.ppermute(near, "gx", near_pairs)
        far_halo = lax.ppermute(far, "gx", far_pairs)
        edge_in = lax.ppermute(edge, "gy", rim_pairs)
        near_next = kernel(
            functools.partial(advance_kernel, step, 0),
            half,
            (sides, near, far, near_halo, edge_in, near_prior, near_coef, near_mark, amp),
            scratch,
            f"near{step}",
        )
        far_next, edge = kernel(
            functools.partial(advance_kernel, step, 1),
            (half, rims),
            (sides, far, near, far_halo, edge_in, far_prior, far_coef, far_mark, amp, near_next),
            scratch,
            f"far{step}",
        )
        near_prior, far_prior = near, far
        near, far = near_next, far_next
    whole = jax.ShapeDtypeStruct(flat, F32)
    final, filtered = kernel(
        close_kernel,
        (whole, whole),
        (sides, near, far, receiver_field.reshape(flat), receiver_depth),
        (pltpu.VMEM(flat, F32),),
        "close",
    )
    image = lax.all_to_all(filtered.reshape(depth, width, length), "gx", split_axis=0, concat_axis=1, tiled=True)
    return final.reshape(depth, width, length), image


def solution(mesh):
    in_specs = (
        P(None, ("shots", "gx"), "gy"),
        P(None, ("shots", "gx"), "gy"),
        P(None, "gx", "gy"),
        P("shots"),
        P(("shots", "gx"), "gy"),
        P(("shots", "gx"), "gy"),
        P(("shots", "gx"), "gy"),
        P(None, ("shots", "gx"), "gy"),
    )
    out_specs = (P(None, ("shots", "gx"), "gy"), P("gx", "shots", "gy"))
    return jax.shard_map(shards, mesh=mesh, in_specs=in_specs, out_specs=out_specs, check_vma=False)
```

time: 218 us -> 182 us (0.83)
  Pallas kernels: 50.5 us -> 12 us
  waiting for transfers between devices: 19.9 us -> 40 us
  starting transfers between devices: 45.3 us -> 30.1 us
  local copies, waits for them, and re-layouts: 12.1 us -> 3.11 us
  blocking collectives: 87.2 us -> 95 us
    pallas_call x19, Pallas kernels: 50.5 us -> 12 us  [kernel(): pl.pallas_call(body, out_shape=outs, in_specs=[VM] * len(inputs), out_spe...]
    ppermute x24, waiting for transfers between devices: 19.9 us -> 40 us  [the longest x8 31.9 us: shards(): near_halo = lax.ppermute(near, 'gx', near_pairs)]
    ppermute x24, starting transfers between devices: 45.3 us -> 30.1 us  [the longest x8 23.5 us: shards(): near_halo = lax.ppermute(near, 'gx', near_pairs)]
    unnamed x50 -> x16, local copies, waits for them, and re-layouts: 11.3 us -> 2.14 us
    all_to_all x1, blocking collectives: 87.2 us -> 95 us  [shards(): lax.all_to_all(filtered.reshape(depth, width, length), 'gx', split_axis=0...]
  transfers between devices with their start and end apart: 24 -> 24, of which waited for: 15 -> 15; matrix products, arithmetic and copies ran while one was open for 0% -> 0% of each run, Pallas kernels for 20% -> 5%
where the time goes in v3:
time: 182 us; the launch traced here: 181 us
  blocking collectives  95 us (52%)
  waiting for transfers between devices  40 us (22%)
  starting transfers between devices  30.1 us (17%)
  Pallas kernels  12 us (7%)
  local copies, waits for them, and re-layouts  3.11 us (2%)
    all_to_all x1, blocking collectives, shards(): lax.all_to_all(filtered.reshape(depth, width, length), 'gx', split_axis=0...  95 us
    ppermute x8, waiting for transfers between devices, shards(): near_halo = lax.ppermute(near, 'gx', near_pairs)  31.9 us
    ppermute x8, starting transfers between devices, shards(): near_halo = lax.ppermute(near, 'gx', near_pairs)  23.5 us
    pallas_call x19, Pallas kernels, kernel(): pl.pallas_call(body, out_shape=outs, in_specs=[VM] * len(inputs), out_spe...  12 us
    ppermute x8, waiting for transfers between devices, shards(): edge_in = lax.ppermute(edge, 'gy', rim_pairs)  8.1 us
    ppermute x8, starting transfers between devices, shards(): far_halo = lax.ppermute(far, 'gx', far_pairs)  5.41 us
  transfers between devices with their start and end apart: 24, of which 15 were waited for; matrix products, arithmetic and copies ran while one was open for 0% of the time, Pallas kernels for 5%

profile of v3, /device:TPU:46, one launch (start us, length us, event | category | flops | bytes accessed | tf_op | source)
XLA Modules:
  0.0 181.2 jit_solution(8432861888918685879)
XLA Ops:
  0.7 1.0 copy-done
  2.0 2.2 %collective-permute-start = (f32[4,128,128]{2,1,0:T(8,128)S(1)}, f32[4,128,128]{2,1,0:T(8,128)S(1)}, u32[]{:S(2)}, u32[]{:S(2)}) collective-permute-start(f32[4,128,128]{2,1,0:T(8,128)S(1)} %get-tuple-element.29.self_ref.other_ref.prior_ref), channel_id=1, source_target_pairs={{0,2},{4,6},{8,10},{12,14},{16,18},{20,22},{24,26},{28,30},{32,34}... | collective-permute-start | bytes 786440 | tf_op jit(solution)/shard_map/ppermute | solution.py:229
  4.2 0.7 collective-permute-start.2
  5.6 0.6 copy-done.3
  6.3 0.6 tables.1
  6.9 3.7 %collective-permute-done.halo_ref = f32[4,128,128]{2,1,0:T(8,128)S(1)} collective-permute-done((f32[4,128,128]{2,1,0:T(8,128)S(1)}, f32[4,128,128]{2,1,0:T(8,128)S(1)}, u32[]{:S(2)}, u32[]{:S(2)}) %collective-permute-start) | collective-permute-done | bytes 262176 | tf_op jit(solution)/shard_map/ppermute | solution.py:229
  10.6 0.6 near0.1.rest_0_.self_ref.other_ref.prior_ref
  11.2 1.9 %collective-permute-start.3 = (f32[4,128,128]{2,1,0:T(8,128)S(1)}, f32[4,128,128]{2,1,0:T(8,128)S(1)}, u32[]{:S(2)}, u32[]{:S(2)}) collective-permute-start(f32[4,128,128]{2,1,0:T(8,128)S(1)} %near0.1.rest_0_.self_ref.other_ref.prior_ref), channel_id=1, source_target_pairs={{0,2},{4,6},{8,10},{12,14},{16,18},{20,22},{24,26},{28,30},{32,34}... | collective-permute-start | bytes 786440 | tf_op jit(solution)/shard_map/ppermute | solution.py:229
  13.1 0.6 far0.1
  13.8 0.7 collective-permute-start.5
  14.6 1.2 collective-permute-done.4.rim_in_ref
  15.8 3.9 %collective-permute-done.3.halo_ref = f32[4,128,128]{2,1,0:T(8,128)S(1)} collective-permute-done((f32[4,128,128]{2,1,0:T(8,128)S(1)}, f32[4,128,128]{2,1,0:T(8,128)S(1)}, u32[]{:S(2)}, u32[]{:S(2)}) %collective-permute-start.3) | collective-permute-done | bytes 262176 | tf_op jit(solution)/shard_map/ppermute | solution.py:229
  20.3 2.9 %collective-permute-start.6 = (f32[4,128,128]{2,1,0:T(8,128)S(1)}, f32[4,128,128]{2,1,0:T(8,128)S(1)}, u32[]{:S(2)}, u32[]{:S(2)}) collective-permute-start(f32[4,128,128]{2,1,0:T(8,128)S(1)} %near1.1.rest_0_.self_ref.other_ref.prior_ref), channel_id=1, source_target_pairs={{0,2},{4,6},{8,10},{12,14},{16,18},{20,22},{24,26},{28,30},{32,34}... | collective-permute-start | bytes 786440 | tf_op jit(solution)/shard_map/ppermute | solution.py:229
  23.2 0.6 far1.1
  23.8 0.7 collective-permute-start.8
  24.6 1.2 collective-permute-done.7.rim_in_ref
  25.8 4.0 %collective-permute-done.6.halo_ref = f32[4,128,128]{2,1,0:T(8,128)S(1)} collective-permute-done((f32[4,128,128]{2,1,0:T(8,128)S(1)}, f32[4,128,128]{2,1,0:T(8,128)S(1)}, u32[]{:S(2)}, u32[]{:S(2)}) %collective-permute-start.6) | collective-permute-done | bytes 262176 | tf_op jit(solution)/shard_map/ppermute | solution.py:229
  30.4 3.6 %collective-permute-start.9 = (f32[4,128,128]{2,1,0:T(8,128)S(1)}, f32[4,128,128]{2,1,0:T(8,128)S(1)}, u32[]{:S(2)}, u32[]{:S(2)}) collective-permute-start(f32[4,128,128]{2,1,0:T(8,128)S(1)} %near2.1.rest_0_.self_ref.other_ref.prior_ref), channel_id=1, source_target_pairs={{0,2},{4,6},{8,10},{12,14},{16,18},{20,22},{24,26},{28,30},{32,34}... | collective-permute-start | bytes 786440 | tf_op jit(solution)/shard_map/ppermute | solution.py:229
  34.1 0.6 far2.1
  34.7 0.7 collective-permute-start.11
  35.5 1.2 collective-permute-done.10.rim_in_ref
  36.7 4.0 %collective-permute-done.9.halo_ref = f32[4,128,128]{2,1,0:T(8,128)S(1)} collective-permute-done((f32[4,128,128]{2,1,0:T(8,128)S(1)}, f32[4,128,128]{2,1,0:T(8,128)S(1)}, u32[]{:S(2)}, u32[]{:S(2)}) %collective-permute-start.9) | collective-permute-done | bytes 262176 | tf_op jit(solution)/shard_map/ppermute | solution.py:229
  41.3 3.5 %collective-permute-start.12 = (f32[4,128,128]{2,1,0:T(8,128)S(1)}, f32[4,128,128]{2,1,0:T(8,128)S(1)}, u32[]{:S(2)}, u32[]{:S(2)}) collective-permute-start(f32[4,128,128]{2,1,0:T(8,128)S(1)} %near3.1.rest_0_.self_ref.other_ref.prior_ref), channel_id=1, source_target_pairs={{0,2},{4,6},{8,10},{12,14},{16,18},{20,22},{24,26},{28,30},{32,34}... | collective-permute-start | bytes 786440 | tf_op jit(solution)/shard_map/ppermute | solution.py:229
  44.8 0.6 far3.1
  45.4 0.7 collective-permute-start.14
  46.2 1.2 collective-permute-done.13.rim_in_ref
  47.4 4.0 %collective-permute-done.12.halo_ref = f32[4,128,128]{2,1,0:T(8,128)S(1)} collective-permute-done((f32[4,128,128]{2,1,0:T(8,128)S(1)}, f32[4,128,128]{2,1,0:T(8,128)S(1)}, u32[]{:S(2)}, u32[]{:S(2)}) %collective-permute-start.12) | collective-permute-done | bytes 262176 | tf_op jit(solution)/shard_map/ppermute | solution.py:229
  52.0 3.6 %collective-permute-start.15 = (f32[4,128,128]{2,1,0:T(8,128)S(1)}, f32[4,128,128]{2,1,0:T(8,128)S(1)}, u32[]{:S(2)}, u32[]{:S(2)}) collective-permute-start(f32[4,128,128]{2,1,0:T(8,128)S(1)} %near4.1.rest_0_.self_ref.other_ref.prior_ref), channel_id=1, source_target_pairs={{0,2},{4,6},{8,10},{12,14},{16,18},{20,22},{24,26},{28,30},{32,34}... | collective-permute-start | bytes 786440 | tf_op jit(solution)/shard_map/ppermute | solution.py:229
  55.6 0.6 far4.1
  56.2 0.7 collective-permute-start.17
  57.0 1.2 collective-permute-done.16.rim_in_ref
  58.2 4.0 %collective-permute-done.15.halo_ref = f32[4,128,128]{2,1,0:T(8,128)S(1)} collective-permute-done((f32[4,128,128]{2,1,0:T(8,128)S(1)}, f32[4,128,128]{2,1,0:T(8,128)S(1)}, u32[]{:S(2)}, u32[]{:S(2)}) %collective-permute-start.15) | collective-permute-done | bytes 262176 | tf_op jit(solution)/shard_map/ppermute | solution.py:229
  62.8 2.7 %collective-permute-start.18 = (f32[4,128,128]{2,1,0:T(8,128)S(1)}, f32[4,128,128]{2,1,0:T(8,128)S(1)}, u32[]{:S(2)}, u32[]{:S(2)}) collective-permute-start(f32[4,128,128]{2,1,0:T(8,128)S(1)} %near5.1.rest_0_.self_ref.other_ref.prior_ref), channel_id=1, source_target_pairs={{0,2},{4,6},{8,10},{12,14},{16,18},{20,22},{24,26},{28,30},{32,34}... | collective-permute-start | bytes 786440 | tf_op jit(solution)/shard_map/ppermute | solution.py:229
  65.5 0.6 far5.1
  66.1 0.7 collective-permute-start.20
  67.0 1.2 collective-permute-done.19.rim_in_ref
  68.1 4.0 %collective-permute-done.18.halo_ref = f32[4,128,128]{2,1,0:T(8,128)S(1)} collective-permute-done((f32[4,128,128]{2,1,0:T(8,128)S(1)}, f32[4,128,128]{2,1,0:T(8,128)S(1)}, u32[]{:S(2)}, u32[]{:S(2)}) %collective-permute-start.18) | collective-permute-done | bytes 262176 | tf_op jit(solution)/shard_map/ppermute | solution.py:229
  72.2 0.6 near6.1.rest_0_.self_ref.other_ref
  72.8 3.0 %collective-permute-start.21 = (f32[4,128,128]{2,1,0:T(8,128)S(1)}, f32[4,128,128]{2,1,0:T(8,128)S(1)}, u32[]{:S(2)}, u32[]{:S(2)}) collective-permute-start(f32[4,128,128]{2,1,0:T(8,128)S(1)} %near6.1.rest_0_.self_ref.other_ref), channel_id=1, source_target_pairs={{0,2},{4,6},{8,10},{12,14},{16,18},{20,22},{24,26},{28,30},{32,34}... | collective-permute-start | bytes 786440 | tf_op jit(solution)/shard_map/ppermute | solution.py:229
  75.8 0.6 far6.1
  76.4 0.7 collective-permute-start.23
  77.3 1.2 collective-permute-done.22.rim_in_ref
  78.4 4.0 %collective-permute-done.21.halo_ref = f32[4,128,128]{2,1,0:T(8,128)S(1)} collective-permute-done((f32[4,128,128]{2,1,0:T(8,128)S(1)}, f32[4,128,128]{2,1,0:T(8,128)S(1)}, u32[]{:S(2)}, u32[]{:S(2)}) %collective-permute-start.21) | collective-permute-done | bytes 262176 | tf_op jit(solution)/shard_map/ppermute | solution.py:229
  82.5 0.6 near7.1.rest_0_.near_ref
  83.1 1.2 far7.1
  84.3 1.0 close.1
  85.3 95.0 %all_to_all.18 = f32[128,8,128]{2,1,0:T(8,128)S(1)} all-to-all(f32[128,8,128]{2,1,0:T(8,128)S(1)} %bitcast.17), channel_id=1, replica_groups=mesh['shots'=4,'gx'=32,'gy'=2] {'gx'}, dimensions={0} | all-to-all | bytes 1048576 | tf_op jit(solution)/shard_map/all_to_all | solution.py:256
  180.4 0.8 copy.12
  (41 shorter events, 5.0 us)
Async XLA Ops:
  0.7 1.0 copy-start
  1.8 3.3 %copy-start.6 = (bf16[128,8,128]{2,1,0:T(8,128)(2,1)S(1)}, bf16[128,8,128]{2,1,0:T(8,128)(2,1)}, u32[]{:S(2)}) copy-start(bf16[128,8,128]{2,1,0:T(8,128)(2,1)} %param.10) | copy-start | bytes 786436
  2.0 3.7 %copy-start.1 = (f32[128,8,128]{2,1,0:T(8,128)S(1)}, f32[128,8,128]{2,1,0:T(8,128)}, u32[]{:S(2)}) copy-start(f32[128,8,128]{2,1,0:T(8,128)} %param.9) | copy-start | bytes 1572868
  2.0 8.6 %collective-permute-start = (f32[4,128,128]{2,1,0:T(8,128)S(1)}, f32[4,128,128]{2,1,0:T(8,128)S(1)}, u32[]{:S(2)}, u32[]{:S(2)}) collective-permute-start(f32[4,128,128]{2,1,0:T(8,128)S(1)} %get-tuple-element.29.self_ref.other_ref.prior_ref), channel_id=1, source_target_pairs={{0,2},{4,6},{8,10},{12,14},{16,18},{20,22},{24,26},{28,30},{32,34}... | collective-permute-start | bytes 786440 | tf_op jit(solution)/shard_map/ppermute | solution.py:229
  4.2 8.9 %collective-permute-start.2 = (f32[4,128,128]{2,1,0:T(8,128)S(1)}, f32[4,128,128]{2,1,0:T(8,128)S(1)}, u32[]{:S(2)}, u32[]{:S(2)}) collective-permute-start(f32[4,128,128]{2,1,0:T(8,128)S(1)} %get-tuple-element.30.other_ref.self_ref.prior_ref), channel_id=1, source_target_pairs={{2,4},{6,8},{10,12},{14,16},{18,20},{22,24},{26,28},{30,32},{34,36... | collective-permute-start | bytes 786440 | tf_op jit(solution)/shard_map/ppermute | solution.py:230
  4.9 0.7 copy-start.7
  4.9 2.0 %collective-permute-start.1 = (f32[8,4,128]{2,1,0:T(4,128)S(1)}, f32[8,4,128]{2,1,0:T(4,128)S(1)}, u32[]{:S(2)}, u32[]{:S(2)}) collective-permute-start(f32[8,4,128]{2,1,0:T(4,128)S(1)} %get-tuple-element.31), channel_id=1, source_target_pairs={{0,1},{1,0},{2,3},{3,2},{4,5},{5,4},{6,7},{7,6},{8,9},{9,8},{10,11... | collective-permute-start | bytes 49160 | tf_op jit(solution)/shard_map/ppermute | solution.py:231
  5.6 0.7 copy-start.3
  5.6 0.7 copy-start.4
  11.2 8.4 %collective-permute-start.3 = (f32[4,128,128]{2,1,0:T(8,128)S(1)}, f32[4,128,128]{2,1,0:T(8,128)S(1)}, u32[]{:S(2)}, u32[]{:S(2)}) collective-permute-start(f32[4,128,128]{2,1,0:T(8,128)S(1)} %near0.1.rest_0_.self_ref.other_ref.prior_ref), channel_id=1, source_target_pairs={{0,2},{4,6},{8,10},{12,14},{16,18},{20,22},{24,26},{28,30},{32,34}... | collective-permute-start | bytes 786440 | tf_op jit(solution)/shard_map/ppermute | solution.py:229
  13.8 9.4 %collective-permute-start.5 = (f32[4,128,128]{2,1,0:T(8,128)S(1)}, f32[4,128,128]{2,1,0:T(8,128)S(1)}, u32[]{:S(2)}, u32[]{:S(2)}) collective-permute-start(f32[4,128,128]{2,1,0:T(8,128)S(1)} %get-tuple-element.39.other_ref.self_ref.prior_ref), channel_id=1, source_target_pairs={{2,4},{6,8},{10,12},{14,16},{18,20},{22,24},{26,28},{30,32},{34,36... | collective-permute-start | bytes 786440 | tf_op jit(solution)/shard_map/ppermute | solution.py:230
  14.4 1.3 collective-permute-start.4
  20.3 9.6 %collective-permute-start.6 = (f32[4,128,128]{2,1,0:T(8,128)S(1)}, f32[4,128,128]{2,1,0:T(8,128)S(1)}, u32[]{:S(2)}, u32[]{:S(2)}) collective-permute-start(f32[4,128,128]{2,1,0:T(8,128)S(1)} %near1.1.rest_0_.self_ref.other_ref.prior_ref), channel_id=1, source_target_pairs={{0,2},{4,6},{8,10},{12,14},{16,18},{20,22},{24,26},{28,30},{32,34}... | collective-permute-start | bytes 786440 | tf_op jit(solution)/shard_map/ppermute | solution.py:229
  23.8 10.3 %collective-permute-start.8 = (f32[4,128,128]{2,1,0:T(8,128)S(1)}, f32[4,128,128]{2,1,0:T(8,128)S(1)}, u32[]{:S(2)}, u32[]{:S(2)}) collective-permute-start(f32[4,128,128]{2,1,0:T(8,128)S(1)} %get-tuple-element.41.other_ref.self_ref.prior_ref), channel_id=1, source_target_pairs={{2,4},{6,8},{10,12},{14,16},{18,20},{22,24},{26,28},{30,32},{34,36... | collective-permute-start | bytes 786440 | tf_op jit(solution)/shard_map/ppermute | solution.py:230
  24.5 1.3 collective-permute-start.7
  30.4 10.3 %collective-permute-start.9 = (f32[4,128,128]{2,1,0:T(8,128)S(1)}, f32[4,128,128]{2,1,0:T(8,128)S(1)}, u32[]{:S(2)}, u32[]{:S(2)}) collective-permute-start(f32[4,128,128]{2,1,0:T(8,128)S(1)} %near2.1.rest_0_.self_ref.other_ref.prior_ref), channel_id=1, source_target_pairs={{0,2},{4,6},{8,10},{12,14},{16,18},{20,22},{24,26},{28,30},{32,34}... | collective-permute-start | bytes 786440 | tf_op jit(solution)/shard_map/ppermute | solution.py:229
  34.7 10.1 %collective-permute-start.11 = (f32[4,128,128]{2,1,0:T(8,128)S(1)}, f32[4,128,128]{2,1,0:T(8,128)S(1)}, u32[]{:S(2)}, u32[]{:S(2)}) collective-permute-start(f32[4,128,128]{2,1,0:T(8,128)S(1)} %get-tuple-element.43.other_ref.self_ref.prior_ref), channel_id=1, source_target_pairs={{2,4},{6,8},{10,12},{14,16},{18,20},{22,24},{26,28},{30,32},{34,36... | collective-permute-start | bytes 786440 | tf_op jit(solution)/shard_map/ppermute | solution.py:230
  35.4 1.3 collective-permute-start.10
  41.3 10.1 %collective-permute-start.12 = (f32[4,128,128]{2,1,0:T(8,128)S(1)}, f32[4,128,128]{2,1,0:T(8,128)S(1)}, u32[]{:S(2)}, u32[]{:S(2)}) collective-permute-start(f32[4,128,128]{2,1,0:T(8,128)S(1)} %near3.1.rest_0_.self_ref.other_ref.prior_ref), channel_id=1, source_target_pairs={{0,2},{4,6},{8,10},{12,14},{16,18},{20,22},{24,26},{28,30},{32,34}... | collective-permute-start | bytes 786440 | tf_op jit(solution)/shard_map/ppermute | solution.py:229
  45.4 10.2 %collective-permute-start.14 = (f32[4,128,128]{2,1,0:T(8,128)S(1)}, f32[4,128,128]{2,1,0:T(8,128)S(1)}, u32[]{:S(2)}, u32[]{:S(2)}) collective-permute-start(f32[4,128,128]{2,1,0:T(8,128)S(1)} %get-tuple-element.45.other_ref.self_ref.prior_ref), channel_id=1, source_target_pairs={{2,4},{6,8},{10,12},{14,16},{18,20},{22,24},{26,28},{30,32},{34,36... | collective-permute-start | bytes 786440 | tf_op jit(solution)/shard_map/ppermute | solution.py:230
  46.1 1.3 collective-permute-start.13
  52.0 10.2 %collective-permute-start.15 = (f32[4,128,128]{2,1,0:T(8,128)S(1)}, f32[4,128,128]{2,1,0:T(8,128)S(1)}, u32[]{:S(2)}, u32[]{:S(2)}) collective-permute-start(f32[4,128,128]{2,1,0:T(8,128)S(1)} %near4.1.rest_0_.self_ref.other_ref.prior_ref), channel_id=1, source_target_pairs={{0,2},{4,6},{8,10},{12,14},{16,18},{20,22},{24,26},{28,30},{32,34}... | collective-permute-start | bytes 786440 | tf_op jit(solution)/shard_map/ppermute | solution.py:229
  56.2 9.3 %collective-permute-start.17 = (f32[4,128,128]{2,1,0:T(8,128)S(1)}, f32[4,128,128]{2,1,0:T(8,128)S(1)}, u32[]{:S(2)}, u32[]{:S(2)}) collective-permute-start(f32[4,128,128]{2,1,0:T(8,128)S(1)} %get-tuple-element.47.other_ref.self_ref.prior_ref), channel_id=1, source_target_pairs={{2,4},{6,8},{10,12},{14,16},{18,20},{22,24},{26,28},{30,32},{34,36... | collective-permute-start | bytes 786440 | tf_op jit(solution)/shard_map/ppermute | solution.py:230
  56.9 1.3 collective-permute-start.16
  62.8 9.4 %collective-permute-start.18 = (f32[4,128,128]{2,1,0:T(8,128)S(1)}, f32[4,128,128]{2,1,0:T(8,128)S(1)}, u32[]{:S(2)}, u32[]{:S(2)}) collective-permute-start(f32[4,128,128]{2,1,0:T(8,128)S(1)} %near5.1.rest_0_.self_ref.other_ref.prior_ref), channel_id=1, source_target_pairs={{0,2},{4,6},{8,10},{12,14},{16,18},{20,22},{24,26},{28,30},{32,34}... | collective-permute-start | bytes 786440 | tf_op jit(solution)/shard_map/ppermute | solution.py:229
  66.1 9.7 %collective-permute-start.20 = (f32[4,128,128]{2,1,0:T(8,128)S(1)}, f32[4,128,128]{2,1,0:T(8,128)S(1)}, u32[]{:S(2)}, u32[]{:S(2)}) collective-permute-start(f32[4,128,128]{2,1,0:T(8,128)S(1)} %get-tuple-element.49.other_ref.self_ref.prior_ref), channel_id=1, source_target_pairs={{2,4},{6,8},{10,12},{14,16},{18,20},{22,24},{26,28},{30,32},{34,36... | collective-permute-start | bytes 786440 | tf_op jit(solution)/shard_map/ppermute | solution.py:230
  66.8 1.3 collective-permute-start.19
  72.8 9.7 %collective-permute-start.21 = (f32[4,128,128]{2,1,0:T(8,128)S(1)}, f32[4,128,128]{2,1,0:T(8,128)S(1)}, u32[]{:S(2)}, u32[]{:S(2)}) collective-permute-start(f32[4,128,128]{2,1,0:T(8,128)S(1)} %near6.1.rest_0_.self_ref.other_ref), channel_id=1, source_target_pairs={{0,2},{4,6},{8,10},{12,14},{16,18},{20,22},{24,26},{28,30},{32,34}... | collective-permute-start | bytes 786440 | tf_op jit(solution)/shard_map/ppermute | solution.py:229
  76.4 6.6 %collective-permute-start.23 = (f32[4,128,128]{2,1,0:T(8,128)S(1)}, f32[4,128,128]{2,1,0:T(8,128)S(1)}, u32[]{:S(2)}, u32[]{:S(2)}) collective-permute-start(f32[4,128,128]{2,1,0:T(8,128)S(1)} %get-tuple-element.51.other_ref.self_ref), channel_id=1, source_target_pairs={{2,4},{6,8},{10,12},{14,16},{18,20},{22,24},{26,28},{30,32},{34,36... | collective-permute-start | bytes 786440 | tf_op jit(solution)/shard_map/ppermute | solution.py:230
  77.1 1.3 collective-permute-start.22
  83.1 1.2 copy-start.2
  83.1 1.2 copy-start.5

commit v4 on v3

--- a/solution.py
+++ b/solution.py
@@ -27,9 +27,9 @@
 def split_planes(src_ref, odd, put):
     depth = src_ref.shape[0] // (2 * REACH)
     for i in range(REACH):
-        right = src_ref[pl.ds(REACH + i, depth, stride=2 * REACH), :].T
-        left = src_ref[pl.ds(REACH - 1 - i, depth, stride=2 * REACH), :].T
-        put(i, choose(odd, right.shape, left, right), choose(odd, right.shape, right, left))
+        right = src_ref[pl.ds(REACH + i, depth, stride=2 * REACH), :]
+        left = src_ref[pl.ds(REACH - 1 - i, depth, stride=2 * REACH), :]
+        put(i, choose(odd, right.shape, left, right).T, choose(odd, right.shape, right, left).T)
 
 
 def rim(plane_ref, i, first):
@@ -37,15 +37,20 @@
     return choose(first, (REACH, depth), plane_ref[i, length - REACH : length, :], plane_ref[i, 0:REACH, :])
 
 
-def open_kernel(sides_ref, p_ref, near_ref, far_ref, rim_ref):
-    odd = sides_ref[0:1, :]
-    first = sides_ref[1:2, :]
-
+def open_near_kernel(sides_ref, p_ref, near_ref):
     def put(i, near, far):
         near_ref[i] = near
+
+    split_planes(p_ref, sides_ref[0:1, :], put)
+
+
+def open_far_kernel(sides_ref, p_ref, near_ref, far_ref, rim_ref):
+    first = sides_ref[1:2, :]
+
+    def put(i, near, far):
         far_ref[i] = far
 
-    split_planes(p_ref, odd, put)
+    split_planes(p_ref, sides_ref[0:1, :], put)
     for i in range(REACH):
         rim_ref[i] = rim(near_ref, i, first)
         rim_ref[REACH + i] = rim(far_ref, i, first)
@@ -99,10 +104,10 @@
     pad_ref, deep_ref = rest[-2:]
     first = sides_ref[1:2, :]
     planes, length, depth = self_ref.shape
-    if half:
+    if len(rest) > 3:
         near_new_ref, out_ref, rim_ref = rest[:3]
     else:
-        out_ref = rest[0]
+        out_ref, rim_ref = rest[0], None
     for i in range(planes):
         edge = rim_in_ref[half * REACH + i]
         none = jnp.zeros_like(edge)
@@ -141,13 +146,56 @@
                 + coef_ref[i, at, :] * total
                 + mark_ref[i, at, :] * amp_ref[at, column : column + 1]
             )
-    if half:
+    if rim_ref is not None:
         for i in range(planes):
             rim_ref[i] = rim(near_new_ref, i, first)
             rim_ref[REACH + i] = rim(out_ref, i, first)
 
 
-def close_kernel(sides_ref, near_ref, far_ref, receiver_ref, receiver_depth_ref, p_ref, image_ref, product_ref):
+def image_half(is_near, sides_ref, half_ref, receiver_ref, receiver_depth_ref, image_ref, pad_ref, row, stride):
+    odd = sides_ref[0:1, :]
+    length, depth = half_ref.shape[1:]
+    width = 2 * REACH
+    levels = lax.broadcasted_iota(jnp.int32, (depth, length), 0).astype(F32)
+    start = receiver_depth_ref[...].astype(F32)
+    pad_ref[0:8, :] = jnp.zeros((8, length), F32)
+    pad_ref[8 + depth : 16 + depth, :] = jnp.zeros((8, length), F32)
+    for j in range(REACH):
+        rising, falling = half_ref[j], half_ref[REACH - 1 - j]
+        low = receiver_ref[pl.ds(j, depth, stride=width), :]
+        high = receiver_ref[pl.ds(REACH + j, depth, stride=width), :]
+        start_low, start_high = start[j : j + 1, :], start[REACH + j : REACH + j + 1, :]
+        if is_near:
+            field = choose(odd, rising.shape, falling, rising).T
+            receiver = choose(odd, low.shape, low, high)
+            begin = choose(odd, start_low.shape, start_low, start_high)
+        else:
+            field = choose(odd, rising.shape, rising, falling).T
+            receiver = choose(odd, low.shape, high, low)
+            begin = choose(odd, start_low.shape, start_high, start_low)
+        begin = jnp.broadcast_to(begin, levels.shape)
+        product = field * jnp.where(levels >= begin, receiver, jnp.zeros_like(receiver))
+        pad_ref[8 : 8 + depth, :] = product
+        image_ref[pl.ds(row + j, depth, stride=stride), :] = (
+            2.0 * product - pad_ref[7 : 7 + depth, :] - pad_ref[9 : 9 + depth, :]
+        )
+
+
+def image_near_kernel(sides_ref, near_ref, receiver_ref, receiver_depth_ref, image_ref, pad_ref):
+    image_half(True, sides_ref, near_ref, receiver_ref, receiver_depth_ref, image_ref, pad_ref, 0, REACH)
+
+
+def last_kernel(step, sides_ref, *rest):
+    receiver_ref, receiver_depth_ref, part_ref, far_ref, image_ref, side_ref, deep_ref, pad_ref = rest[-8:]
+    advance_kernel(step, 1, sides_ref, *rest[:-8], far_ref, side_ref, deep_ref)
+    width = 2 * REACH
+    depth = part_ref.shape[0] // REACH
+    image_half(False, sides_ref, far_ref, receiver_ref, receiver_depth_ref, image_ref, pad_ref, REACH, width)
+    for j in range(REACH):
+        image_ref[pl.ds(j, depth, stride=width), :] = part_ref[pl.ds(j, depth, stride=REACH), :]
+
+
+def final_kernel(sides_ref, near_ref, far_ref, p_ref):
     odd = sides_ref[0:1, :]
     width = 2 * REACH
     depth = p_ref.shape[0] // width
@@ -155,19 +203,17 @@
         near, far = near_ref[i], far_ref[i]
         p_ref[pl.ds(REACH + i, depth, stride=width), :] = choose(odd, near.shape, far, near).T
         p_ref[pl.ds(REACH - 1 - i, depth, stride=width), :] = choose(odd, near.shape, near, far).T
-    start = receiver_depth_ref[...]
-    for z in range(depth):
-        at = slice(z * width, (z + 1) * width)
-        field = receiver_ref[at, :]
-        product_ref[at, :] = p_ref[at, :] * jnp.where(start <= z, field, jnp.zeros_like(field))
-    for z in range(depth):
-        at = slice(z * width, (z + 1) * width)
-        value = 2.0 * product_ref[at, :]
-        if z > 0:
-            value = value - product_ref[(z - 1) * width : z * width, :]
-        if z < depth - 1:
-            value = value - product_ref[(z + 1) * width : (z + 2) * width, :]
-        image_ref[at, :] = value
+
+
+def join_kernel(levels, parts_ref, image_ref):
+    width = 2 * REACH
+    for source in range(parts_ref.shape[0] // (levels * width)):
+        for z in range(levels):
+            at = (source * levels + z) * width
+            block = parts_ref[at : at + width, :]
+            if source % 2 == 0:
+                block = jnp.concatenate([block[REACH:], block[:REACH]], axis=0)
+            image_ref[z, source * width : (source + 1) * width, :] = block
 
 
 def pairs(size, first):
@@ -196,6 +242,7 @@
     flat = (depth * width, length)
     half = jax.ShapeDtypeStruct((REACH, length, depth), F32)
     rims = jax.ShapeDtypeStruct((2 * REACH, REACH, depth), F32)
+    whole = jax.ShapeDtypeStruct(flat, F32)
     square = jax.ShapeDtypeStruct((length, length), F32)
     wave = jnp.broadcast_to(wavelet[:, None], (wavelet.shape[0], length))
 
@@ -210,7 +257,9 @@
             name=name,
         )(*inputs)
 
-    near, far, edge = kernel(open_kernel, (half, half, rims), (sides, pressure.reshape(flat)), name="open")
+    start = pressure.reshape(flat)
+    near = kernel(open_near_kernel, half, (sides, start), name="open_near")
+    far, edge = kernel(open_far_kernel, (half, rims), (sides, start, near), name="open_far")
     near_prior, far_prior, near_coef, far_coef, near_mark, far_mark, amp = kernel(
         tables_kernel,
         (half,) * 6 + (square,),
@@ -225,6 +274,8 @@
         name="tables",
     )
     scratch = (pltpu.VMEM((REACH, length + 16, depth), F32), pltpu.VMEM((REACH * length, depth), F32))
+    pad = (pltpu.VMEM((depth + 16, length), F32),)
+    receiver = receiver_field.reshape(flat)
     for step in range(STEPS):
         near_halo = lax.ppermute(near, "gx", near_pairs)
         far_halo = lax.ppermute(far, "gx", far_pairs)
@@ -236,24 +287,41 @@
             scratch,
             f"near{step}",
         )
-        far_next, edge = kernel(
-            functools.partial(advance_kernel, step, 1),
-            (half, rims),
-            (sides, far, near, far_halo, edge_in, far_prior, far_coef, far_mark, amp, near_next),
-            scratch,
-            f"far{step}",
-        )
+        far_inputs = (sides, far, near, far_halo, edge_in, far_prior, far_coef, far_mark, amp)
+        if step < STEPS - 1:
+            far_next, edge = kernel(
+                functools.partial(advance_kernel, step, 1),
+                (half, rims),
+                far_inputs + (near_next,),
+                scratch,
+                f"far{step}",
+            )
+        else:
+            part = kernel(
+                image_near_kernel,
+                jax.ShapeDtypeStruct((depth * REACH, length), F32),
+                (sides, near_next, receiver, receiver_depth),
+                pad,
+                "image_near",
+            )
+            far_next, filtered = kernel(
+                functools.partial(last_kernel, step),
+                (half, whole),
+                far_inputs + (receiver, receiver_depth, part),
+                scratch + pad,
+                f"far{step}",
+            )
         near_prior, far_prior = near, far
         near, far = near_next, far_next
-    whole = jax.ShapeDtypeStruct(flat, F32)
-    final, filtered = kernel(
-        close_kernel,
-        (whole, whole),
-        (sides, near, far, receiver_field.reshape(flat), receiver_depth),
-        (pltpu.VMEM(flat, F32),),
-        "close",
+    levels = depth // size
+    parts = lax.all_to_all(filtered, "gx", split_axis=0, concat_axis=0, tiled=True)
+    final = kernel(final_kernel, whole, (sides, near, far), name="final")
+    image = kernel(
+        functools.partial(join_kernel, levels),
+        jax.ShapeDtypeStruct((levels, size * width, length), F32),
+        (parts,),
+        name="join",
     )
-    image = lax.all_to_all(filtered.reshape(depth, width, length), "gx", split_axis=0, concat_axis=1, tiled=True)
     return final.reshape(depth, width, length), image
 
 

time: 182 us -> 182 us (level)
  blocking collectives: 95 us -> 0 us
  waiting for transfers between devices: 40 us -> 98.5 us
  starting transfers between devices: 30.1 us -> 65.6 us
  Pallas kernels: 12 us -> 13.9 us
    all_to_all x1 -> x0, blocking collectives: 95 us -> none  [shards(): lax.all_to_all(filtered.reshape(depth, width, length), 'gx', split_axis=0...]
    all_to_all x0 -> x1, waiting for transfers between devices: none -> 59 us  [shards(): lax.all_to_all(filtered, 'gx', split_axis=0, concat_axis=0, tiled=True)]
    all_to_all x0 -> x1, starting transfers between devices: none -> 35 us  [shards(): lax.all_to_all(filtered, 'gx', split_axis=0, concat_axis=0, tiled=True)]
    pallas_call x19 -> x22, Pallas kernels: 12 us -> 13.9 us  [kernel(): pl.pallas_call(body, out_shape=outs, in_specs=[VM] * len(inputs), out_spe...]
  transfers between devices with their start and end apart: 24 -> 25, of which waited for: 15 -> 16; matrix products, arithmetic and copies ran while one was open for 0% -> 0% of each run, Pallas kernels for 5% -> 6%
where the time goes in v4:
time: 182 us; the launch traced here: 181 us
  waiting for transfers between devices  98.5 us (54%)
  starting transfers between devices  65.6 us (36%)
  Pallas kernels  13.9 us (8%)
  local copies, waits for them, and re-layouts  2.32 us (1%)
    all_to_all x1, waiting for transfers between devices, shards(): lax.all_to_all(filtered, 'gx', split_axis=0, concat_axis=0, tiled=True)  59 us
    all_to_all x1, starting transfers between devices, shards(): lax.all_to_all(filtered, 'gx', split_axis=0, concat_axis=0, tiled=True)  35 us
    ppermute x8, waiting for transfers between devices, shards(): near_halo = lax.ppermute(near, 'gx', near_pairs)  31.4 us
    ppermute x8, starting transfers between devices, shards(): near_halo = lax.ppermute(near, 'gx', near_pairs)  23.9 us
    pallas_call x22, Pallas kernels, kernel(): pl.pallas_call(body, out_shape=outs, in_specs=[VM] * len(inputs), out_spe...  13.9 us
    ppermute x8, waiting for transfers between devices, shards(): edge_in = lax.ppermute(edge, 'gy', rim_pairs)  8.1 us
    ppermute x8, starting transfers between devices, shards(): far_halo = lax.ppermute(far, 'gx', far_pairs)  5.55 us
  transfers between devices with their start and end apart: 25, of which 16 were waited for; matrix products, arithmetic and copies ran while one was open for 0% of the time, Pallas kernels for 6%

profile of v4, /device:TPU:46, one launch (start us, length us, event | category | flops | bytes accessed | tf_op | source)
XLA Modules:
  0.0 181.3 jit_solution(14482261095834880744)
XLA Ops:
  0.7 1.0 copy-done.1
  1.9 2.2 %collective-permute-start = (f32[4,128,128]{2,1,0:T(8,128)S(1)}, f32[4,128,128]{2,1,0:T(8,128)S(1)}, u32[]{:S(2)}, u32[]{:S(2)}) collective-permute-start(f32[4,128,128]{2,1,0:T(8,128)S(1)} %open_near.1.near_ref.self_ref.other_ref.prior_ref), channel_id=1, source_target_pairs={{0,2},{4,6},{8,10},{12,14},{16,18},{20,22},{24,26},{28,30},{32,34}... | collective-permute-start | bytes 786440 | tf_op jit(solution)/shard_map/ppermute | solution.py:280
  4.3 0.8 collective-permute-start.2
  7.1 3.4 %collective-permute-done.halo_ref = f32[4,128,128]{2,1,0:T(8,128)S(1)} collective-permute-done((f32[4,128,128]{2,1,0:T(8,128)S(1)}, f32[4,128,128]{2,1,0:T(8,128)S(1)}, u32[]{:S(2)}, u32[]{:S(2)}) %collective-permute-start) | collective-permute-done | bytes 262176 | tf_op jit(solution)/shard_map/ppermute | solution.py:280
  10.6 0.6 near0.1.rest_0_.self_ref.other_ref.prior_ref
  11.2 2.2 %collective-permute-start.3 = (f32[4,128,128]{2,1,0:T(8,128)S(1)}, f32[4,128,128]{2,1,0:T(8,128)S(1)}, u32[]{:S(2)}, u32[]{:S(2)}) collective-permute-start(f32[4,128,128]{2,1,0:T(8,128)S(1)} %near0.1.rest_0_.self_ref.other_ref.prior_ref), channel_id=1, source_target_pairs={{0,2},{4,6},{8,10},{12,14},{16,18},{20,22},{24,26},{28,30},{32,34}... | collective-permute-start | bytes 786440 | tf_op jit(solution)/shard_map/ppermute | solution.py:280
  13.4 0.6 far0.1
  14.0 0.7 collective-permute-start.5
  14.8 1.2 collective-permute-done.4.rim_in_ref
  16.0 3.9 %collective-permute-done.3.halo_ref = f32[4,128,128]{2,1,0:T(8,128)S(1)} collective-permute-done((f32[4,128,128]{2,1,0:T(8,128)S(1)}, f32[4,128,128]{2,1,0:T(8,128)S(1)}, u32[]{:S(2)}, u32[]{:S(2)}) %collective-permute-start.3) | collective-permute-done | bytes 262176 | tf_op jit(solution)/shard_map/ppermute | solution.py:280
  19.9 0.6 near1.1.rest_0_.self_ref.other_ref.prior_ref
  20.5 2.9 %collective-permute-start.6 = (f32[4,128,128]{2,1,0:T(8,128)S(1)}, f32[4,128,128]{2,1,0:T(8,128)S(1)}, u32[]{:S(2)}, u32[]{:S(2)}) collective-permute-start(f32[4,128,128]{2,1,0:T(8,128)S(1)} %near1.1.rest_0_.self_ref.other_ref.prior_ref), channel_id=1, source_target_pairs={{0,2},{4,6},{8,10},{12,14},{16,18},{20,22},{24,26},{28,30},{32,34}... | collective-permute-start | bytes 786440 | tf_op jit(solution)/shard_map/ppermute | solution.py:280
  23.5 0.6 far1.1
  24.1 0.7 collective-permute-start.8
  24.9 1.2 collective-permute-done.7.rim_in_ref
  26.1 4.0 %collective-permute-done.6.halo_ref = f32[4,128,128]{2,1,0:T(8,128)S(1)} collective-permute-done((f32[4,128,128]{2,1,0:T(8,128)S(1)}, f32[4,128,128]{2,1,0:T(8,128)S(1)}, u32[]{:S(2)}, u32[]{:S(2)}) %collective-permute-start.6) | collective-permute-done | bytes 262176 | tf_op jit(solution)/shard_map/ppermute | solution.py:280
  30.7 3.7 %collective-permute-start.9 = (f32[4,128,128]{2,1,0:T(8,128)S(1)}, f32[4,128,128]{2,1,0:T(8,128)S(1)}, u32[]{:S(2)}, u32[]{:S(2)}) collective-permute-start(f32[4,128,128]{2,1,0:T(8,128)S(1)} %near2.1.rest_0_.self_ref.other_ref.prior_ref), channel_id=1, source_target_pairs={{0,2},{4,6},{8,10},{12,14},{16,18},{20,22},{24,26},{28,30},{32,34}... | collective-permute-start | bytes 786440 | tf_op jit(solution)/shard_map/ppermute | solution.py:280
  34.4 0.6 far2.1
  35.0 0.7 collective-permute-start.11
  35.9 1.2 collective-permute-done.10.rim_in_ref
  37.0 4.0 %collective-permute-done.9.halo_ref = f32[4,128,128]{2,1,0:T(8,128)S(1)} collective-permute-done((f32[4,128,128]{2,1,0:T(8,128)S(1)}, f32[4,128,128]{2,1,0:T(8,128)S(1)}, u32[]{:S(2)}, u32[]{:S(2)}) %collective-permute-start.9) | collective-permute-done | bytes 262176 | tf_op jit(solution)/shard_map/ppermute | solution.py:280
  41.6 3.5 %collective-permute-start.12 = (f32[4,128,128]{2,1,0:T(8,128)S(1)}, f32[4,128,128]{2,1,0:T(8,128)S(1)}, u32[]{:S(2)}, u32[]{:S(2)}) collective-permute-start(f32[4,128,128]{2,1,0:T(8,128)S(1)} %near3.1.rest_0_.self_ref.other_ref.prior_ref), channel_id=1, source_target_pairs={{0,2},{4,6},{8,10},{12,14},{16,18},{20,22},{24,26},{28,30},{32,34}... | collective-permute-start | bytes 786440 | tf_op jit(solution)/shard_map/ppermute | solution.py:280
  45.1 0.6 far3.1
  45.8 0.7 collective-permute-start.14
  46.6 1.2 collective-permute-done.13.rim_in_ref
  47.7 4.0 %collective-permute-done.12.halo_ref = f32[4,128,128]{2,1,0:T(8,128)S(1)} collective-permute-done((f32[4,128,128]{2,1,0:T(8,128)S(1)}, f32[4,128,128]{2,1,0:T(8,128)S(1)}, u32[]{:S(2)}, u32[]{:S(2)}) %collective-permute-start.12) | collective-permute-done | bytes 262176 | tf_op jit(solution)/shard_map/ppermute | solution.py:280
  51.8 0.6 near4.1.rest_0_.self_ref.other_ref.prior_ref
  52.4 3.6 %collective-permute-start.15 = (f32[4,128,128]{2,1,0:T(8,128)S(1)}, f32[4,128,128]{2,1,0:T(8,128)S(1)}, u32[]{:S(2)}, u32[]{:S(2)}) collective-permute-start(f32[4,128,128]{2,1,0:T(8,128)S(1)} %near4.1.rest_0_.self_ref.other_ref.prior_ref), channel_id=1, source_target_pairs={{0,2},{4,6},{8,10},{12,14},{16,18},{20,22},{24,26},{28,30},{32,34}... | collective-permute-start | bytes 786440 | tf_op jit(solution)/shard_map/ppermute | solution.py:280
  56.0 0.6 far4.1
  56.6 0.7 collective-permute-start.17
  57.4 1.2 collective-permute-done.16.rim_in_ref
  58.6 4.0 %collective-permute-done.15.halo_ref = f32[4,128,128]{2,1,0:T(8,128)S(1)} collective-permute-done((f32[4,128,128]{2,1,0:T(8,128)S(1)}, f32[4,128,128]{2,1,0:T(8,128)S(1)}, u32[]{:S(2)}, u32[]{:S(2)}) %collective-permute-start.15) | collective-permute-done | bytes 262176 | tf_op jit(solution)/shard_map/ppermute | solution.py:280
  63.2 2.7 %collective-permute-start.18 = (f32[4,128,128]{2,1,0:T(8,128)S(1)}, f32[4,128,128]{2,1,0:T(8,128)S(1)}, u32[]{:S(2)}, u32[]{:S(2)}) collective-permute-start(f32[4,128,128]{2,1,0:T(8,128)S(1)} %near5.1.rest_0_.self_ref.other_ref.prior_ref), channel_id=1, source_target_pairs={{0,2},{4,6},{8,10},{12,14},{16,18},{20,22},{24,26},{28,30},{32,34}... | collective-permute-start | bytes 786440 | tf_op jit(solution)/shard_map/ppermute | solution.py:280
  65.9 0.6 far5.1
  66.6 0.7 collective-permute-start.20
  67.4 1.2 collective-permute-done.19.rim_in_ref
  68.6 4.0 %collective-permute-done.18.halo_ref = f32[4,128,128]{2,1,0:T(8,128)S(1)} collective-permute-done((f32[4,128,128]{2,1,0:T(8,128)S(1)}, f32[4,128,128]{2,1,0:T(8,128)S(1)}, u32[]{:S(2)}, u32[]{:S(2)}) %collective-permute-start.18) | collective-permute-done | bytes 262176 | tf_op jit(solution)/shard_map/ppermute | solution.py:280
  73.2 3.1 %collective-permute-start.21 = (f32[4,128,128]{2,1,0:T(8,128)S(1)}, f32[4,128,128]{2,1,0:T(8,128)S(1)}, u32[]{:S(2)}, u32[]{:S(2)}) collective-permute-start(f32[4,128,128]{2,1,0:T(8,128)S(1)} %near6.1.rest_0_.self_ref.rest_1_), channel_id=1, source_target_pairs={{0,2},{4,6},{8,10},{12,14},{16,18},{20,22},{24,26},{28,30},{32,34}... | collective-permute-start | bytes 786440 | tf_op jit(solution)/shard_map/ppermute | solution.py:280
  76.3 0.6 far6.1
  76.9 0.7 collective-permute-start.23
  77.8 1.2 collective-permute-done.22.rim_in_ref.rest_3_
  78.9 4.0 %collective-permute-done.21.halo_ref = f32[4,128,128]{2,1,0:T(8,128)S(1)} collective-permute-done((f32[4,128,128]{2,1,0:T(8,128)S(1)}, f32[4,128,128]{2,1,0:T(8,128)S(1)}, u32[]{:S(2)}, u32[]{:S(2)}) %collective-permute-start.21) | collective-permute-done | bytes 262176 | tf_op jit(solution)/shard_map/ppermute | solution.py:280
  82.9 0.6 near7.1.near_ref
  83.8 1.7 far7.1
  85.5 35.0 %all-to-all-start = ((f32[32,32,128]{2,1,0:T(8,128)}), f32[32,32,128]{2,1,0:T(8,128)S(1)}, u32[]{:S(2)}, u32[]{:S(2)}) async-start(f32[32,32,128]{2,1,0:T(8,128)} %bitcast.5), calls=%async_computation | async-start | bytes 1048576 | tf_op jit(solution)/shard_map/all_to_all | solution.py:317
  120.5 1.0 final.1
  121.5 59.0 %all-to-all-done = f32[32,32,128]{2,1,0:T(8,128)S(1)} async-done(((f32[32,32,128]{2,1,0:T(8,128)}), f32[32,32,128]{2,1,0:T(8,128)S(1)}, u32[]{:S(2)}, u32[]{:S(2)}) %all-to-all-start) | async-done | bytes 524320 | tf_op jit(solution)/shard_map/all_to_all | solution.py:317
  180.5 0.8 join.1
  (44 shorter events, 6.0 us)
Async XLA Ops:
  0.7 1.0 copy-start.1
  1.9 3.4 %copy-start.6 = (bf16[128,8,128]{2,1,0:T(8,128)(2,1)S(1)}, bf16[128,8,128]{2,1,0:T(8,128)(2,1)}, u32[]{:S(2)}) copy-start(bf16[128,8,128]{2,1,0:T(8,128)(2,1)} %param.10) | copy-start | bytes 786436
  1.9 8.6 %collective-permute-start = (f32[4,128,128]{2,1,0:T(8,128)S(1)}, f32[4,128,128]{2,1,0:T(8,128)S(1)}, u32[]{:S(2)}, u32[]{:S(2)}) collective-permute-start(f32[4,128,128]{2,1,0:T(8,128)S(1)} %open_near.1.near_ref.self_ref.other_ref.prior_ref), channel_id=1, source_target_pairs={{0,2},{4,6},{8,10},{12,14},{16,18},{20,22},{24,26},{28,30},{32,34}... | collective-permute-start | bytes 786440 | tf_op jit(solution)/shard_map/ppermute | solution.py:280
  4.3 1.6 copy-start.2
  4.3 9.1 %collective-permute-start.2 = (f32[4,128,128]{2,1,0:T(8,128)S(1)}, f32[4,128,128]{2,1,0:T(8,128)S(1)}, u32[]{:S(2)}, u32[]{:S(2)}) collective-permute-start(f32[4,128,128]{2,1,0:T(8,128)S(1)} %get-tuple-element.27.other_ref.self_ref.prior_ref), channel_id=1, source_target_pairs={{2,4},{6,8},{10,12},{14,16},{18,20},{22,24},{26,28},{30,32},{34,36... | collective-permute-start | bytes 786440 | tf_op jit(solution)/shard_map/ppermute | solution.py:281
  5.1 0.7 copy-start.7
  5.2 2.0 %collective-permute-start.1 = (f32[8,4,128]{2,1,0:T(4,128)S(1)}, f32[8,4,128]{2,1,0:T(4,128)S(1)}, u32[]{:S(2)}, u32[]{:S(2)}) collective-permute-start(f32[8,4,128]{2,1,0:T(4,128)S(1)} %get-tuple-element.28), channel_id=1, source_target_pairs={{0,1},{1,0},{2,3},{3,2},{4,5},{5,4},{6,7},{7,6},{8,9},{9,8},{10,11... | collective-permute-start | bytes 49160 | tf_op jit(solution)/shard_map/ppermute | solution.py:282
  5.8 0.7 copy-start.4
  5.8 0.7 copy-start.5
  11.2 8.7 %collective-permute-start.3 = (f32[4,128,128]{2,1,0:T(8,128)S(1)}, f32[4,128,128]{2,1,0:T(8,128)S(1)}, u32[]{:S(2)}, u32[]{:S(2)}) collective-permute-start(f32[4,128,128]{2,1,0:T(8,128)S(1)} %near0.1.rest_0_.self_ref.other_ref.prior_ref), channel_id=1, source_target_pairs={{0,2},{4,6},{8,10},{12,14},{16,18},{20,22},{24,26},{28,30},{32,34}... | collective-permute-start | bytes 786440 | tf_op jit(solution)/shard_map/ppermute | solution.py:280
  14.0 9.4 %collective-permute-start.5 = (f32[4,128,128]{2,1,0:T(8,128)S(1)}, f32[4,128,128]{2,1,0:T(8,128)S(1)}, u32[]{:S(2)}, u32[]{:S(2)}) collective-permute-start(f32[4,128,128]{2,1,0:T(8,128)S(1)} %get-tuple-element.36.other_ref.self_ref.prior_ref), channel_id=1, source_target_pairs={{2,4},{6,8},{10,12},{14,16},{18,20},{22,24},{26,28},{30,32},{34,36... | collective-permute-start | bytes 786440 | tf_op jit(solution)/shard_map/ppermute | solution.py:281
  14.7 1.3 collective-permute-start.4
  20.5 9.6 %collective-permute-start.6 = (f32[4,128,128]{2,1,0:T(8,128)S(1)}, f32[4,128,128]{2,1,0:T(8,128)S(1)}, u32[]{:S(2)}, u32[]{:S(2)}) collective-permute-start(f32[4,128,128]{2,1,0:T(8,128)S(1)} %near1.1.rest_0_.self_ref.other_ref.prior_ref), channel_id=1, source_target_pairs={{0,2},{4,6},{8,10},{12,14},{16,18},{20,22},{24,26},{28,30},{32,34}... | collective-permute-start | bytes 786440 | tf_op jit(solution)/shard_map/ppermute | solution.py:280
  24.1 10.3 %collective-permute-start.8 = (f32[4,128,128]{2,1,0:T(8,128)S(1)}, f32[4,128,128]{2,1,0:T(8,128)S(1)}, u32[]{:S(2)}, u32[]{:S(2)}) collective-permute-start(f32[4,128,128]{2,1,0:T(8,128)S(1)} %get-tuple-element.38.other_ref.self_ref.prior_ref), channel_id=1, source_target_pairs={{2,4},{6,8},{10,12},{14,16},{18,20},{22,24},{26,28},{30,32},{34,36... | collective-permute-start | bytes 786440 | tf_op jit(solution)/shard_map/ppermute | solution.py:281
  24.8 1.3 collective-permute-start.7
  30.7 10.3 %collective-permute-start.9 = (f32[4,128,128]{2,1,0:T(8,128)S(1)}, f32[4,128,128]{2,1,0:T(8,128)S(1)}, u32[]{:S(2)}, u32[]{:S(2)}) collective-permute-start(f32[4,128,128]{2,1,0:T(8,128)S(1)} %near2.1.rest_0_.self_ref.other_ref.prior_ref), channel_id=1, source_target_pairs={{0,2},{4,6},{8,10},{12,14},{16,18},{20,22},{24,26},{28,30},{32,34}... | collective-permute-start | bytes 786440 | tf_op jit(solution)/shard_map/ppermute | solution.py:280
  35.0 10.1 %collective-permute-start.11 = (f32[4,128,128]{2,1,0:T(8,128)S(1)}, f32[4,128,128]{2,1,0:T(8,128)S(1)}, u32[]{:S(2)}, u32[]{:S(2)}) collective-permute-start(f32[4,128,128]{2,1,0:T(8,128)S(1)} %get-tuple-element.40.other_ref.self_ref.prior_ref), channel_id=1, source_target_pairs={{2,4},{6,8},{10,12},{14,16},{18,20},{22,24},{26,28},{30,32},{34,36... | collective-permute-start | bytes 786440 | tf_op jit(solution)/shard_map/ppermute | solution.py:281
  35.7 1.3 collective-permute-start.10
  41.6 10.1 %collective-permute-start.12 = (f32[4,128,128]{2,1,0:T(8,128)S(1)}, f32[4,128,128]{2,1,0:T(8,128)S(1)}, u32[]{:S(2)}, u32[]{:S(2)}) collective-permute-start(f32[4,128,128]{2,1,0:T(8,128)S(1)} %near3.1.rest_0_.self_ref.other_ref.prior_ref), channel_id=1, source_target_pairs={{0,2},{4,6},{8,10},{12,14},{16,18},{20,22},{24,26},{28,30},{32,34}... | collective-permute-start | bytes 786440 | tf_op jit(solution)/shard_map/ppermute | solution.py:280
  45.8 10.2 %collective-permute-start.14 = (f32[4,128,128]{2,1,0:T(8,128)S(1)}, f32[4,128,128]{2,1,0:T(8,128)S(1)}, u32[]{:S(2)}, u32[]{:S(2)}) collective-permute-start(f32[4,128,128]{2,1,0:T(8,128)S(1)} %get-tuple-element.42.other_ref.self_ref.prior_ref), channel_id=1, source_target_pairs={{2,4},{6,8},{10,12},{14,16},{18,20},{22,24},{26,28},{30,32},{34,36... | collective-permute-start | bytes 786440 | tf_op jit(solution)/shard_map/ppermute | solution.py:281
  46.4 1.3 collective-permute-start.13
  52.4 10.2 %collective-permute-start.15 = (f32[4,128,128]{2,1,0:T(8,128)S(1)}, f32[4,128,128]{2,1,0:T(8,128)S(1)}, u32[]{:S(2)}, u32[]{:S(2)}) collective-permute-start(f32[4,128,128]{2,1,0:T(8,128)S(1)} %near4.1.rest_0_.self_ref.other_ref.prior_ref), channel_id=1, source_target_pairs={{0,2},{4,6},{8,10},{12,14},{16,18},{20,22},{24,26},{28,30},{32,34}... | collective-permute-start | bytes 786440 | tf_op jit(solution)/shard_map/ppermute | solution.py:280
  56.6 9.3 %collective-permute-start.17 = (f32[4,128,128]{2,1,0:T(8,128)S(1)}, f32[4,128,128]{2,1,0:T(8,128)S(1)}, u32[]{:S(2)}, u32[]{:S(2)}) collective-permute-start(f32[4,128,128]{2,1,0:T(8,128)S(1)} %get-tuple-element.44.other_ref.self_ref.prior_ref), channel_id=1, source_target_pairs={{2,4},{6,8},{10,12},{14,16},{18,20},{22,24},{26,28},{30,32},{34,36... | collective-permute-start | bytes 786440 | tf_op jit(solution)/shard_map/ppermute | solution.py:281
  57.3 1.3 collective-permute-start.16
  63.2 9.4 %collective-permute-start.18 = (f32[4,128,128]{2,1,0:T(8,128)S(1)}, f32[4,128,128]{2,1,0:T(8,128)S(1)}, u32[]{:S(2)}, u32[]{:S(2)}) collective-permute-start(f32[4,128,128]{2,1,0:T(8,128)S(1)} %near5.1.rest_0_.self_ref.other_ref.prior_ref), channel_id=1, source_target_pairs={{0,2},{4,6},{8,10},{12,14},{16,18},{20,22},{24,26},{28,30},{32,34}... | collective-permute-start | bytes 786440 | tf_op jit(solution)/shard_map/ppermute | solution.py:280
  66.6 9.7 %collective-permute-start.20 = (f32[4,128,128]{2,1,0:T(8,128)S(1)}, f32[4,128,128]{2,1,0:T(8,128)S(1)}, u32[]{:S(2)}, u32[]{:S(2)}) collective-permute-start(f32[4,128,128]{2,1,0:T(8,128)S(1)} %get-tuple-element.46.other_ref.self_ref.rest_4_), channel_id=1, source_target_pairs={{2,4},{6,8},{10,12},{14,16},{18,20},{22,24},{26,28},{30,32},{34,36... | collective-permute-start | bytes 786440 | tf_op jit(solution)/shard_map/ppermute | solution.py:281
  67.2 1.3 collective-permute-start.19
  73.2 9.7 %collective-permute-start.21 = (f32[4,128,128]{2,1,0:T(8,128)S(1)}, f32[4,128,128]{2,1,0:T(8,128)S(1)}, u32[]{:S(2)}, u32[]{:S(2)}) collective-permute-start(f32[4,128,128]{2,1,0:T(8,128)S(1)} %near6.1.rest_0_.self_ref.rest_1_), channel_id=1, source_target_pairs={{0,2},{4,6},{8,10},{12,14},{16,18},{20,22},{24,26},{28,30},{32,34}... | collective-permute-start | bytes 786440 | tf_op jit(solution)/shard_map/ppermute | solution.py:280
  76.9 6.9 %collective-permute-start.23 = (f32[4,128,128]{2,1,0:T(8,128)S(1)}, f32[4,128,128]{2,1,0:T(8,128)S(1)}, u32[]{:S(2)}, u32[]{:S(2)}) collective-permute-start(f32[4,128,128]{2,1,0:T(8,128)S(1)} %get-tuple-element.48.other_ref.rest_0_), channel_id=1, source_target_pairs={{2,4},{6,8},{10,12},{14,16},{18,20},{22,24},{26,28},{30,32},{34,36... | collective-permute-start | bytes 786440 | tf_op jit(solution)/shard_map/ppermute | solution.py:281
  77.6 6.0 %copy-start = (f32[128,8,128]{2,1,0:T(8,128)S(1)}, f32[128,8,128]{2,1,0:T(8,128)}, u32[]{:S(2)}) copy-start(f32[128,8,128]{2,1,0:T(8,128)} %param.15) | copy-start | bytes 1572868
  77.6 1.3 collective-permute-start.22
  82.9 0.7 copy-start.3
  85.5 95.0 %all-to-all-start = ((f32[32,32,128]{2,1,0:T(8,128)}), f32[32,32,128]{2,1,0:T(8,128)S(1)}, u32[]{:S(2)}, u32[]{:S(2)}) async-start(f32[32,32,128]{2,1,0:T(8,128)} %bitcast.5), calls=%async_computation | async-start | bytes 1048576 | tf_op jit(solution)/shard_map/all_to_all | solution.py:317

commit v5 on v4

--- a/solution.py
+++ b/solution.py
@@ -104,10 +104,7 @@
     pad_ref, deep_ref = rest[-2:]
     first = sides_ref[1:2, :]
     planes, length, depth = self_ref.shape
-    if len(rest) > 3:
-        near_new_ref, out_ref, rim_ref = rest[:3]
-    else:
-        out_ref, rim_ref = rest[0], None
+    out_ref = rest[-3]
     for i in range(planes):
         edge = rim_in_ref[half * REACH + i]
         none = jnp.zeros_like(edge)
@@ -131,11 +128,14 @@
         at = slice(row, row + CHUNK)
         line = [other_ref[REACH - 1 - i, at, :] for i in range(REACH)]
         line += [self_ref[i, at, :] for i in range(REACH)]
-        line += [halo_ref[REACH - 1 - i, at, :] for i in range(REACH)]
+        if halo_ref is not None:
+            line += [halo_ref[REACH - 1 - i, at, :] for i in range(REACH)]
         for i in range(planes):
             total = deep_ref[i * length + row : i * length + row + CHUNK, :]
             for k in range(1, REACH + 1):
-                around = line[REACH + i - k] + line[REACH + i + k]
+                around = line[REACH + i - k]
+                if REACH + i + k < len(line):
+                    around = around + line[REACH + i + k]
                 around = around + pad_ref[i, 8 + row - k : 8 + row - k + CHUNK, :]
                 around = around + pad_ref[i, 8 + row + k : 8 + row + k + CHUNK, :]
                 total = total + COEFS[k - 1] * around
@@ -146,10 +146,29 @@
                 + coef_ref[i, at, :] * total
                 + mark_ref[i, at, :] * amp_ref[at, column : column + 1]
             )
-    if rim_ref is not None:
+
+
+def inner_kernel(step, half, sides_ref, self_ref, other_ref, *rest):
+    advance_kernel(step, half, sides_ref, self_ref, other_ref, None, *rest)
+
+
+def add_halo(base_ref, coef_ref, halo_ref, out_ref):
+    planes, length, _ = base_ref.shape
+    for row in range(0, length, CHUNK):
+        at = slice(row, row + CHUNK)
         for i in range(planes):
-            rim_ref[i] = rim(near_new_ref, i, first)
-            rim_ref[REACH + i] = rim(out_ref, i, first)
+            for k in range(REACH - i, REACH + 1):
+                term = COEFS[k - 1] * halo_ref[2 * REACH - 1 - i - k, at, :]
+                total = term if k == REACH - i else total + term
+            out_ref[i, at, :] = base_ref[i, at, :] + coef_ref[i, at, :] * total
+
+
+def outer_kernel(sides_ref, base_ref, coef_ref, halo_ref, near_ref, out_ref, rim_ref):
+    first = sides_ref[1:2, :]
+    add_halo(base_ref, coef_ref, halo_ref, out_ref)
+    for i in range(REACH):
+        rim_ref[i] = rim(near_ref, i, first)
+        rim_ref[REACH + i] = rim(out_ref, i, first)
 
 
 def image_half(is_near, sides_ref, half_ref, receiver_ref, receiver_depth_ref, image_ref, pad_ref, row, stride):
@@ -185,9 +204,10 @@
     image_half(True, sides_ref, near_ref, receiver_ref, receiver_depth_ref, image_ref, pad_ref, 0, REACH)
 
 
-def last_kernel(step, sides_ref, *rest):
-    receiver_ref, receiver_depth_ref, part_ref, far_ref, image_ref, side_ref, deep_ref, pad_ref = rest[-8:]
-    advance_kernel(step, 1, sides_ref, *rest[:-8], far_ref, side_ref, deep_ref)
+def last_kernel(
+    sides_ref, base_ref, coef_ref, halo_ref, receiver_ref, receiver_depth_ref, part_ref, far_ref, image_ref, pad_ref
+):
+    add_halo(base_ref, coef_ref, halo_ref, far_ref)
     width = 2 * REACH
     depth = part_ref.shape[0] // REACH
     image_half(False, sides_ref, far_ref, receiver_ref, receiver_depth_ref, image_ref, pad_ref, REACH, width)
@@ -287,14 +307,16 @@
             scratch,
             f"near{step}",
         )
-        far_inputs = (sides, far, near, far_halo, edge_in, far_prior, far_coef, far_mark, amp)
+        base = kernel(
+            functools.partial(inner_kernel, step, 1),
+            half,
+            (sides, far, near, edge_in, far_prior, far_coef, far_mark, amp, near_next),
+            scratch,
+            f"inner{step}",
+        )
         if step < STEPS - 1:
             far_next, edge = kernel(
-                functools.partial(advance_kernel, step, 1),
-                (half, rims),
-                far_inputs + (near_next,),
-                scratch,
-                f"far{step}",
+                outer_kernel, (half, rims), (sides, base, far_coef, far_halo, near_next), name=f"far{step}"
             )
         else:
             part = kernel(
@@ -305,10 +327,10 @@
                 "image_near",
             )
             far_next, filtered = kernel(
-                functools.partial(last_kernel, step),
+                last_kernel,
                 (half, whole),
-                far_inputs + (receiver, receiver_depth, part),
-                scratch + pad,
+                (sides, base, far_coef, far_halo, receiver, receiver_depth, part),
+                pad,
                 f"far{step}",
             )
         near_prior, far_prior = near, far

time: 182 us -> 178 us (0.978)
  starting transfers between devices: 65.6 us -> 61.2 us
    all_to_all x1, starting transfers between devices: 35 us -> 32.5 us  [shards(): lax.all_to_all(filtered, 'gx', split_axis=0, concat_axis=0, tiled=True)]
    ppermute x8, starting transfers between devices: 23.9 us -> 22 us  [shards(): near_halo = lax.ppermute(near, 'gx', near_pairs)]
    pallas_call x22 -> x30, Pallas kernels: 13.9 us -> 13.5 us  [kernel(): pl.pallas_call(body, out_shape=outs, in_specs=[VM] * len(inputs), out_spe...]
where the time goes in v5:
time: 178 us; the launch traced here: 177 us
  waiting for transfers between devices  99.1 us (56%)
  starting transfers between devices  61.2 us (34%)
  Pallas kernels  13.5 us (8%)
  local copies, waits for them, and re-layouts  2.36 us (1%)
    all_to_all x1, waiting for transfers between devices, shards(): lax.all_to_all(filtered, 'gx', split_axis=0, concat_axis=0, tiled=True)  59.5 us
    all_to_all x1, starting transfers between devices, shards(): lax.all_to_all(filtered, 'gx', split_axis=0, concat_axis=0, tiled=True)  32.5 us
    ppermute x8, waiting for transfers between devices, shards(): near_halo = lax.ppermute(near, 'gx', near_pairs)  31.5 us
    ppermute x8, starting transfers between devices, shards(): near_halo = lax.ppermute(near, 'gx', near_pairs)  22 us
    pallas_call x30, Pallas kernels, kernel(): pl.pallas_call(body, out_shape=outs, in_specs=[VM] * len(inputs), out_spe...  13.5 us
    ppermute x8, waiting for transfers between devices, shards(): edge_in = lax.ppermute(edge, 'gy', rim_pairs)  8.1 us
    ppermute x8, starting transfers between devices, shards(): far_halo = lax.ppermute(far, 'gx', far_pairs)  5.55 us
  transfers between devices with their start and end apart: 25, of which 16 were waited for; matrix products, arithmetic and copies ran while one was open for 0% of the time, Pallas kernels for 6%

profile of v5, /device:TPU:46, one launch (start us, length us, event | category | flops | bytes accessed | tf_op | source)
XLA Modules:
  0.0 177.3 jit_solution(8302164434633912502)
XLA Ops:
  0.7 1.0 copy-done.1
  1.9 2.2 %collective-permute-start = (f32[4,128,128]{2,1,0:T(8,128)S(1)}, f32[4,128,128]{2,1,0:T(8,128)S(1)}, u32[]{:S(2)}, u32[]{:S(2)}) collective-permute-start(f32[4,128,128]{2,1,0:T(8,128)S(1)} %open_near.1.near_ref.self_ref.other_ref.prior_ref), channel_id=1, source_target_pairs={{0,2},{4,6},{8,10},{12,14},{16,18},{20,22},{24,26},{28,30},{32,34}... | collective-permute-start | bytes 786440 | tf_op jit(solution)/shard_map/ppermute | solution.py:300
  4.3 0.8 collective-permute-start.2
  5.9 0.6 copy-done.4
  6.5 0.6 tables.1
  7.1 3.4 %collective-permute-done.halo_ref = f32[4,128,128]{2,1,0:T(8,128)S(1)} collective-permute-done((f32[4,128,128]{2,1,0:T(8,128)S(1)}, f32[4,128,128]{2,1,0:T(8,128)S(1)}, u32[]{:S(2)}, u32[]{:S(2)}) %collective-permute-start) | collective-permute-done | bytes 262176 | tf_op jit(solution)/shard_map/ppermute | solution.py:300
  10.6 0.6 near0.1.rest_5_.near_ref.self_ref.other_ref.prior_ref
  11.1 2.2 %collective-permute-start.3 = (f32[4,128,128]{2,1,0:T(8,128)S(1)}, f32[4,128,128]{2,1,0:T(8,128)S(1)}, u32[]{:S(2)}, u32[]{:S(2)}) collective-permute-start(f32[4,128,128]{2,1,0:T(8,128)S(1)} %near0.1.rest_5_.near_ref.self_ref.other_ref.prior_ref), channel_id=1, source_target_pairs={{0,2},{4,6},{8,10},{12,14},{16,18},{20,22},{24,26},{28,30},{32,34}... | collective-permute-start | bytes 786440 | tf_op jit(solution)/shard_map/ppermute | solution.py:300
  14.0 0.7 collective-permute-start.5
  14.8 1.2 collective-permute-done.4.rim_in_ref.rest_0_
  16.0 3.9 %collective-permute-done.3.halo_ref = f32[4,128,128]{2,1,0:T(8,128)S(1)} collective-permute-done((f32[4,128,128]{2,1,0:T(8,128)S(1)}, f32[4,128,128]{2,1,0:T(8,128)S(1)}, u32[]{:S(2)}, u32[]{:S(2)}) %collective-permute-start.3) | collective-permute-done | bytes 262176 | tf_op jit(solution)/shard_map/ppermute | solution.py:300
  19.9 0.6 near1.1.rest_5_.near_ref.self_ref.other_ref.prior_ref
  20.5 2.9 %collective-permute-start.6 = (f32[4,128,128]{2,1,0:T(8,128)S(1)}, f32[4,128,128]{2,1,0:T(8,128)S(1)}, u32[]{:S(2)}, u32[]{:S(2)}) collective-permute-start(f32[4,128,128]{2,1,0:T(8,128)S(1)} %near1.1.rest_5_.near_ref.self_ref.other_ref.prior_ref), channel_id=1, source_target_pairs={{0,2},{4,6},{8,10},{12,14},{16,18},{20,22},{24,26},{28,30},{32,34}... | collective-permute-start | bytes 786440 | tf_op jit(solution)/shard_map/ppermute | solution.py:300
  24.0 0.7 collective-permute-start.8
  24.9 1.2 collective-permute-done.7.rim_in_ref.rest_0_
  26.0 4.0 %collective-permute-done.6.halo_ref = f32[4,128,128]{2,1,0:T(8,128)S(1)} collective-permute-done((f32[4,128,128]{2,1,0:T(8,128)S(1)}, f32[4,128,128]{2,1,0:T(8,128)S(1)}, u32[]{:S(2)}, u32[]{:S(2)}) %collective-permute-start.6) | collective-permute-done | bytes 262176 | tf_op jit(solution)/shard_map/ppermute | solution.py:300
  30.1 0.6 near2.1.rest_5_.near_ref.self_ref.other_ref.prior_ref
  30.7 3.1 %collective-permute-start.9 = (f32[4,128,128]{2,1,0:T(8,128)S(1)}, f32[4,128,128]{2,1,0:T(8,128)S(1)}, u32[]{:S(2)}, u32[]{:S(2)}) collective-permute-start(f32[4,128,128]{2,1,0:T(8,128)S(1)} %near2.1.rest_5_.near_ref.self_ref.other_ref.prior_ref), channel_id=1, source_target_pairs={{0,2},{4,6},{8,10},{12,14},{16,18},{20,22},{24,26},{28,30},{32,34}... | collective-permute-start | bytes 786440 | tf_op jit(solution)/shard_map/ppermute | solution.py:300
  34.4 0.7 collective-permute-start.11
  35.2 1.2 collective-permute-done.10.rim_in_ref.rest_0_
  36.4 4.0 %collective-permute-done.9.halo_ref = f32[4,128,128]{2,1,0:T(8,128)S(1)} collective-permute-done((f32[4,128,128]{2,1,0:T(8,128)S(1)}, f32[4,128,128]{2,1,0:T(8,128)S(1)}, u32[]{:S(2)}, u32[]{:S(2)}) %collective-permute-start.9) | collective-permute-done | bytes 262176 | tf_op jit(solution)/shard_map/ppermute | solution.py:300
  40.4 0.6 near3.1.rest_5_.near_ref.self_ref.other_ref.prior_ref
  41.0 2.9 %collective-permute-start.12 = (f32[4,128,128]{2,1,0:T(8,128)S(1)}, f32[4,128,128]{2,1,0:T(8,128)S(1)}, u32[]{:S(2)}, u32[]{:S(2)}) collective-permute-start(f32[4,128,128]{2,1,0:T(8,128)S(1)} %near3.1.rest_5_.near_ref.self_ref.other_ref.prior_ref), channel_id=1, source_target_pairs={{0,2},{4,6},{8,10},{12,14},{16,18},{20,22},{24,26},{28,30},{32,34}... | collective-permute-start | bytes 786440 | tf_op jit(solution)/shard_map/ppermute | solution.py:300
  44.6 0.7 collective-permute-start.14
  45.4 1.2 collective-permute-done.13.rim_in_ref.rest_0_
  46.6 4.0 %collective-permute-done.12.halo_ref = f32[4,128,128]{2,1,0:T(8,128)S(1)} collective-permute-done((f32[4,128,128]{2,1,0:T(8,128)S(1)}, f32[4,128,128]{2,1,0:T(8,128)S(1)}, u32[]{:S(2)}, u32[]{:S(2)}) %collective-permute-start.12) | collective-permute-done | bytes 262176 | tf_op jit(solution)/shard_map/ppermute | solution.py:300
  50.6 0.6 near4.1.rest_5_.near_ref.self_ref.other_ref.prior_ref
  51.2 3.0 %collective-permute-start.15 = (f32[4,128,128]{2,1,0:T(8,128)S(1)}, f32[4,128,128]{2,1,0:T(8,128)S(1)}, u32[]{:S(2)}, u32[]{:S(2)}) collective-permute-start(f32[4,128,128]{2,1,0:T(8,128)S(1)} %near4.1.rest_5_.near_ref.self_ref.other_ref.prior_ref), channel_id=1, source_target_pairs={{0,2},{4,6},{8,10},{12,14},{16,18},{20,22},{24,26},{28,30},{32,34}... | collective-permute-start | bytes 786440 | tf_op jit(solution)/shard_map/ppermute | solution.py:300
  54.8 0.7 collective-permute-start.17
  55.7 1.2 collective-permute-done.16.rim_in_ref.rest_0_
  56.8 4.0 %collective-permute-done.15.halo_ref = f32[4,128,128]{2,1,0:T(8,128)S(1)} collective-permute-done((f32[4,128,128]{2,1,0:T(8,128)S(1)}, f32[4,128,128]{2,1,0:T(8,128)S(1)}, u32[]{:S(2)}, u32[]{:S(2)}) %collective-permute-start.15) | collective-permute-done | bytes 262176 | tf_op jit(solution)/shard_map/ppermute | solution.py:300
  60.9 0.6 near5.1.rest_5_.near_ref.self_ref.other_ref.prior_ref
  61.5 2.7 %collective-permute-start.18 = (f32[4,128,128]{2,1,0:T(8,128)S(1)}, f32[4,128,128]{2,1,0:T(8,128)S(1)}, u32[]{:S(2)}, u32[]{:S(2)}) collective-permute-start(f32[4,128,128]{2,1,0:T(8,128)S(1)} %near5.1.rest_5_.near_ref.self_ref.other_ref.prior_ref), channel_id=1, source_target_pairs={{0,2},{4,6},{8,10},{12,14},{16,18},{20,22},{24,26},{28,30},{32,34}... | collective-permute-start | bytes 786440 | tf_op jit(solution)/shard_map/ppermute | solution.py:300
  64.8 0.7 collective-permute-start.20
  65.6 1.2 collective-permute-done.19.rim_in_ref.rest_0_
  66.8 4.0 %collective-permute-done.18.halo_ref = f32[4,128,128]{2,1,0:T(8,128)S(1)} collective-permute-done((f32[4,128,128]{2,1,0:T(8,128)S(1)}, f32[4,128,128]{2,1,0:T(8,128)S(1)}, u32[]{:S(2)}, u32[]{:S(2)}) %collective-permute-start.18) | collective-permute-done | bytes 262176 | tf_op jit(solution)/shard_map/ppermute | solution.py:300
  70.8 0.6 near6.1.rest_5_.near_ref.self_ref.other_ref
  71.4 2.8 %collective-permute-start.21 = (f32[4,128,128]{2,1,0:T(8,128)S(1)}, f32[4,128,128]{2,1,0:T(8,128)S(1)}, u32[]{:S(2)}, u32[]{:S(2)}) collective-permute-start(f32[4,128,128]{2,1,0:T(8,128)S(1)} %near6.1.rest_5_.near_ref.self_ref.other_ref), channel_id=1, source_target_pairs={{0,2},{4,6},{8,10},{12,14},{16,18},{20,22},{24,26},{28,30},{32,34}... | collective-permute-start | bytes 786440 | tf_op jit(solution)/shard_map/ppermute | solution.py:300
  74.9 0.7 collective-permute-start.23
  75.7 1.2 collective-permute-done.22.rim_in_ref.rest_0_
  76.9 4.0 %collective-permute-done.21.halo_ref = f32[4,128,128]{2,1,0:T(8,128)S(1)} collective-permute-done((f32[4,128,128]{2,1,0:T(8,128)S(1)}, f32[4,128,128]{2,1,0:T(8,128)S(1)}, u32[]{:S(2)}, u32[]{:S(2)}) %collective-permute-start.21) | collective-permute-done | bytes 262176 | tf_op jit(solution)/shard_map/ppermute | solution.py:300
  80.9 0.6 near7.1.rest_5_.near_ref
  81.8 0.5 inner7.1.base_ref
  82.3 1.1 far7.1
  83.4 32.5 %all-to-all-start = ((f32[32,32,128]{2,1,0:T(8,128)}), f32[32,32,128]{2,1,0:T(8,128)S(1)}, u32[]{:S(2)}, u32[]{:S(2)}) async-start(f32[32,32,128]{2,1,0:T(8,128)} %bitcast.5), calls=%async_computation | async-start | bytes 1048576 | tf_op jit(solution)/shard_map/all_to_all | solution.py:339
  115.9 1.0 final.1
  116.9 59.5 %all-to-all-done = f32[32,32,128]{2,1,0:T(8,128)S(1)} async-done(((f32[32,32,128]{2,1,0:T(8,128)}), f32[32,32,128]{2,1,0:T(8,128)S(1)}, u32[]{:S(2)}, u32[]{:S(2)}) %all-to-all-start) | async-done | bytes 524320 | tf_op jit(solution)/shard_map/all_to_all | solution.py:339
  176.4 0.8 join.1
  (52 shorter events, 6.7 us)
Async XLA Ops:
  0.7 1.0 copy-start.1
  1.9 3.4 %copy-start.6 = (bf16[128,8,128]{2,1,0:T(8,128)(2,1)S(1)}, bf16[128,8,128]{2,1,0:T(8,128)(2,1)}, u32[]{:S(2)}) copy-start(bf16[128,8,128]{2,1,0:T(8,128)(2,1)} %param.10) | copy-start | bytes 786436
  1.9 8.6 %collective-permute-start = (f32[4,128,128]{2,1,0:T(8,128)S(1)}, f32[4,128,128]{2,1,0:T(8,128)S(1)}, u32[]{:S(2)}, u32[]{:S(2)}) collective-permute-start(f32[4,128,128]{2,1,0:T(8,128)S(1)} %open_near.1.near_ref.self_ref.other_ref.prior_ref), channel_id=1, source_target_pairs={{0,2},{4,6},{8,10},{12,14},{16,18},{20,22},{24,26},{28,30},{32,34}... | collective-permute-start | bytes 786440 | tf_op jit(solution)/shard_map/ppermute | solution.py:300
  4.3 1.6 copy-start.2
  4.3 9.6 %collective-permute-start.2 = (f32[4,128,128]{2,1,0:T(8,128)S(1)}, f32[4,128,128]{2,1,0:T(8,128)S(1)}, u32[]{:S(2)}, u32[]{:S(2)}) collective-permute-start(f32[4,128,128]{2,1,0:T(8,128)S(1)} %get-tuple-element.27.other_ref.self_ref.rest_1_), channel_id=1, source_target_pairs={{2,4},{6,8},{10,12},{14,16},{18,20},{22,24},{26,28},{30,32},{34,36... | collective-permute-start | bytes 786440 | tf_op jit(solution)/shard_map/ppermute | solution.py:301
  5.1 0.7 copy-start.7
  5.2 2.0 %collective-permute-start.1 = (f32[8,4,128]{2,1,0:T(4,128)S(1)}, f32[8,4,128]{2,1,0:T(4,128)S(1)}, u32[]{:S(2)}, u32[]{:S(2)}) collective-permute-start(f32[8,4,128]{2,1,0:T(4,128)S(1)} %get-tuple-element.28), channel_id=1, source_target_pairs={{0,1},{1,0},{2,3},{3,2},{4,5},{5,4},{6,7},{7,6},{8,9},{9,8},{10,11... | collective-permute-start | bytes 49160 | tf_op jit(solution)/shard_map/ppermute | solution.py:302
  5.8 0.7 copy-start.4
  5.8 0.7 copy-start.5
  11.1 8.7 %collective-permute-start.3 = (f32[4,128,128]{2,1,0:T(8,128)S(1)}, f32[4,128,128]{2,1,0:T(8,128)S(1)}, u32[]{:S(2)}, u32[]{:S(2)}) collective-permute-start(f32[4,128,128]{2,1,0:T(8,128)S(1)} %near0.1.rest_5_.near_ref.self_ref.other_ref.prior_ref), channel_id=1, source_target_pairs={{0,2},{4,6},{8,10},{12,14},{16,18},{20,22},{24,26},{28,30},{32,34}... | collective-permute-start | bytes 786440 | tf_op jit(solution)/shard_map/ppermute | solution.py:300
  14.0 10.0 %collective-permute-start.5 = (f32[4,128,128]{2,1,0:T(8,128)S(1)}, f32[4,128,128]{2,1,0:T(8,128)S(1)}, u32[]{:S(2)}, u32[]{:S(2)}) collective-permute-start(f32[4,128,128]{2,1,0:T(8,128)S(1)} %get-tuple-element.36.other_ref.self_ref.rest_1_), channel_id=1, source_target_pairs={{2,4},{6,8},{10,12},{14,16},{18,20},{22,24},{26,28},{30,32},{34,36... | collective-permute-start | bytes 786440 | tf_op jit(solution)/shard_map/ppermute | solution.py:301
  14.7 1.3 collective-permute-start.4
  20.5 9.6 %collective-permute-start.6 = (f32[4,128,128]{2,1,0:T(8,128)S(1)}, f32[4,128,128]{2,1,0:T(8,128)S(1)}, u32[]{:S(2)}, u32[]{:S(2)}) collective-permute-start(f32[4,128,128]{2,1,0:T(8,128)S(1)} %near1.1.rest_5_.near_ref.self_ref.other_ref.prior_ref), channel_id=1, source_target_pairs={{0,2},{4,6},{8,10},{12,14},{16,18},{20,22},{24,26},{28,30},{32,34}... | collective-permute-start | bytes 786440 | tf_op jit(solution)/shard_map/ppermute | solution.py:300
  24.0 10.3 %collective-permute-start.8 = (f32[4,128,128]{2,1,0:T(8,128)S(1)}, f32[4,128,128]{2,1,0:T(8,128)S(1)}, u32[]{:S(2)}, u32[]{:S(2)}) collective-permute-start(f32[4,128,128]{2,1,0:T(8,128)S(1)} %get-tuple-element.38.other_ref.self_ref.rest_1_), channel_id=1, source_target_pairs={{2,4},{6,8},{10,12},{14,16},{18,20},{22,24},{26,28},{30,32},{34,36... | collective-permute-start | bytes 786440 | tf_op jit(solution)/shard_map/ppermute | solution.py:301
  24.7 1.3 collective-permute-start.7
  30.7 9.8 %collective-permute-start.9 = (f32[4,128,128]{2,1,0:T(8,128)S(1)}, f32[4,128,128]{2,1,0:T(8,128)S(1)}, u32[]{:S(2)}, u32[]{:S(2)}) collective-permute-start(f32[4,128,128]{2,1,0:T(8,128)S(1)} %near2.1.rest_5_.near_ref.self_ref.other_ref.prior_ref), channel_id=1, source_target_pairs={{0,2},{4,6},{8,10},{12,14},{16,18},{20,22},{24,26},{28,30},{32,34}... | collective-permute-start | bytes 786440 | tf_op jit(solution)/shard_map/ppermute | solution.py:300
  34.4 10.1 %collective-permute-start.11 = (f32[4,128,128]{2,1,0:T(8,128)S(1)}, f32[4,128,128]{2,1,0:T(8,128)S(1)}, u32[]{:S(2)}, u32[]{:S(2)}) collective-permute-start(f32[4,128,128]{2,1,0:T(8,128)S(1)} %get-tuple-element.40.other_ref.self_ref.rest_1_), channel_id=1, source_target_pairs={{2,4},{6,8},{10,12},{14,16},{18,20},{22,24},{26,28},{30,32},{34,36... | collective-permute-start | bytes 786440 | tf_op jit(solution)/shard_map/ppermute | solution.py:301
  35.1 1.3 collective-permute-start.10
  41.0 9.6 %collective-permute-start.12 = (f32[4,128,128]{2,1,0:T(8,128)S(1)}, f32[4,128,128]{2,1,0:T(8,128)S(1)}, u32[]{:S(2)}, u32[]{:S(2)}) collective-permute-start(f32[4,128,128]{2,1,0:T(8,128)S(1)} %near3.1.rest_5_.near_ref.self_ref.other_ref.prior_ref), channel_id=1, source_target_pairs={{0,2},{4,6},{8,10},{12,14},{16,18},{20,22},{24,26},{28,30},{32,34}... | collective-permute-start | bytes 786440 | tf_op jit(solution)/shard_map/ppermute | solution.py:300
  44.6 10.2 %collective-permute-start.14 = (f32[4,128,128]{2,1,0:T(8,128)S(1)}, f32[4,128,128]{2,1,0:T(8,128)S(1)}, u32[]{:S(2)}, u32[]{:S(2)}) collective-permute-start(f32[4,128,128]{2,1,0:T(8,128)S(1)} %get-tuple-element.42.other_ref.self_ref.rest_1_), channel_id=1, source_target_pairs={{2,4},{6,8},{10,12},{14,16},{18,20},{22,24},{26,28},{30,32},{34,36... | collective-permute-start | bytes 786440 | tf_op jit(solution)/shard_map/ppermute | solution.py:301
  45.3 1.3 collective-permute-start.13
  51.2 9.7 %collective-permute-start.15 = (f32[4,128,128]{2,1,0:T(8,128)S(1)}, f32[4,128,128]{2,1,0:T(8,128)S(1)}, u32[]{:S(2)}, u32[]{:S(2)}) collective-permute-start(f32[4,128,128]{2,1,0:T(8,128)S(1)} %near4.1.rest_5_.near_ref.self_ref.other_ref.prior_ref), channel_id=1, source_target_pairs={{0,2},{4,6},{8,10},{12,14},{16,18},{20,22},{24,26},{28,30},{32,34}... | collective-permute-start | bytes 786440 | tf_op jit(solution)/shard_map/ppermute | solution.py:300
  54.8 9.8 %collective-permute-start.17 = (f32[4,128,128]{2,1,0:T(8,128)S(1)}, f32[4,128,128]{2,1,0:T(8,128)S(1)}, u32[]{:S(2)}, u32[]{:S(2)}) collective-permute-start(f32[4,128,128]{2,1,0:T(8,128)S(1)} %get-tuple-element.44.other_ref.self_ref.rest_1_), channel_id=1, source_target_pairs={{2,4},{6,8},{10,12},{14,16},{18,20},{22,24},{26,28},{30,32},{34,36... | collective-permute-start | bytes 786440 | tf_op jit(solution)/shard_map/ppermute | solution.py:301
  55.5 1.3 collective-permute-start.16
  61.5 9.3 %collective-permute-start.18 = (f32[4,128,128]{2,1,0:T(8,128)S(1)}, f32[4,128,128]{2,1,0:T(8,128)S(1)}, u32[]{:S(2)}, u32[]{:S(2)}) collective-permute-start(f32[4,128,128]{2,1,0:T(8,128)S(1)} %near5.1.rest_5_.near_ref.self_ref.other_ref.prior_ref), channel_id=1, source_target_pairs={{0,2},{4,6},{8,10},{12,14},{16,18},{20,22},{24,26},{28,30},{32,34}... | collective-permute-start | bytes 786440 | tf_op jit(solution)/shard_map/ppermute | solution.py:300
  64.8 10.0 %collective-permute-start.20 = (f32[4,128,128]{2,1,0:T(8,128)S(1)}, f32[4,128,128]{2,1,0:T(8,128)S(1)}, u32[]{:S(2)}, u32[]{:S(2)}) collective-permute-start(f32[4,128,128]{2,1,0:T(8,128)S(1)} %get-tuple-element.46.other_ref.self_ref.rest_1_), channel_id=1, source_target_pairs={{2,4},{6,8},{10,12},{14,16},{18,20},{22,24},{26,28},{30,32},{34,36... | collective-permute-start | bytes 786440 | tf_op jit(solution)/shard_map/ppermute | solution.py:301
  65.5 1.3 collective-permute-start.19
  71.4 9.5 %collective-permute-start.21 = (f32[4,128,128]{2,1,0:T(8,128)S(1)}, f32[4,128,128]{2,1,0:T(8,128)S(1)}, u32[]{:S(2)}, u32[]{:S(2)}) collective-permute-start(f32[4,128,128]{2,1,0:T(8,128)S(1)} %near6.1.rest_5_.near_ref.self_ref.other_ref), channel_id=1, source_target_pairs={{0,2},{4,6},{8,10},{12,14},{16,18},{20,22},{24,26},{28,30},{32,34}... | collective-permute-start | bytes 786440 | tf_op jit(solution)/shard_map/ppermute | solution.py:300
  74.9 7.5 %collective-permute-start.23 = (f32[4,128,128]{2,1,0:T(8,128)S(1)}, f32[4,128,128]{2,1,0:T(8,128)S(1)}, u32[]{:S(2)}, u32[]{:S(2)}) collective-permute-start(f32[4,128,128]{2,1,0:T(8,128)S(1)} %get-tuple-element.48.other_ref.self_ref), channel_id=1, source_target_pairs={{2,4},{6,8},{10,12},{14,16},{18,20},{22,24},{26,28},{30,32},{34,36... | collective-permute-start | bytes 786440 | tf_op jit(solution)/shard_map/ppermute | solution.py:301
  75.5 5.9 %copy-start = (f32[128,8,128]{2,1,0:T(8,128)S(1)}, f32[128,8,128]{2,1,0:T(8,128)}, u32[]{:S(2)}) copy-start(f32[128,8,128]{2,1,0:T(8,128)} %param.15) | copy-start | bytes 1572868
  75.6 1.3 collective-permute-start.22
  80.9 0.7 copy-start.3
  83.4 93.0 %all-to-all-start = ((f32[32,32,128]{2,1,0:T(8,128)}), f32[32,32,128]{2,1,0:T(8,128)S(1)}, u32[]{:S(2)}, u32[]{:S(2)}) async-start(f32[32,32,128]{2,1,0:T(8,128)} %bitcast.5), calls=%async_computation | async-start | bytes 1048576 | tf_op jit(solution)/shard_map/all_to_all | solution.py:339

commit v6 on v5

--- a/solution.py
+++ b/solution.py
@@ -6,6 +6,7 @@
 from jax.experimental import pallas as pl
 from jax.experimental.pallas import tpu as pltpu
 from jax.sharding import PartitionSpec as P
+
 
 STEPS = 8
 
@@ -266,7 +267,7 @@
     square = jax.ShapeDtypeStruct((length, length), F32)
     wave = jnp.broadcast_to(wavelet[:, None], (wavelet.shape[0], length))
 
-    def kernel(body, outs, inputs, scratch=(), name=None):
+    def kernel(body, outs, inputs, scratch=()):
         return pl.pallas_call(
             body,
             out_shape=outs,
@@ -274,12 +275,11 @@
             out_specs=jax.tree.map(lambda _: VM, outs),
             scratch_shapes=list(scratch),
             compiler_params=PARAMS,
-            name=name,
         )(*inputs)
 
     start = pressure.reshape(flat)
-    near = kernel(open_near_kernel, half, (sides, start), name="open_near")
-    far, edge = kernel(open_far_kernel, (half, rims), (sides, start, near), name="open_far")
+    near = kernel(open_near_kernel, half, (sides, start))
+    far, edge = kernel(open_far_kernel, (half, rims), (sides, start, near))
     near_prior, far_prior, near_coef, far_coef, near_mark, far_mark, amp = kernel(
         tables_kernel,
         (half,) * 6 + (square,),
@@ -291,58 +291,45 @@
             delay_steps,
             source_depth,
         ),
-        name="tables",
     )
     scratch = (pltpu.VMEM((REACH, length + 16, depth), F32), pltpu.VMEM((REACH * length, depth), F32))
     pad = (pltpu.VMEM((depth + 16, length), F32),)
     receiver = receiver_field.reshape(flat)
     for step in range(STEPS):
         near_halo = lax.ppermute(near, "gx", near_pairs)
+        edge_in = lax.ppermute(edge, "gy", rim_pairs)
         far_halo = lax.ppermute(far, "gx", far_pairs)
-        edge_in = lax.ppermute(edge, "gy", rim_pairs)
         near_next = kernel(
             functools.partial(advance_kernel, step, 0),
             half,
             (sides, near, far, near_halo, edge_in, near_prior, near_coef, near_mark, amp),
             scratch,
-            f"near{step}",
         )
         base = kernel(
             functools.partial(inner_kernel, step, 1),
             half,
             (sides, far, near, edge_in, far_prior, far_coef, far_mark, amp, near_next),
             scratch,
-            f"inner{step}",
         )
         if step < STEPS - 1:
-            far_next, edge = kernel(
-                outer_kernel, (half, rims), (sides, base, far_coef, far_halo, near_next), name=f"far{step}"
-            )
+            far_next, edge = kernel(outer_kernel, (half, rims), (sides, base, far_coef, far_halo, near_next))
         else:
             part = kernel(
                 image_near_kernel,
                 jax.ShapeDtypeStruct((depth * REACH, length), F32),
                 (sides, near_next, receiver, receiver_depth),
                 pad,
-                "image_near",
             )
             far_next, filtered = kernel(
-                last_kernel,
-                (half, whole),
-                (sides, base, far_coef, far_halo, receiver, receiver_depth, part),
-                pad,
-                f"far{step}",
+                last_kernel, (half, whole), (sides, base, far_coef, far_halo, receiver, receiver_depth, part), pad
             )
         near_prior, far_prior = near, far
         near, far = near_next, far_next
     levels = depth // size
     parts = lax.all_to_all(filtered, "gx", split_axis=0, concat_axis=0, tiled=True)
-    final = kernel(final_kernel, whole, (sides, near, far), name="final")
+    final = kernel(final_kernel, whole, (sides, near, far))
     image = kernel(
-        functools.partial(join_kernel, levels),
-        jax.ShapeDtypeStruct((levels, size * width, length), F32),
-        (parts,),
-        name="join",
+        functools.partial(join_kernel, levels), jax.ShapeDtypeStruct((levels, size * width, length), F32), (parts,)
     )
     return final.reshape(depth, width, length), image
 

time: 178 us -> 178 us (level)
  no operation moved by 1% of the time
where the time goes in v6:
time: 178 us; the launch traced here: 177 us
  waiting for transfers between devices  99.1 us (56%)
  starting transfers between devices  61.2 us (34%)
  Pallas kernels  13.5 us (8%)
  local copies, waits for them, and re-layouts  2.36 us (1%)
    all_to_all x1, waiting for transfers between devices, shards(): lax.all_to_all(filtered, 'gx', split_axis=0, concat_axis=0, tiled=True)  59.5 us
    all_to_all x1, starting transfers between devices, shards(): lax.all_to_all(filtered, 'gx', split_axis=0, concat_axis=0, tiled=True)  32.5 us
    ppermute x8, waiting for transfers between devices, shards(): near_halo = lax.ppermute(near, 'gx', near_pairs)  31.5 us
    ppermute x8, starting transfers between devices, shards(): near_halo = lax.ppermute(near, 'gx', near_pairs)  22 us
    pallas_call x30, Pallas kernels, kernel(): pl.pallas_call(body, out_shape=outs, in_specs=[VM] * len(inputs), out_spe...  13.5 us
    ppermute x8, waiting for transfers between devices, shards(): edge_in = lax.ppermute(edge, 'gy', rim_pairs)  8.1 us
    ppermute x8, starting transfers between devices, shards(): far_halo = lax.ppermute(far, 'gx', far_pairs)  5.55 us
  transfers between devices with their start and end apart: 25, of which 16 were waited for; matrix products, arithmetic and copies ran while one was open for 0% of the time, Pallas kernels for 6%

profile of v6, /device:TPU:46, one launch (start us, length us, event | category | flops | bytes accessed | tf_op | source)
XLA Modules:
  0.0 177.3 jit_solution(8302164434633912502)
XLA Ops:
  0.7 1.0 copy-done.1
  1.9 2.2 %collective-permute-start = (f32[4,128,128]{2,1,0:T(8,128)S(1)}, f32[4,128,128]{2,1,0:T(8,128)S(1)}, u32[]{:S(2)}, u32[]{:S(2)}) collective-permute-start(f32[4,128,128]{2,1,0:T(8,128)S(1)} %shard_map.95.near_ref.self_ref.other_ref.prior_ref), channel_id=1, source_target_pairs={{0,2},{4,6},{8,10},{12,14},{16,18},{20,22},{24,26},{28,30},{32,34}... | collective-permute-start | bytes 786440 | tf_op jit(solution)/shard_map/ppermute | solution.py:299
  4.3 0.8 collective-permute-start.2
  5.9 0.6 copy-done.4
  6.5 0.6 shard_map.97
  7.1 3.4 %collective-permute-done.halo_ref = f32[4,128,128]{2,1,0:T(8,128)S(1)} collective-permute-done((f32[4,128,128]{2,1,0:T(8,128)S(1)}, f32[4,128,128]{2,1,0:T(8,128)S(1)}, u32[]{:S(2)}, u32[]{:S(2)}) %collective-permute-start) | collective-permute-done | bytes 262176 | tf_op jit(solution)/shard_map/ppermute | solution.py:299
  10.6 0.6 shard_map.98.rest_5_.near_ref.self_ref.other_ref.prior_ref
  11.1 2.2 %collective-permute-start.3 = (f32[4,128,128]{2,1,0:T(8,128)S(1)}, f32[4,128,128]{2,1,0:T(8,128)S(1)}, u32[]{:S(2)}, u32[]{:S(2)}) collective-permute-start(f32[4,128,128]{2,1,0:T(8,128)S(1)} %shard_map.98.rest_5_.near_ref.self_ref.other_ref.prior_ref), channel_id=1, source_target_pairs={{0,2},{4,6},{8,10},{12,14},{16,18},{20,22},{24,26},{28,30},{32,34}... | collective-permute-start | bytes 786440 | tf_op jit(solution)/shard_map/ppermute | solution.py:299
  14.0 0.7 collective-permute-start.5
  14.8 1.2 collective-permute-done.4.rim_in_ref.rest_0_
  16.0 3.9 %collective-permute-done.3.halo_ref = f32[4,128,128]{2,1,0:T(8,128)S(1)} collective-permute-done((f32[4,128,128]{2,1,0:T(8,128)S(1)}, f32[4,128,128]{2,1,0:T(8,128)S(1)}, u32[]{:S(2)}, u32[]{:S(2)}) %collective-permute-start.3) | collective-permute-done | bytes 262176 | tf_op jit(solution)/shard_map/ppermute | solution.py:299
  19.9 0.6 shard_map.101.rest_5_.near_ref.self_ref.other_ref.prior_ref
  20.5 2.9 %collective-permute-start.6 = (f32[4,128,128]{2,1,0:T(8,128)S(1)}, f32[4,128,128]{2,1,0:T(8,128)S(1)}, u32[]{:S(2)}, u32[]{:S(2)}) collective-permute-start(f32[4,128,128]{2,1,0:T(8,128)S(1)} %shard_map.101.rest_5_.near_ref.self_ref.other_ref.prior_ref), channel_id=1, source_target_pairs={{0,2},{4,6},{8,10},{12,14},{16,18},{20,22},{24,26},{28,30},{32,34}... | collective-permute-start | bytes 786440 | tf_op jit(solution)/shard_map/ppermute | solution.py:299
  24.0 0.7 collective-permute-start.8
  24.9 1.2 collective-permute-done.7.rim_in_ref.rest_0_
  26.0 4.0 %collective-permute-done.6.halo_ref = f32[4,128,128]{2,1,0:T(8,128)S(1)} collective-permute-done((f32[4,128,128]{2,1,0:T(8,128)S(1)}, f32[4,128,128]{2,1,0:T(8,128)S(1)}, u32[]{:S(2)}, u32[]{:S(2)}) %collective-permute-start.6) | collective-permute-done | bytes 262176 | tf_op jit(solution)/shard_map/ppermute | solution.py:299
  30.1 0.6 shard_map.104.rest_5_.near_ref.self_ref.other_ref.prior_ref
  30.7 3.1 %collective-permute-start.9 = (f32[4,128,128]{2,1,0:T(8,128)S(1)}, f32[4,128,128]{2,1,0:T(8,128)S(1)}, u32[]{:S(2)}, u32[]{:S(2)}) collective-permute-start(f32[4,128,128]{2,1,0:T(8,128)S(1)} %shard_map.104.rest_5_.near_ref.self_ref.other_ref.prior_ref), channel_id=1, source_target_pairs={{0,2},{4,6},{8,10},{12,14},{16,18},{20,22},{24,26},{28,30},{32,34}... | collective-permute-start | bytes 786440 | tf_op jit(solution)/shard_map/ppermute | solution.py:299
  34.4 0.7 collective-permute-start.11
  35.2 1.2 collective-permute-done.10.rim_in_ref.rest_0_
  36.4 4.0 %collective-permute-done.9.halo_ref = f32[4,128,128]{2,1,0:T(8,128)S(1)} collective-permute-done((f32[4,128,128]{2,1,0:T(8,128)S(1)}, f32[4,128,128]{2,1,0:T(8,128)S(1)}, u32[]{:S(2)}, u32[]{:S(2)}) %collective-permute-start.9) | collective-permute-done | bytes 262176 | tf_op jit(solution)/shard_map/ppermute | solution.py:299
  40.4 0.6 shard_map.107.rest_5_.near_ref.self_ref.other_ref.prior_ref
  41.0 2.9 %collective-permute-start.12 = (f32[4,128,128]{2,1,0:T(8,128)S(1)}, f32[4,128,128]{2,1,0:T(8,128)S(1)}, u32[]{:S(2)}, u32[]{:S(2)}) collective-permute-start(f32[4,128,128]{2,1,0:T(8,128)S(1)} %shard_map.107.rest_5_.near_ref.self_ref.other_ref.prior_ref), channel_id=1, source_target_pairs={{0,2},{4,6},{8,10},{12,14},{16,18},{20,22},{24,26},{28,30},{32,34}... | collective-permute-start | bytes 786440 | tf_op jit(solution)/shard_map/ppermute | solution.py:299
  44.6 0.7 collective-permute-start.14
  45.4 1.2 collective-permute-done.13.rim_in_ref.rest_0_
  46.6 4.0 %collective-permute-done.12.halo_ref = f32[4,128,128]{2,1,0:T(8,128)S(1)} collective-permute-done((f32[4,128,128]{2,1,0:T(8,128)S(1)}, f32[4,128,128]{2,1,0:T(8,128)S(1)}, u32[]{:S(2)}, u32[]{:S(2)}) %collective-permute-start.12) | collective-permute-done | bytes 262176 | tf_op jit(solution)/shard_map/ppermute | solution.py:299
  50.6 0.6 shard_map.110.rest_5_.near_ref.self_ref.other_ref.prior_ref
  51.2 3.0 %collective-permute-start.15 = (f32[4,128,128]{2,1,0:T(8,128)S(1)}, f32[4,128,128]{2,1,0:T(8,128)S(1)}, u32[]{:S(2)}, u32[]{:S(2)}) collective-permute-start(f32[4,128,128]{2,1,0:T(8,128)S(1)} %shard_map.110.rest_5_.near_ref.self_ref.other_ref.prior_ref), channel_id=1, source_target_pairs={{0,2},{4,6},{8,10},{12,14},{16,18},{20,22},{24,26},{28,30},{32,34}... | collective-permute-start | bytes 786440 | tf_op jit(solution)/shard_map/ppermute | solution.py:299
  54.8 0.7 collective-permute-start.17
  55.7 1.2 collective-permute-done.16.rim_in_ref.rest_0_
  56.8 4.0 %collective-permute-done.15.halo_ref = f32[4,128,128]{2,1,0:T(8,128)S(1)} collective-permute-done((f32[4,128,128]{2,1,0:T(8,128)S(1)}, f32[4,128,128]{2,1,0:T(8,128)S(1)}, u32[]{:S(2)}, u32[]{:S(2)}) %collective-permute-start.15) | collective-permute-done | bytes 262176 | tf_op jit(solution)/shard_map/ppermute | solution.py:299
  60.9 0.6 shard_map.113.rest_5_.near_ref.self_ref.other_ref.prior_ref
  61.5 2.7 %collective-permute-start.18 = (f32[4,128,128]{2,1,0:T(8,128)S(1)}, f32[4,128,128]{2,1,0:T(8,128)S(1)}, u32[]{:S(2)}, u32[]{:S(2)}) collective-permute-start(f32[4,128,128]{2,1,0:T(8,128)S(1)} %shard_map.113.rest_5_.near_ref.self_ref.other_ref.prior_ref), channel_id=1, source_target_pairs={{0,2},{4,6},{8,10},{12,14},{16,18},{20,22},{24,26},{28,30},{32,34}... | collective-permute-start | bytes 786440 | tf_op jit(solution)/shard_map/ppermute | solution.py:299
  64.8 0.7 collective-permute-start.20
  65.6 1.2 collective-permute-done.19.rim_in_ref.rest_0_
  66.8 4.0 %collective-permute-done.18.halo_ref = f32[4,128,128]{2,1,0:T(8,128)S(1)} collective-permute-done((f32[4,128,128]{2,1,0:T(8,128)S(1)}, f32[4,128,128]{2,1,0:T(8,128)S(1)}, u32[]{:S(2)}, u32[]{:S(2)}) %collective-permute-start.18) | collective-permute-done | bytes 262176 | tf_op jit(solution)/shard_map/ppermute | solution.py:299
  70.8 0.6 shard_map.116.rest_5_.near_ref.self_ref.other_ref
  71.4 2.8 %collective-permute-start.21 = (f32[4,128,128]{2,1,0:T(8,128)S(1)}, f32[4,128,128]{2,1,0:T(8,128)S(1)}, u32[]{:S(2)}, u32[]{:S(2)}) collective-permute-start(f32[4,128,128]{2,1,0:T(8,128)S(1)} %shard_map.116.rest_5_.near_ref.self_ref.other_ref), channel_id=1, source_target_pairs={{0,2},{4,6},{8,10},{12,14},{16,18},{20,22},{24,26},{28,30},{32,34}... | collective-permute-start | bytes 786440 | tf_op jit(solution)/shard_map/ppermute | solution.py:299
  74.9 0.7 collective-permute-start.23
  75.7 1.2 collective-permute-done.22.rim_in_ref.rest_0_
  76.9 4.0 %collective-permute-done.21.halo_ref = f32[4,128,128]{2,1,0:T(8,128)S(1)} collective-permute-done((f32[4,128,128]{2,1,0:T(8,128)S(1)}, f32[4,128,128]{2,1,0:T(8,128)S(1)}, u32[]{:S(2)}, u32[]{:S(2)}) %collective-permute-start.21) | collective-permute-done | bytes 262176 | tf_op jit(solution)/shard_map/ppermute | solution.py:299
  80.9 0.6 shard_map.119.rest_5_.near_ref
  81.8 0.5 shard_map.120.base_ref
  82.3 1.1 shard_map.122
  83.4 32.5 %all-to-all-start = ((f32[32,32,128]{2,1,0:T(8,128)}), f32[32,32,128]{2,1,0:T(8,128)S(1)}, u32[]{:S(2)}, u32[]{:S(2)}) async-start(f32[32,32,128]{2,1,0:T(8,128)} %bitcast.5), calls=%async_computation | async-start | bytes 1048576 | tf_op jit(solution)/shard_map/all_to_all | solution.py:329
  115.9 1.0 shard_map.123
  116.9 59.5 %all-to-all-done = f32[32,32,128]{2,1,0:T(8,128)S(1)} async-done(((f32[32,32,128]{2,1,0:T(8,128)}), f32[32,32,128]{2,1,0:T(8,128)S(1)}, u32[]{:S(2)}, u32[]{:S(2)}) %all-to-all-start) | async-done | bytes 524320 | tf_op jit(solution)/shard_map/all_to_all | solution.py:329
  176.4 0.8 shard_map.124
  (52 shorter events, 6.7 us)
Async XLA Ops:
  0.7 1.0 copy-start.1
  1.9 3.4 %copy-start.6 = (bf16[128,8,128]{2,1,0:T(8,128)(2,1)S(1)}, bf16[128,8,128]{2,1,0:T(8,128)(2,1)}, u32[]{:S(2)}) copy-start(bf16[128,8,128]{2,1,0:T(8,128)(2,1)} %param.10) | copy-start | bytes 786436
  1.9 8.6 %collective-permute-start = (f32[4,128,128]{2,1,0:T(8,128)S(1)}, f32[4,128,128]{2,1,0:T(8,128)S(1)}, u32[]{:S(2)}, u32[]{:S(2)}) collective-permute-start(f32[4,128,128]{2,1,0:T(8,128)S(1)} %shard_map.95.near_ref.self_ref.other_ref.prior_ref), channel_id=1, source_target_pairs={{0,2},{4,6},{8,10},{12,14},{16,18},{20,22},{24,26},{28,30},{32,34}... | collective-permute-start | bytes 786440 | tf_op jit(solution)/shard_map/ppermute | solution.py:299
  4.3 1.6 copy-start.2
  4.3 9.6 %collective-permute-start.2 = (f32[4,128,128]{2,1,0:T(8,128)S(1)}, f32[4,128,128]{2,1,0:T(8,128)S(1)}, u32[]{:S(2)}, u32[]{:S(2)}) collective-permute-start(f32[4,128,128]{2,1,0:T(8,128)S(1)} %get-tuple-element.27.other_ref.self_ref.rest_1_), channel_id=1, source_target_pairs={{2,4},{6,8},{10,12},{14,16},{18,20},{22,24},{26,28},{30,32},{34,36... | collective-permute-start | bytes 786440 | tf_op jit(solution)/shard_map/ppermute | solution.py:301
  5.1 0.7 copy-start.7
  5.2 2.0 %collective-permute-start.1 = (f32[8,4,128]{2,1,0:T(4,128)S(1)}, f32[8,4,128]{2,1,0:T(4,128)S(1)}, u32[]{:S(2)}, u32[]{:S(2)}) collective-permute-start(f32[8,4,128]{2,1,0:T(4,128)S(1)} %get-tuple-element.28), channel_id=1, source_target_pairs={{0,1},{1,0},{2,3},{3,2},{4,5},{5,4},{6,7},{7,6},{8,9},{9,8},{10,11... | collective-permute-start | bytes 49160 | tf_op jit(solution)/shard_map/ppermute | solution.py:300
  5.8 0.7 copy-start.4
  5.8 0.7 copy-start.5
  11.1 8.7 %collective-permute-start.3 = (f32[4,128,128]{2,1,0:T(8,128)S(1)}, f32[4,128,128]{2,1,0:T(8,128)S(1)}, u32[]{:S(2)}, u32[]{:S(2)}) collective-permute-start(f32[4,128,128]{2,1,0:T(8,128)S(1)} %shard_map.98.rest_5_.near_ref.self_ref.other_ref.prior_ref), channel_id=1, source_target_pairs={{0,2},{4,6},{8,10},{12,14},{16,18},{20,22},{24,26},{28,30},{32,34}... | collective-permute-start | bytes 786440 | tf_op jit(solution)/shard_map/ppermute | solution.py:299
  14.0 10.0 %collective-permute-start.5 = (f32[4,128,128]{2,1,0:T(8,128)S(1)}, f32[4,128,128]{2,1,0:T(8,128)S(1)}, u32[]{:S(2)}, u32[]{:S(2)}) collective-permute-start(f32[4,128,128]{2,1,0:T(8,128)S(1)} %get-tuple-element.36.other_ref.self_ref.rest_1_), channel_id=1, source_target_pairs={{2,4},{6,8},{10,12},{14,16},{18,20},{22,24},{26,28},{30,32},{34,36... | collective-permute-start | bytes 786440 | tf_op jit(solution)/shard_map/ppermute | solution.py:301
  14.7 1.3 collective-permute-start.4
  20.5 9.6 %collective-permute-start.6 = (f32[4,128,128]{2,1,0:T(8,128)S(1)}, f32[4,128,128]{2,1,0:T(8,128)S(1)}, u32[]{:S(2)}, u32[]{:S(2)}) collective-permute-start(f32[4,128,128]{2,1,0:T(8,128)S(1)} %shard_map.101.rest_5_.near_ref.self_ref.other_ref.prior_ref), channel_id=1, source_target_pairs={{0,2},{4,6},{8,10},{12,14},{16,18},{20,22},{24,26},{28,30},{32,34}... | collective-permute-start | bytes 786440 | tf_op jit(solution)/shard_map/ppermute | solution.py:299
  24.0 10.3 %collective-permute-start.8 = (f32[4,128,128]{2,1,0:T(8,128)S(1)}, f32[4,128,128]{2,1,0:T(8,128)S(1)}, u32[]{:S(2)}, u32[]{:S(2)}) collective-permute-start(f32[4,128,128]{2,1,0:T(8,128)S(1)} %get-tuple-element.38.other_ref.self_ref.rest_1_), channel_id=1, source_target_pairs={{2,4},{6,8},{10,12},{14,16},{18,20},{22,24},{26,28},{30,32},{34,36... | collective-permute-start | bytes 786440 | tf_op jit(solution)/shard_map/ppermute | solution.py:301
  24.7 1.3 collective-permute-start.7
  30.7 9.8 %collective-permute-start.9 = (f32[4,128,128]{2,1,0:T(8,128)S(1)}, f32[4,128,128]{2,1,0:T(8,128)S(1)}, u32[]{:S(2)}, u32[]{:S(2)}) collective-permute-start(f32[4,128,128]{2,1,0:T(8,128)S(1)} %shard_map.104.rest_5_.near_ref.self_ref.other_ref.prior_ref), channel_id=1, source_target_pairs={{0,2},{4,6},{8,10},{12,14},{16,18},{20,22},{24,26},{28,30},{32,34}... | collective-permute-start | bytes 786440 | tf_op jit(solution)/shard_map/ppermute | solution.py:299
  34.4 10.1 %collective-permute-start.11 = (f32[4,128,128]{2,1,0:T(8,128)S(1)}, f32[4,128,128]{2,1,0:T(8,128)S(1)}, u32[]{:S(2)}, u32[]{:S(2)}) collective-permute-start(f32[4,128,128]{2,1,0:T(8,128)S(1)} %get-tuple-element.40.other_ref.self_ref.rest_1_), channel_id=1, source_target_pairs={{2,4},{6,8},{10,12},{14,16},{18,20},{22,24},{26,28},{30,32},{34,36... | collective-permute-start | bytes 786440 | tf_op jit(solution)/shard_map/ppermute | solution.py:301
  35.1 1.3 collective-permute-start.10
  41.0 9.6 %collective-permute-start.12 = (f32[4,128,128]{2,1,0:T(8,128)S(1)}, f32[4,128,128]{2,1,0:T(8,128)S(1)}, u32[]{:S(2)}, u32[]{:S(2)}) collective-permute-start(f32[4,128,128]{2,1,0:T(8,128)S(1)} %shard_map.107.rest_5_.near_ref.self_ref.other_ref.prior_ref), channel_id=1, source_target_pairs={{0,2},{4,6},{8,10},{12,14},{16,18},{20,22},{24,26},{28,30},{32,34}... | collective-permute-start | bytes 786440 | tf_op jit(solution)/shard_map/ppermute | solution.py:299
  44.6 10.2 %collective-permute-start.14 = (f32[4,128,128]{2,1,0:T(8,128)S(1)}, f32[4,128,128]{2,1,0:T(8,128)S(1)}, u32[]{:S(2)}, u32[]{:S(2)}) collective-permute-start(f32[4,128,128]{2,1,0:T(8,128)S(1)} %get-tuple-element.42.other_ref.self_ref.rest_1_), channel_id=1, source_target_pairs={{2,4},{6,8},{10,12},{14,16},{18,20},{22,24},{26,28},{30,32},{34,36... | collective-permute-start | bytes 786440 | tf_op jit(solution)/shard_map/ppermute | solution.py:301
  45.3 1.3 collective-permute-start.13
  51.2 9.7 %collective-permute-start.15 = (f32[4,128,128]{2,1,0:T(8,128)S(1)}, f32[4,128,128]{2,1,0:T(8,128)S(1)}, u32[]{:S(2)}, u32[]{:S(2)}) collective-permute-start(f32[4,128,128]{2,1,0:T(8,128)S(1)} %shard_map.110.rest_5_.near_ref.self_ref.other_ref.prior_ref), channel_id=1, source_target_pairs={{0,2},{4,6},{8,10},{12,14},{16,18},{20,22},{24,26},{28,30},{32,34}... | collective-permute-start | bytes 786440 | tf_op jit(solution)/shard_map/ppermute | solution.py:299
  54.8 9.8 %collective-permute-start.17 = (f32[4,128,128]{2,1,0:T(8,128)S(1)}, f32[4,128,128]{2,1,0:T(8,128)S(1)}, u32[]{:S(2)}, u32[]{:S(2)}) collective-permute-start(f32[4,128,128]{2,1,0:T(8,128)S(1)} %get-tuple-element.44.other_ref.self_ref.rest_1_), channel_id=1, source_target_pairs={{2,4},{6,8},{10,12},{14,16},{18,20},{22,24},{26,28},{30,32},{34,36... | collective-permute-start | bytes 786440 | tf_op jit(solution)/shard_map/ppermute | solution.py:301
  55.5 1.3 collective-permute-start.16
  61.5 9.3 %collective-permute-start.18 = (f32[4,128,128]{2,1,0:T(8,128)S(1)}, f32[4,128,128]{2,1,0:T(8,128)S(1)}, u32[]{:S(2)}, u32[]{:S(2)}) collective-permute-start(f32[4,128,128]{2,1,0:T(8,128)S(1)} %shard_map.113.rest_5_.near_ref.self_ref.other_ref.prior_ref), channel_id=1, source_target_pairs={{0,2},{4,6},{8,10},{12,14},{16,18},{20,22},{24,26},{28,30},{32,34}... | collective-permute-start | bytes 786440 | tf_op jit(solution)/shard_map/ppermute | solution.py:299
  64.8 10.0 %collective-permute-start.20 = (f32[4,128,128]{2,1,0:T(8,128)S(1)}, f32[4,128,128]{2,1,0:T(8,128)S(1)}, u32[]{:S(2)}, u32[]{:S(2)}) collective-permute-start(f32[4,128,128]{2,1,0:T(8,128)S(1)} %get-tuple-element.46.other_ref.self_ref.rest_1_), channel_id=1, source_target_pairs={{2,4},{6,8},{10,12},{14,16},{18,20},{22,24},{26,28},{30,32},{34,36... | collective-permute-start | bytes 786440 | tf_op jit(solution)/shard_map/ppermute | solution.py:301
  65.5 1.3 collective-permute-start.19
  71.4 9.5 %collective-permute-start.21 = (f32[4,128,128]{2,1,0:T(8,128)S(1)}, f32[4,128,128]{2,1,0:T(8,128)S(1)}, u32[]{:S(2)}, u32[]{:S(2)}) collective-permute-start(f32[4,128,128]{2,1,0:T(8,128)S(1)} %shard_map.116.rest_5_.near_ref.self_ref.other_ref), channel_id=1, source_target_pairs={{0,2},{4,6},{8,10},{12,14},{16,18},{20,22},{24,26},{28,30},{32,34}... | collective-permute-start | bytes 786440 | tf_op jit(solution)/shard_map/ppermute | solution.py:299
  74.9 7.5 %collective-permute-start.23 = (f32[4,128,128]{2,1,0:T(8,128)S(1)}, f32[4,128,128]{2,1,0:T(8,128)S(1)}, u32[]{:S(2)}, u32[]{:S(2)}) collective-permute-start(f32[4,128,128]{2,1,0:T(8,128)S(1)} %get-tuple-element.48.other_ref.self_ref), channel_id=1, source_target_pairs={{2,4},{6,8},{10,12},{14,16},{18,20},{22,24},{26,28},{30,32},{34,36... | collective-permute-start | bytes 786440 | tf_op jit(solution)/shard_map/ppermute | solution.py:301
  75.5 5.9 %copy-start = (f32[128,8,128]{2,1,0:T(8,128)S(1)}, f32[128,8,128]{2,1,0:T(8,128)}, u32[]{:S(2)}) copy-start(f32[128,8,128]{2,1,0:T(8,128)} %param.15) | copy-start | bytes 1572868
  75.6 1.3 collective-permute-start.22
  80.9 0.7 copy-start.3
  83.4 93.0 %all-to-all-start = ((f32[32,32,128]{2,1,0:T(8,128)}), f32[32,32,128]{2,1,0:T(8,128)S(1)}, u32[]{:S(2)}, u32[]{:S(2)}) async-start(f32[32,32,128]{2,1,0:T(8,128)} %bitcast.5), calls=%async_computation | async-start | bytes 1048576 | tf_op jit(solution)/shard_map/all_to_all | solution.py:329

commit v7 on v5

--- a/solution.py
+++ b/solution.py
@@ -215,7 +215,7 @@
         image_ref[pl.ds(j, depth, stride=width), :] = part_ref[pl.ds(j, depth, stride=REACH), :]
 
 
-def final_kernel(sides_ref, near_ref, far_ref, p_ref):
+def close_kernel(levels, sides_ref, parts_ref, near_ref, far_ref, p_ref, image_ref):
     odd = sides_ref[0:1, :]
     width = 2 * REACH
     depth = p_ref.shape[0] // width
@@ -223,10 +223,6 @@
         near, far = near_ref[i], far_ref[i]
         p_ref[pl.ds(REACH + i, depth, stride=width), :] = choose(odd, near.shape, far, near).T
         p_ref[pl.ds(REACH - 1 - i, depth, stride=width), :] = choose(odd, near.shape, near, far).T
-
-
-def join_kernel(levels, parts_ref, image_ref):
-    width = 2 * REACH
     for source in range(parts_ref.shape[0] // (levels * width)):
         for z in range(levels):
             at = (source * levels + z) * width
@@ -337,12 +333,11 @@
         near, far = near_next, far_next
     levels = depth // size
     parts = lax.all_to_all(filtered, "gx", split_axis=0, concat_axis=0, tiled=True)
-    final = kernel(final_kernel, whole, (sides, near, far), name="final")
-    image = kernel(
-        functools.partial(join_kernel, levels),
-        jax.ShapeDtypeStruct((levels, size * width, length), F32),
-        (parts,),
-        name="join",
+    final, image = kernel(
+        functools.partial(close_kernel, levels),
+        (whole, jax.ShapeDtypeStruct((levels, size * width, length), F32)),
+        (sides, parts, near, far),
+        name="close",
     )
     return final.reshape(depth, width, length), image
 

time: 178 us -> 177 us (level)
  blocking collectives: 0 us -> 92.8 us
  waiting for transfers between devices: 99.1 us -> 39.6 us
  starting transfers between devices: 61.2 us -> 28.7 us
    all_to_all x0 -> x1, blocking collectives: none -> 92.8 us  [shards(): lax.all_to_all(filtered, 'gx', split_axis=0, concat_axis=0, tiled=True)]
    all_to_all x1 -> x0, waiting for transfers between devices: 59.5 us -> none  [shards(): lax.all_to_all(filtered, 'gx', split_axis=0, concat_axis=0, tiled=True)]
    all_to_all x1 -> x0, starting transfers between devices: 32.5 us -> none  [shards(): lax.all_to_all(filtered, 'gx', split_axis=0, concat_axis=0, tiled=True)]
    pallas_call x30 -> x29, Pallas kernels: 13.5 us -> 12.1 us  [kernel(): pl.pallas_call(body, out_shape=outs, in_specs=[VM] * len(inputs), out_spe...]
  transfers between devices with their start and end apart: 25 -> 24, of which waited for: 16 -> 15; matrix products, arithmetic and copies ran while one was open for 0% -> 0% of each run, Pallas kernels for 6% -> 6%
where the time goes in v7:
time: 177 us
  blocking collectives  92.8 us (52%)
  waiting for transfers between devices  39.6 us (22%)
  starting transfers between devices  28.7 us (16%)
  Pallas kernels  12.1 us (7%)
  local copies, waits for them, and re-layouts  2.36 us (1%)
    all_to_all x1, blocking collectives, shards(): lax.all_to_all(filtered, 'gx', split_axis=0, concat_axis=0, tiled=True)  92.8 us
    ppermute x8, waiting for transfers between devices, shards(): near_halo = lax.ppermute(near, 'gx', near_pairs)  31.5 us
    ppermute x8, starting transfers between devices, shards(): near_halo = lax.ppermute(near, 'gx', near_pairs)  22 us
    pallas_call x29, Pallas kernels, kernel(): pl.pallas_call(body, out_shape=outs, in_specs=[VM] * len(inputs), out_spe...  12.1 us
    ppermute x8, waiting for transfers between devices, shards(): edge_in = lax.ppermute(edge, 'gy', rim_pairs)  8.1 us
    ppermute x8, starting transfers between devices, shards(): far_halo = lax.ppermute(far, 'gx', far_pairs)  5.55 us
  transfers between devices with their start and end apart: 24, of which 15 were waited for; matrix products, arithmetic and copies ran while one was open for 0% of the time, Pallas kernels for 6%

profile of v7, /device:TPU:46, one launch (start us, length us, event | category | flops | bytes accessed | tf_op | source)
XLA Modules:
  0.0 176.6 jit_solution(9878063584253115867)
XLA Ops:
  0.7 1.0 copy-done.1
  1.9 2.2 %collective-permute-start.1 = (f32[4,128,128]{2,1,0:T(8,128)S(1)}, f32[4,128,128]{2,1,0:T(8,128)S(1)}, u32[]{:S(2)}, u32[]{:S(2)}) collective-permute-start(f32[4,128,128]{2,1,0:T(8,128)S(1)} %open_near.1.near_ref.self_ref.other_ref.prior_ref), channel_id=1, source_target_pairs={{0,2},{4,6},{8,10},{12,14},{16,18},{20,22},{24,26},{28,30},{32,34}... | collective-permute-start | bytes 786440 | tf_op jit(solution)/shard_map/ppermute | solution.py:296
  4.3 0.8 collective-permute-start.2
  5.9 0.6 copy-done.4
  6.5 0.6 tables.1
  7.1 3.4 %collective-permute-done.1.halo_ref = f32[4,128,128]{2,1,0:T(8,128)S(1)} collective-permute-done((f32[4,128,128]{2,1,0:T(8,128)S(1)}, f32[4,128,128]{2,1,0:T(8,128)S(1)}, u32[]{:S(2)}, u32[]{:S(2)}) %collective-permute-start.1) | collective-permute-done | bytes 262176 | tf_op jit(solution)/shard_map/ppermute | solution.py:296
  10.6 0.6 near0.1.rest_5_.near_ref.self_ref.other_ref.prior_ref
  11.2 2.2 %collective-permute-start.4 = (f32[4,128,128]{2,1,0:T(8,128)S(1)}, f32[4,128,128]{2,1,0:T(8,128)S(1)}, u32[]{:S(2)}, u32[]{:S(2)}) collective-permute-start(f32[4,128,128]{2,1,0:T(8,128)S(1)} %near0.1.rest_5_.near_ref.self_ref.other_ref.prior_ref), channel_id=1, source_target_pairs={{0,2},{4,6},{8,10},{12,14},{16,18},{20,22},{24,26},{28,30},{32,34}... | collective-permute-start | bytes 786440 | tf_op jit(solution)/shard_map/ppermute | solution.py:296
  13.4 0.6 inner0.1.base_ref
  14.0 0.7 collective-permute-start.5
  14.9 1.2 collective-permute-done.3.rim_in_ref.rest_0_
  16.0 3.9 %collective-permute-done.4.halo_ref = f32[4,128,128]{2,1,0:T(8,128)S(1)} collective-permute-done((f32[4,128,128]{2,1,0:T(8,128)S(1)}, f32[4,128,128]{2,1,0:T(8,128)S(1)}, u32[]{:S(2)}, u32[]{:S(2)}) %collective-permute-start.4) | collective-permute-done | bytes 262176 | tf_op jit(solution)/shard_map/ppermute | solution.py:296
  19.9 0.6 near1.1.rest_5_.near_ref.self_ref.other_ref.prior_ref
  20.5 3.0 %collective-permute-start.7 = (f32[4,128,128]{2,1,0:T(8,128)S(1)}, f32[4,128,128]{2,1,0:T(8,128)S(1)}, u32[]{:S(2)}, u32[]{:S(2)}) collective-permute-start(f32[4,128,128]{2,1,0:T(8,128)S(1)} %near1.1.rest_5_.near_ref.self_ref.other_ref.prior_ref), channel_id=1, source_target_pairs={{0,2},{4,6},{8,10},{12,14},{16,18},{20,22},{24,26},{28,30},{32,34}... | collective-permute-start | bytes 786440 | tf_op jit(solution)/shard_map/ppermute | solution.py:296
  23.4 0.5 inner1.1.base_ref
  24.1 0.7 collective-permute-start.8
  24.9 1.2 collective-permute-done.6.rim_in_ref.rest_0_
  26.1 4.0 %collective-permute-done.7.halo_ref = f32[4,128,128]{2,1,0:T(8,128)S(1)} collective-permute-done((f32[4,128,128]{2,1,0:T(8,128)S(1)}, f32[4,128,128]{2,1,0:T(8,128)S(1)}, u32[]{:S(2)}, u32[]{:S(2)}) %collective-permute-start.7) | collective-permute-done | bytes 262176 | tf_op jit(solution)/shard_map/ppermute | solution.py:296
  30.1 0.6 near2.1.rest_5_.near_ref.self_ref.other_ref.prior_ref
  30.7 3.1 %collective-permute-start.10 = (f32[4,128,128]{2,1,0:T(8,128)S(1)}, f32[4,128,128]{2,1,0:T(8,128)S(1)}, u32[]{:S(2)}, u32[]{:S(2)}) collective-permute-start(f32[4,128,128]{2,1,0:T(8,128)S(1)} %near2.1.rest_5_.near_ref.self_ref.other_ref.prior_ref), channel_id=1, source_target_pairs={{0,2},{4,6},{8,10},{12,14},{16,18},{20,22},{24,26},{28,30},{32,34}... | collective-permute-start | bytes 786440 | tf_op jit(solution)/shard_map/ppermute | solution.py:296
  34.4 0.7 collective-permute-start.11
  35.2 1.2 collective-permute-done.9.rim_in_ref.rest_0_
  36.4 4.0 %collective-permute-done.10.halo_ref = f32[4,128,128]{2,1,0:T(8,128)S(1)} collective-permute-done((f32[4,128,128]{2,1,0:T(8,128)S(1)}, f32[4,128,128]{2,1,0:T(8,128)S(1)}, u32[]{:S(2)}, u32[]{:S(2)}) %collective-permute-start.10) | collective-permute-done | bytes 262176 | tf_op jit(solution)/shard_map/ppermute | solution.py:296
  40.4 0.6 near3.1.rest_5_.near_ref.self_ref.other_ref.prior_ref
  41.0 2.9 %collective-permute-start.13 = (f32[4,128,128]{2,1,0:T(8,128)S(1)}, f32[4,128,128]{2,1,0:T(8,128)S(1)}, u32[]{:S(2)}, u32[]{:S(2)}) collective-permute-start(f32[4,128,128]{2,1,0:T(8,128)S(1)} %near3.1.rest_5_.near_ref.self_ref.other_ref.prior_ref), channel_id=1, source_target_pairs={{0,2},{4,6},{8,10},{12,14},{16,18},{20,22},{24,26},{28,30},{32,34}... | collective-permute-start | bytes 786440 | tf_op jit(solution)/shard_map/ppermute | solution.py:296
  43.9 0.5 inner3.1.base_ref
  44.6 0.7 collective-permute-start.14
  45.4 1.2 collective-permute-done.12.rim_in_ref.rest_0_
  46.6 4.0 %collective-permute-done.13.halo_ref = f32[4,128,128]{2,1,0:T(8,128)S(1)} collective-permute-done((f32[4,128,128]{2,1,0:T(8,128)S(1)}, f32[4,128,128]{2,1,0:T(8,128)S(1)}, u32[]{:S(2)}, u32[]{:S(2)}) %collective-permute-start.13) | collective-permute-done | bytes 262176 | tf_op jit(solution)/shard_map/ppermute | solution.py:296
  50.6 0.6 near4.1.rest_5_.near_ref.self_ref.other_ref.prior_ref
  51.2 3.0 %collective-permute-start.16 = (f32[4,128,128]{2,1,0:T(8,128)S(1)}, f32[4,128,128]{2,1,0:T(8,128)S(1)}, u32[]{:S(2)}, u32[]{:S(2)}) collective-permute-start(f32[4,128,128]{2,1,0:T(8,128)S(1)} %near4.1.rest_5_.near_ref.self_ref.other_ref.prior_ref), channel_id=1, source_target_pairs={{0,2},{4,6},{8,10},{12,14},{16,18},{20,22},{24,26},{28,30},{32,34}... | collective-permute-start | bytes 786440 | tf_op jit(solution)/shard_map/ppermute | solution.py:296
  54.8 0.7 collective-permute-start.17
  55.7 1.2 collective-permute-done.15.rim_in_ref.rest_0_
  56.8 4.0 %collective-permute-done.16.halo_ref = f32[4,128,128]{2,1,0:T(8,128)S(1)} collective-permute-done((f32[4,128,128]{2,1,0:T(8,128)S(1)}, f32[4,128,128]{2,1,0:T(8,128)S(1)}, u32[]{:S(2)}, u32[]{:S(2)}) %collective-permute-start.16) | collective-permute-done | bytes 262176 | tf_op jit(solution)/shard_map/ppermute | solution.py:296
  60.9 0.6 near5.1.rest_5_.near_ref.self_ref.other_ref.prior_ref
  61.5 2.7 %collective-permute-start.19 = (f32[4,128,128]{2,1,0:T(8,128)S(1)}, f32[4,128,128]{2,1,0:T(8,128)S(1)}, u32[]{:S(2)}, u32[]{:S(2)}) collective-permute-start(f32[4,128,128]{2,1,0:T(8,128)S(1)} %near5.1.rest_5_.near_ref.self_ref.other_ref.prior_ref), channel_id=1, source_target_pairs={{0,2},{4,6},{8,10},{12,14},{16,18},{20,22},{24,26},{28,30},{32,34}... | collective-permute-start | bytes 786440 | tf_op jit(solution)/shard_map/ppermute | solution.py:296
  64.8 0.7 collective-permute-start.20
  65.6 1.2 collective-permute-done.18.rim_in_ref.rest_0_
  66.8 4.0 %collective-permute-done.19.halo_ref = f32[4,128,128]{2,1,0:T(8,128)S(1)} collective-permute-done((f32[4,128,128]{2,1,0:T(8,128)S(1)}, f32[4,128,128]{2,1,0:T(8,128)S(1)}, u32[]{:S(2)}, u32[]{:S(2)}) %collective-permute-start.19) | collective-permute-done | bytes 262176 | tf_op jit(solution)/shard_map/ppermute | solution.py:296
  70.8 0.6 near6.1.rest_5_.near_ref.self_ref.other_ref
  71.4 2.9 %collective-permute-start.22 = (f32[4,128,128]{2,1,0:T(8,128)S(1)}, f32[4,128,128]{2,1,0:T(8,128)S(1)}, u32[]{:S(2)}, u32[]{:S(2)}) collective-permute-start(f32[4,128,128]{2,1,0:T(8,128)S(1)} %near6.1.rest_5_.near_ref.self_ref.other_ref), channel_id=1, source_target_pairs={{0,2},{4,6},{8,10},{12,14},{16,18},{20,22},{24,26},{28,30},{32,34}... | collective-permute-start | bytes 786440 | tf_op jit(solution)/shard_map/ppermute | solution.py:296
  74.9 0.7 collective-permute-start.23
  75.7 1.2 collective-permute-done.21.rim_in_ref.rest_0_
  76.9 4.0 %collective-permute-done.22.halo_ref = f32[4,128,128]{2,1,0:T(8,128)S(1)} collective-permute-done((f32[4,128,128]{2,1,0:T(8,128)S(1)}, f32[4,128,128]{2,1,0:T(8,128)S(1)}, u32[]{:S(2)}, u32[]{:S(2)}) %collective-permute-start.22) | collective-permute-done | bytes 262176 | tf_op jit(solution)/shard_map/ppermute | solution.py:296
  80.9 0.6 near7.1.rest_5_.near_ref
  81.8 0.5 inner7.1.base_ref
  82.6 92.8 %all_to_all.11 = f32[32,32,128]{2,1,0:T(8,128)S(1)} all-to-all(f32[32,32,128]{2,1,0:T(8,128)S(1)} %bitcast.15), channel_id=1, replica_groups=mesh['shots'=4,'gx'=32,'gy'=2] {'gx'}, dimensions={0} | all-to-all | bytes 1048576 | tf_op jit(solution)/shard_map/all_to_all | solution.py:335
  175.4 1.1 close.1
  (50 shorter events, 5.3 us)
Async XLA Ops:
  0.7 1.0 copy-start.1
  1.9 3.4 %copy-start.6 = (bf16[128,8,128]{2,1,0:T(8,128)(2,1)S(1)}, bf16[128,8,128]{2,1,0:T(8,128)(2,1)}, u32[]{:S(2)}) copy-start(bf16[128,8,128]{2,1,0:T(8,128)(2,1)} %param.10) | copy-start | bytes 786436
  1.9 8.6 %collective-permute-start.1 = (f32[4,128,128]{2,1,0:T(8,128)S(1)}, f32[4,128,128]{2,1,0:T(8,128)S(1)}, u32[]{:S(2)}, u32[]{:S(2)}) collective-permute-start(f32[4,128,128]{2,1,0:T(8,128)S(1)} %open_near.1.near_ref.self_ref.other_ref.prior_ref), channel_id=1, source_target_pairs={{0,2},{4,6},{8,10},{12,14},{16,18},{20,22},{24,26},{28,30},{32,34}... | collective-permute-start | bytes 786440 | tf_op jit(solution)/shard_map/ppermute | solution.py:296
  4.3 1.6 copy-start.2
  4.3 9.6 %collective-permute-start.2 = (f32[4,128,128]{2,1,0:T(8,128)S(1)}, f32[4,128,128]{2,1,0:T(8,128)S(1)}, u32[]{:S(2)}, u32[]{:S(2)}) collective-permute-start(f32[4,128,128]{2,1,0:T(8,128)S(1)} %get-tuple-element.29.other_ref.self_ref.rest_1_), channel_id=1, source_target_pairs={{2,4},{6,8},{10,12},{14,16},{18,20},{22,24},{26,28},{30,32},{34,36... | collective-permute-start | bytes 786440 | tf_op jit(solution)/shard_map/ppermute | solution.py:297
  5.1 0.7 copy-start.7
  5.2 2.0 %collective-permute-start = (f32[8,4,128]{2,1,0:T(4,128)S(1)}, f32[8,4,128]{2,1,0:T(4,128)S(1)}, u32[]{:S(2)}, u32[]{:S(2)}) collective-permute-start(f32[8,4,128]{2,1,0:T(4,128)S(1)} %get-tuple-element.30), channel_id=1, source_target_pairs={{0,1},{1,0},{2,3},{3,2},{4,5},{5,4},{6,7},{7,6},{8,9},{9,8},{10,11... | collective-permute-start | bytes 49160 | tf_op jit(solution)/shard_map/ppermute | solution.py:298
  5.8 0.7 copy-start.4
  5.8 0.7 copy-start.5
  11.2 8.7 %collective-permute-start.4 = (f32[4,128,128]{2,1,0:T(8,128)S(1)}, f32[4,128,128]{2,1,0:T(8,128)S(1)}, u32[]{:S(2)}, u32[]{:S(2)}) collective-permute-start(f32[4,128,128]{2,1,0:T(8,128)S(1)} %near0.1.rest_5_.near_ref.self_ref.other_ref.prior_ref), channel_id=1, source_target_pairs={{0,2},{4,6},{8,10},{12,14},{16,18},{20,22},{24,26},{28,30},{32,34}... | collective-permute-start | bytes 786440 | tf_op jit(solution)/shard_map/ppermute | solution.py:296
  14.0 10.0 %collective-permute-start.5 = (f32[4,128,128]{2,1,0:T(8,128)S(1)}, f32[4,128,128]{2,1,0:T(8,128)S(1)}, u32[]{:S(2)}, u32[]{:S(2)}) collective-permute-start(f32[4,128,128]{2,1,0:T(8,128)S(1)} %get-tuple-element.38.other_ref.self_ref.rest_1_), channel_id=1, source_target_pairs={{2,4},{6,8},{10,12},{14,16},{18,20},{22,24},{26,28},{30,32},{34,36... | collective-permute-start | bytes 786440 | tf_op jit(solution)/shard_map/ppermute | solution.py:297
  14.7 1.3 collective-permute-start.3
  20.5 9.6 %collective-permute-start.7 = (f32[4,128,128]{2,1,0:T(8,128)S(1)}, f32[4,128,128]{2,1,0:T(8,128)S(1)}, u32[]{:S(2)}, u32[]{:S(2)}) collective-permute-start(f32[4,128,128]{2,1,0:T(8,128)S(1)} %near1.1.rest_5_.near_ref.self_ref.other_ref.prior_ref), channel_id=1, source_target_pairs={{0,2},{4,6},{8,10},{12,14},{16,18},{20,22},{24,26},{28,30},{32,34}... | collective-permute-start | bytes 786440 | tf_op jit(solution)/shard_map/ppermute | solution.py:296
  24.1 10.2 %collective-permute-start.8 = (f32[4,128,128]{2,1,0:T(8,128)S(1)}, f32[4,128,128]{2,1,0:T(8,128)S(1)}, u32[]{:S(2)}, u32[]{:S(2)}) collective-permute-start(f32[4,128,128]{2,1,0:T(8,128)S(1)} %get-tuple-element.40.other_ref.self_ref.rest_1_), channel_id=1, source_target_pairs={{2,4},{6,8},{10,12},{14,16},{18,20},{22,24},{26,28},{30,32},{34,36... | collective-permute-start | bytes 786440 | tf_op jit(solution)/shard_map/ppermute | solution.py:297
  24.8 1.3 collective-permute-start.6
  30.7 9.7 %collective-permute-start.10 = (f32[4,128,128]{2,1,0:T(8,128)S(1)}, f32[4,128,128]{2,1,0:T(8,128)S(1)}, u32[]{:S(2)}, u32[]{:S(2)}) collective-permute-start(f32[4,128,128]{2,1,0:T(8,128)S(1)} %near2.1.rest_5_.near_ref.self_ref.other_ref.prior_ref), channel_id=1, source_target_pairs={{0,2},{4,6},{8,10},{12,14},{16,18},{20,22},{24,26},{28,30},{32,34}... | collective-permute-start | bytes 786440 | tf_op jit(solution)/shard_map/ppermute | solution.py:296
  34.4 10.1 %collective-permute-start.11 = (f32[4,128,128]{2,1,0:T(8,128)S(1)}, f32[4,128,128]{2,1,0:T(8,128)S(1)}, u32[]{:S(2)}, u32[]{:S(2)}) collective-permute-start(f32[4,128,128]{2,1,0:T(8,128)S(1)} %get-tuple-element.42.other_ref.self_ref.rest_1_), channel_id=1, source_target_pairs={{2,4},{6,8},{10,12},{14,16},{18,20},{22,24},{26,28},{30,32},{34,36... | collective-permute-start | bytes 786440 | tf_op jit(solution)/shard_map/ppermute | solution.py:297
  35.1 1.3 collective-permute-start.9
  41.0 9.6 %collective-permute-start.13 = (f32[4,128,128]{2,1,0:T(8,128)S(1)}, f32[4,128,128]{2,1,0:T(8,128)S(1)}, u32[]{:S(2)}, u32[]{:S(2)}) collective-permute-start(f32[4,128,128]{2,1,0:T(8,128)S(1)} %near3.1.rest_5_.near_ref.self_ref.other_ref.prior_ref), channel_id=1, source_target_pairs={{0,2},{4,6},{8,10},{12,14},{16,18},{20,22},{24,26},{28,30},{32,34}... | collective-permute-start | bytes 786440 | tf_op jit(solution)/shard_map/ppermute | solution.py:296
  44.6 10.2 %collective-permute-start.14 = (f32[4,128,128]{2,1,0:T(8,128)S(1)}, f32[4,128,128]{2,1,0:T(8,128)S(1)}, u32[]{:S(2)}, u32[]{:S(2)}) collective-permute-start(f32[4,128,128]{2,1,0:T(8,128)S(1)} %get-tuple-element.44.other_ref.self_ref.rest_1_), channel_id=1, source_target_pairs={{2,4},{6,8},{10,12},{14,16},{18,20},{22,24},{26,28},{30,32},{34,36... | collective-permute-start | bytes 786440 | tf_op jit(solution)/shard_map/ppermute | solution.py:297
  45.3 1.3 collective-permute-start.12
  51.2 9.7 %collective-permute-start.16 = (f32[4,128,128]{2,1,0:T(8,128)S(1)}, f32[4,128,128]{2,1,0:T(8,128)S(1)}, u32[]{:S(2)}, u32[]{:S(2)}) collective-permute-start(f32[4,128,128]{2,1,0:T(8,128)S(1)} %near4.1.rest_5_.near_ref.self_ref.other_ref.prior_ref), channel_id=1, source_target_pairs={{0,2},{4,6},{8,10},{12,14},{16,18},{20,22},{24,26},{28,30},{32,34}... | collective-permute-start | bytes 786440 | tf_op jit(solution)/shard_map/ppermute | solution.py:296
  54.8 9.9 %collective-permute-start.17 = (f32[4,128,128]{2,1,0:T(8,128)S(1)}, f32[4,128,128]{2,1,0:T(8,128)S(1)}, u32[]{:S(2)}, u32[]{:S(2)}) collective-permute-start(f32[4,128,128]{2,1,0:T(8,128)S(1)} %get-tuple-element.46.other_ref.self_ref.rest_1_), channel_id=1, source_target_pairs={{2,4},{6,8},{10,12},{14,16},{18,20},{22,24},{26,28},{30,32},{34,36... | collective-permute-start | bytes 786440 | tf_op jit(solution)/shard_map/ppermute | solution.py:297
  55.5 1.3 collective-permute-start.15
  61.5 9.4 %collective-permute-start.19 = (f32[4,128,128]{2,1,0:T(8,128)S(1)}, f32[4,128,128]{2,1,0:T(8,128)S(1)}, u32[]{:S(2)}, u32[]{:S(2)}) collective-permute-start(f32[4,128,128]{2,1,0:T(8,128)S(1)} %near5.1.rest_5_.near_ref.self_ref.other_ref.prior_ref), channel_id=1, source_target_pairs={{0,2},{4,6},{8,10},{12,14},{16,18},{20,22},{24,26},{28,30},{32,34}... | collective-permute-start | bytes 786440 | tf_op jit(solution)/shard_map/ppermute | solution.py:296
  64.8 10.0 %collective-permute-start.20 = (f32[4,128,128]{2,1,0:T(8,128)S(1)}, f32[4,128,128]{2,1,0:T(8,128)S(1)}, u32[]{:S(2)}, u32[]{:S(2)}) collective-permute-start(f32[4,128,128]{2,1,0:T(8,128)S(1)} %get-tuple-element.48.other_ref.self_ref.rest_1_), channel_id=1, source_target_pairs={{2,4},{6,8},{10,12},{14,16},{18,20},{22,24},{26,28},{30,32},{34,36... | collective-permute-start | bytes 786440 | tf_op jit(solution)/shard_map/ppermute | solution.py:297
  65.5 1.3 collective-permute-start.18
  71.4 9.5 %collective-permute-start.22 = (f32[4,128,128]{2,1,0:T(8,128)S(1)}, f32[4,128,128]{2,1,0:T(8,128)S(1)}, u32[]{:S(2)}, u32[]{:S(2)}) collective-permute-start(f32[4,128,128]{2,1,0:T(8,128)S(1)} %near6.1.rest_5_.near_ref.self_ref.other_ref), channel_id=1, source_target_pairs={{0,2},{4,6},{8,10},{12,14},{16,18},{20,22},{24,26},{28,30},{32,34}... | collective-permute-start | bytes 786440 | tf_op jit(solution)/shard_map/ppermute | solution.py:296
  74.9 7.5 %collective-permute-start.23 = (f32[4,128,128]{2,1,0:T(8,128)S(1)}, f32[4,128,128]{2,1,0:T(8,128)S(1)}, u32[]{:S(2)}, u32[]{:S(2)}) collective-permute-start(f32[4,128,128]{2,1,0:T(8,128)S(1)} %get-tuple-element.50.other_ref.self_ref), channel_id=1, source_target_pairs={{2,4},{6,8},{10,12},{14,16},{18,20},{22,24},{26,28},{30,32},{34,36... | collective-permute-start | bytes 786440 | tf_op jit(solution)/shard_map/ppermute | solution.py:297
  75.6 5.9 %copy-start = (f32[128,8,128]{2,1,0:T(8,128)S(1)}, f32[128,8,128]{2,1,0:T(8,128)}, u32[]{:S(2)}) copy-start(f32[128,8,128]{2,1,0:T(8,128)} %param.15) | copy-start | bytes 1572868
  75.6 1.3 collective-permute-start.21
  80.9 0.7 copy-start.3

commit v8 on v7

--- a/solution.py
+++ b/solution.py
@@ -98,8 +98,8 @@
         mark_far[i] = jnp.where(levels == columns[:, base + REACH + i : base + REACH + i + 1], 1.0, 0.0)
 
 
-def advance_kernel(
-    step, half, sides_ref, self_ref, other_ref, halo_ref, rim_in_ref, prior_ref, coef_ref, mark_ref, amp_ref, *rest
+def inner_kernel(
+    step, half, sides_ref, self_ref, other_ref, rim_in_ref, prior_ref, coef_ref, mark_ref, amp_ref, *rest
 ):
     pad_ref, deep_ref = rest[-2:]
     first = sides_ref[1:2, :]
@@ -128,8 +128,6 @@
         at = slice(row, row + CHUNK)
         line = [other_ref[REACH - 1 - i, at, :] for i in range(REACH)]
         line += [self_ref[i, at, :] for i in range(REACH)]
-        if halo_ref is not None:
-            line += [halo_ref[REACH - 1 - i, at, :] for i in range(REACH)]
         for i in range(planes):
             total = deep_ref[i * length + row : i * length + row + CHUNK, :]
             for k in range(1, REACH + 1):
@@ -146,10 +144,6 @@
                 + coef_ref[i, at, :] * total
                 + mark_ref[i, at, :] * amp_ref[at, column : column + 1]
             )
-
-
-def inner_kernel(step, half, sides_ref, self_ref, other_ref, *rest):
-    advance_kernel(step, half, sides_ref, self_ref, other_ref, None, *rest)
 
 
 def add_halo(base_ref, coef_ref, halo_ref, out_ref):
@@ -296,19 +290,20 @@
         near_halo = lax.ppermute(near, "gx", near_pairs)
         far_halo = lax.ppermute(far, "gx", far_pairs)
         edge_in = lax.ppermute(edge, "gy", rim_pairs)
-        near_next = kernel(
-            functools.partial(advance_kernel, step, 0),
+        near_base = kernel(
+            functools.partial(inner_kernel, step, 0),
             half,
-            (sides, near, far, near_halo, edge_in, near_prior, near_coef, near_mark, amp),
+            (sides, near, far, edge_in, near_prior, near_coef, near_mark, amp),
             scratch,
-            f"near{step}",
+            f"inner_near{step}",
         )
+        near_next = kernel(add_halo, half, (near_base, near_coef, near_halo), name=f"near{step}")
         base = kernel(
             functools.partial(inner_kernel, step, 1),
             half,
             (sides, far, near, edge_in, far_prior, far_coef, far_mark, amp, near_next),
             scratch,
-            f"inner{step}",
+            f"inner_far{step}",
         )
         if step < STEPS - 1:
             far_next, edge = kernel(

time: 177 us -> 178 us (level)
  waiting for transfers between devices: 39.6 us -> 35.1 us
  starting transfers between devices: 28.7 us -> 32.6 us
    ppermute x8, waiting for transfers between devices: 31.5 us -> 27 us  [shards(): near_halo = lax.ppermute(near, 'gx', near_pairs)]
    ppermute x8, starting transfers between devices: 22 us -> 25.8 us  [shards(): near_halo = lax.ppermute(near, 'gx', near_pairs)]
    pallas_call x29 -> x37, Pallas kernels: 12.1 us -> 12.2 us  [kernel(): pl.pallas_call(body, out_shape=outs, in_specs=[VM] * len(inputs), out_spe...]
where the time goes in v8:
time: 178 us
  blocking collectives  93.6 us (53%)
  waiting for transfers between devices  35.1 us (20%)
  starting transfers between devices  32.6 us (18%)
  Pallas kernels  12.2 us (7%)
  local copies, waits for them, and re-layouts  2.88 us (2%)
    all_to_all x1, blocking collectives, shards(): lax.all_to_all(filtered, 'gx', split_axis=0, concat_axis=0, tiled=True)  93.6 us
    ppermute x8, waiting for transfers between devices, shards(): near_halo = lax.ppermute(near, 'gx', near_pairs)  27 us
    ppermute x8, starting transfers between devices, shards(): near_halo = lax.ppermute(near, 'gx', near_pairs)  25.8 us
    pallas_call x37, Pallas kernels, kernel(): pl.pallas_call(body, out_shape=outs, in_specs=[VM] * len(inputs), out_spe...  12.2 us
    ppermute x8, waiting for transfers between devices, shards(): edge_in = lax.ppermute(edge, 'gy', rim_pairs)  8.1 us
    ppermute x8, starting transfers between devices, shards(): far_halo = lax.ppermute(far, 'gx', far_pairs)  5.53 us
  transfers between devices with their start and end apart: 24, of which 15 were waited for; matrix products, arithmetic and copies ran while one was open for 0% of the time, Pallas kernels for 6%

profile of v8, /device:TPU:46, one launch (start us, length us, event | category | flops | bytes accessed | tf_op | source)
XLA Modules:
  0.0 177.5 jit_solution(3716934150840138505)
XLA Ops:
  0.7 1.0 copy-done.1
  1.9 2.2 %collective-permute-start.1 = (f32[4,128,128]{2,1,0:T(8,128)S(1)}, f32[4,128,128]{2,1,0:T(8,128)S(1)}, u32[]{:S(2)}, u32[]{:S(2)}) collective-permute-start(f32[4,128,128]{2,1,0:T(8,128)S(1)} %open_near.1.near_ref.self_ref.other_ref.prior_ref), channel_id=1, source_target_pairs={{0,2},{4,6},{8,10},{12,14},{16,18},{20,22},{24,26},{28,30},{32,34}... | collective-permute-start | bytes 786440 | tf_op jit(solution)/shard_map/ppermute | solution.py:290
  4.3 0.8 collective-permute-start.2
  5.9 0.6 copy-done.4
  6.5 0.6 tables.1
  7.1 0.5 inner_near0.1.base_ref
  7.7 2.9 %collective-permute-done.1.halo_ref = f32[4,128,128]{2,1,0:T(8,128)S(1)} collective-permute-done((f32[4,128,128]{2,1,0:T(8,128)S(1)}, f32[4,128,128]{2,1,0:T(8,128)S(1)}, u32[]{:S(2)}, u32[]{:S(2)}) %collective-permute-start.1) | collective-permute-done | bytes 262176 | tf_op jit(solution)/shard_map/ppermute | solution.py:290
  10.6 2.8 %collective-permute-start.4 = (f32[4,128,128]{2,1,0:T(8,128)S(1)}, f32[4,128,128]{2,1,0:T(8,128)S(1)}, u32[]{:S(2)}, u32[]{:S(2)}) collective-permute-start(f32[4,128,128]{2,1,0:T(8,128)S(1)} %near0.1.rest_0_.near_ref.self_ref.other_ref.prior_ref), channel_id=1, source_target_pairs={{0,2},{4,6},{8,10},{12,14},{16,18},{20,22},{24,26},{28,30},{32,34}... | collective-permute-start | bytes 786440 | tf_op jit(solution)/shard_map/ppermute | solution.py:290
  13.4 0.5 inner_far0.1.base_ref
  14.0 0.7 collective-permute-start.5
  14.8 1.2 collective-permute-done.3.rim_in_ref
  16.5 3.4 %collective-permute-done.4.halo_ref = f32[4,128,128]{2,1,0:T(8,128)S(1)} collective-permute-done((f32[4,128,128]{2,1,0:T(8,128)S(1)}, f32[4,128,128]{2,1,0:T(8,128)S(1)}, u32[]{:S(2)}, u32[]{:S(2)}) %collective-permute-start.4) | collective-permute-done | bytes 262176 | tf_op jit(solution)/shard_map/ppermute | solution.py:290
  20.0 3.5 %collective-permute-start.7 = (f32[4,128,128]{2,1,0:T(8,128)S(1)}, f32[4,128,128]{2,1,0:T(8,128)S(1)}, u32[]{:S(2)}, u32[]{:S(2)}) collective-permute-start(f32[4,128,128]{2,1,0:T(8,128)S(1)} %near1.1.rest_0_.near_ref.self_ref.other_ref.prior_ref), channel_id=1, source_target_pairs={{0,2},{4,6},{8,10},{12,14},{16,18},{20,22},{24,26},{28,30},{32,34}... | collective-permute-start | bytes 786440 | tf_op jit(solution)/shard_map/ppermute | solution.py:290
  24.1 0.7 collective-permute-start.8
  24.9 1.2 collective-permute-done.6.rim_in_ref
  26.1 0.5 inner_near2.1.base_ref
  26.6 3.5 %collective-permute-done.7.halo_ref = f32[4,128,128]{2,1,0:T(8,128)S(1)} collective-permute-done((f32[4,128,128]{2,1,0:T(8,128)S(1)}, f32[4,128,128]{2,1,0:T(8,128)S(1)}, u32[]{:S(2)}, u32[]{:S(2)}) %collective-permute-start.7) | collective-permute-done | bytes 262176 | tf_op jit(solution)/shard_map/ppermute | solution.py:290
  30.2 3.6 %collective-permute-start.10 = (f32[4,128,128]{2,1,0:T(8,128)S(1)}, f32[4,128,128]{2,1,0:T(8,128)S(1)}, u32[]{:S(2)}, u32[]{:S(2)}) collective-permute-start(f32[4,128,128]{2,1,0:T(8,128)S(1)} %near2.1.rest_0_.near_ref.self_ref.other_ref.prior_ref), channel_id=1, source_target_pairs={{0,2},{4,6},{8,10},{12,14},{16,18},{20,22},{24,26},{28,30},{32,34}... | collective-permute-start | bytes 786440 | tf_op jit(solution)/shard_map/ppermute | solution.py:290
  33.8 0.5 inner_far2.1.base_ref
  34.4 0.7 collective-permute-start.11
  35.2 1.2 collective-permute-done.9.rim_in_ref
  36.9 3.5 %collective-permute-done.10.halo_ref = f32[4,128,128]{2,1,0:T(8,128)S(1)} collective-permute-done((f32[4,128,128]{2,1,0:T(8,128)S(1)}, f32[4,128,128]{2,1,0:T(8,128)S(1)}, u32[]{:S(2)}, u32[]{:S(2)}) %collective-permute-start.10) | collective-permute-done | bytes 262176 | tf_op jit(solution)/shard_map/ppermute | solution.py:290
  40.5 3.5 %collective-permute-start.13 = (f32[4,128,128]{2,1,0:T(8,128)S(1)}, f32[4,128,128]{2,1,0:T(8,128)S(1)}, u32[]{:S(2)}, u32[]{:S(2)}) collective-permute-start(f32[4,128,128]{2,1,0:T(8,128)S(1)} %near3.1.rest_0_.near_ref.self_ref.other_ref.prior_ref), channel_id=1, source_target_pairs={{0,2},{4,6},{8,10},{12,14},{16,18},{20,22},{24,26},{28,30},{32,34}... | collective-permute-start | bytes 786440 | tf_op jit(solution)/shard_map/ppermute | solution.py:290
  44.6 0.7 collective-permute-start.14
  45.6 1.2 collective-permute-done.12.rim_in_ref
  46.8 0.6 inner_near4.1.base_ref
  47.3 3.3 %collective-permute-done.13.halo_ref = f32[4,128,128]{2,1,0:T(8,128)S(1)} collective-permute-done((f32[4,128,128]{2,1,0:T(8,128)S(1)}, f32[4,128,128]{2,1,0:T(8,128)S(1)}, u32[]{:S(2)}, u32[]{:S(2)}) %collective-permute-start.13) | collective-permute-done | bytes 262176 | tf_op jit(solution)/shard_map/ppermute | solution.py:290
  50.7 3.6 %collective-permute-start.16 = (f32[4,128,128]{2,1,0:T(8,128)S(1)}, f32[4,128,128]{2,1,0:T(8,128)S(1)}, u32[]{:S(2)}, u32[]{:S(2)}) collective-permute-start(f32[4,128,128]{2,1,0:T(8,128)S(1)} %near4.1.rest_0_.near_ref.self_ref.other_ref.prior_ref), channel_id=1, source_target_pairs={{0,2},{4,6},{8,10},{12,14},{16,18},{20,22},{24,26},{28,30},{32,34}... | collective-permute-start | bytes 786440 | tf_op jit(solution)/shard_map/ppermute | solution.py:290
  54.3 0.6 inner_far4.1.base_ref
  55.0 0.7 collective-permute-start.17
  55.8 1.2 collective-permute-done.15.rim_in_ref
  56.9 0.6 inner_near5.1.base_ref
  57.5 3.5 %collective-permute-done.16.halo_ref = f32[4,128,128]{2,1,0:T(8,128)S(1)} collective-permute-done((f32[4,128,128]{2,1,0:T(8,128)S(1)}, f32[4,128,128]{2,1,0:T(8,128)S(1)}, u32[]{:S(2)}, u32[]{:S(2)}) %collective-permute-start.16) | collective-permute-done | bytes 262176 | tf_op jit(solution)/shard_map/ppermute | solution.py:290
  61.0 3.3 %collective-permute-start.19 = (f32[4,128,128]{2,1,0:T(8,128)S(1)}, f32[4,128,128]{2,1,0:T(8,128)S(1)}, u32[]{:S(2)}, u32[]{:S(2)}) collective-permute-start(f32[4,128,128]{2,1,0:T(8,128)S(1)} %near5.1.rest_0_.near_ref.self_ref.other_ref.prior_ref), channel_id=1, source_target_pairs={{0,2},{4,6},{8,10},{12,14},{16,18},{20,22},{24,26},{28,30},{32,34}... | collective-permute-start | bytes 786440 | tf_op jit(solution)/shard_map/ppermute | solution.py:290
  64.3 0.6 inner_far5.1.base_ref
  64.9 0.7 collective-permute-start.20
  65.8 1.2 collective-permute-done.18.rim_in_ref
  67.5 3.5 %collective-permute-done.19.halo_ref = f32[4,128,128]{2,1,0:T(8,128)S(1)} collective-permute-done((f32[4,128,128]{2,1,0:T(8,128)S(1)}, f32[4,128,128]{2,1,0:T(8,128)S(1)}, u32[]{:S(2)}, u32[]{:S(2)}) %collective-permute-start.19) | collective-permute-done | bytes 262176 | tf_op jit(solution)/shard_map/ppermute | solution.py:290
  71.0 3.3 %collective-permute-start.22 = (f32[4,128,128]{2,1,0:T(8,128)S(1)}, f32[4,128,128]{2,1,0:T(8,128)S(1)}, u32[]{:S(2)}, u32[]{:S(2)}) collective-permute-start(f32[4,128,128]{2,1,0:T(8,128)S(1)} %near6.1.rest_0_.near_ref.self_ref.other_ref), channel_id=1, source_target_pairs={{0,2},{4,6},{8,10},{12,14},{16,18},{20,22},{24,26},{28,30},{32,34}... | collective-permute-start | bytes 786440 | tf_op jit(solution)/shard_map/ppermute | solution.py:290
  74.3 0.5 inner_far6.1.base_ref
  75.0 0.7 collective-permute-start.23
  75.8 1.2 collective-permute-done.21.rim_in_ref
  77.0 0.5 inner_near7.1.base_ref
  77.5 3.5 %collective-permute-done.22.halo_ref = f32[4,128,128]{2,1,0:T(8,128)S(1)} collective-permute-done((f32[4,128,128]{2,1,0:T(8,128)S(1)}, f32[4,128,128]{2,1,0:T(8,128)S(1)}, u32[]{:S(2)}, u32[]{:S(2)}) %collective-permute-start.22) | collective-permute-done | bytes 262176 | tf_op jit(solution)/shard_map/ppermute | solution.py:290
  81.1 0.6 copy-done.3
  81.9 0.5 inner_far7.1.base_ref
  82.7 93.6 %all_to_all.11 = f32[32,32,128]{2,1,0:T(8,128)S(1)} all-to-all(f32[32,32,128]{2,1,0:T(8,128)S(1)} %bitcast.15), channel_id=1, replica_groups=mesh['shots'=4,'gx'=32,'gy'=2] {'gx'}, dimensions={0} | all-to-all | bytes 1048576 | tf_op jit(solution)/shard_map/all_to_all | solution.py:330
  176.4 1.1 close.1
  (58 shorter events, 6.5 us)
Async XLA Ops:
  0.7 1.0 copy-start.1
  1.9 3.4 %copy-start.6 = (bf16[128,8,128]{2,1,0:T(8,128)(2,1)S(1)}, bf16[128,8,128]{2,1,0:T(8,128)(2,1)}, u32[]{:S(2)}) copy-start(bf16[128,8,128]{2,1,0:T(8,128)(2,1)} %param.10) | copy-start | bytes 786436
  1.9 8.6 %collective-permute-start.1 = (f32[4,128,128]{2,1,0:T(8,128)S(1)}, f32[4,128,128]{2,1,0:T(8,128)S(1)}, u32[]{:S(2)}, u32[]{:S(2)}) collective-permute-start(f32[4,128,128]{2,1,0:T(8,128)S(1)} %open_near.1.near_ref.self_ref.other_ref.prior_ref), channel_id=1, source_target_pairs={{0,2},{4,6},{8,10},{12,14},{16,18},{20,22},{24,26},{28,30},{32,34}... | collective-permute-start | bytes 786440 | tf_op jit(solution)/shard_map/ppermute | solution.py:290
  4.3 1.6 copy-start.2
  4.3 9.6 %collective-permute-start.2 = (f32[4,128,128]{2,1,0:T(8,128)S(1)}, f32[4,128,128]{2,1,0:T(8,128)S(1)}, u32[]{:S(2)}, u32[]{:S(2)}) collective-permute-start(f32[4,128,128]{2,1,0:T(8,128)S(1)} %get-tuple-element.29.other_ref.self_ref.prior_ref), channel_id=1, source_target_pairs={{2,4},{6,8},{10,12},{14,16},{18,20},{22,24},{26,28},{30,32},{34,36... | collective-permute-start | bytes 786440 | tf_op jit(solution)/shard_map/ppermute | solution.py:291
  5.1 0.7 copy-start.7
  5.2 2.0 %collective-permute-start = (f32[8,4,128]{2,1,0:T(4,128)S(1)}, f32[8,4,128]{2,1,0:T(4,128)S(1)}, u32[]{:S(2)}, u32[]{:S(2)}) collective-permute-start(f32[8,4,128]{2,1,0:T(4,128)S(1)} %get-tuple-element.30), channel_id=1, source_target_pairs={{0,1},{1,0},{2,3},{3,2},{4,5},{5,4},{6,7},{7,6},{8,9},{9,8},{10,11... | collective-permute-start | bytes 49160 | tf_op jit(solution)/shard_map/ppermute | solution.py:292
  5.8 0.7 copy-start.4
  5.8 0.7 copy-start.5
  10.6 9.3 %collective-permute-start.4 = (f32[4,128,128]{2,1,0:T(8,128)S(1)}, f32[4,128,128]{2,1,0:T(8,128)S(1)}, u32[]{:S(2)}, u32[]{:S(2)}) collective-permute-start(f32[4,128,128]{2,1,0:T(8,128)S(1)} %near0.1.rest_0_.near_ref.self_ref.other_ref.prior_ref), channel_id=1, source_target_pairs={{0,2},{4,6},{8,10},{12,14},{16,18},{20,22},{24,26},{28,30},{32,34}... | collective-permute-start | bytes 786440 | tf_op jit(solution)/shard_map/ppermute | solution.py:290
  14.0 10.0 %collective-permute-start.5 = (f32[4,128,128]{2,1,0:T(8,128)S(1)}, f32[4,128,128]{2,1,0:T(8,128)S(1)}, u32[]{:S(2)}, u32[]{:S(2)}) collective-permute-start(f32[4,128,128]{2,1,0:T(8,128)S(1)} %get-tuple-element.38.other_ref.self_ref.prior_ref), channel_id=1, source_target_pairs={{2,4},{6,8},{10,12},{14,16},{18,20},{22,24},{26,28},{30,32},{34,36... | collective-permute-start | bytes 786440 | tf_op jit(solution)/shard_map/ppermute | solution.py:291
  14.7 1.3 collective-permute-start.3
  20.0 10.1 %collective-permute-start.7 = (f32[4,128,128]{2,1,0:T(8,128)S(1)}, f32[4,128,128]{2,1,0:T(8,128)S(1)}, u32[]{:S(2)}, u32[]{:S(2)}) collective-permute-start(f32[4,128,128]{2,1,0:T(8,128)S(1)} %near1.1.rest_0_.near_ref.self_ref.other_ref.prior_ref), channel_id=1, source_target_pairs={{0,2},{4,6},{8,10},{12,14},{16,18},{20,22},{24,26},{28,30},{32,34}... | collective-permute-start | bytes 786440 | tf_op jit(solution)/shard_map/ppermute | solution.py:290
  24.1 10.3 %collective-permute-start.8 = (f32[4,128,128]{2,1,0:T(8,128)S(1)}, f32[4,128,128]{2,1,0:T(8,128)S(1)}, u32[]{:S(2)}, u32[]{:S(2)}) collective-permute-start(f32[4,128,128]{2,1,0:T(8,128)S(1)} %get-tuple-element.40.other_ref.self_ref.prior_ref), channel_id=1, source_target_pairs={{2,4},{6,8},{10,12},{14,16},{18,20},{22,24},{26,28},{30,32},{34,36... | collective-permute-start | bytes 786440 | tf_op jit(solution)/shard_map/ppermute | solution.py:291
  24.7 1.3 collective-permute-start.6
  30.2 10.3 %collective-permute-start.10 = (f32[4,128,128]{2,1,0:T(8,128)S(1)}, f32[4,128,128]{2,1,0:T(8,128)S(1)}, u32[]{:S(2)}, u32[]{:S(2)}) collective-permute-start(f32[4,128,128]{2,1,0:T(8,128)S(1)} %near2.1.rest_0_.near_ref.self_ref.other_ref.prior_ref), channel_id=1, source_target_pairs={{0,2},{4,6},{8,10},{12,14},{16,18},{20,22},{24,26},{28,30},{32,34}... | collective-permute-start | bytes 786440 | tf_op jit(solution)/shard_map/ppermute | solution.py:290
  34.4 10.1 %collective-permute-start.11 = (f32[4,128,128]{2,1,0:T(8,128)S(1)}, f32[4,128,128]{2,1,0:T(8,128)S(1)}, u32[]{:S(2)}, u32[]{:S(2)}) collective-permute-start(f32[4,128,128]{2,1,0:T(8,128)S(1)} %get-tuple-element.42.other_ref.self_ref.prior_ref), channel_id=1, source_target_pairs={{2,4},{6,8},{10,12},{14,16},{18,20},{22,24},{26,28},{30,32},{34,36... | collective-permute-start | bytes 786440 | tf_op jit(solution)/shard_map/ppermute | solution.py:291
  35.1 1.3 collective-permute-start.9
  40.5 10.1 %collective-permute-start.13 = (f32[4,128,128]{2,1,0:T(8,128)S(1)}, f32[4,128,128]{2,1,0:T(8,128)S(1)}, u32[]{:S(2)}, u32[]{:S(2)}) collective-permute-start(f32[4,128,128]{2,1,0:T(8,128)S(1)} %near3.1.rest_0_.near_ref.self_ref.other_ref.prior_ref), channel_id=1, source_target_pairs={{0,2},{4,6},{8,10},{12,14},{16,18},{20,22},{24,26},{28,30},{32,34}... | collective-permute-start | bytes 786440 | tf_op jit(solution)/shard_map/ppermute | solution.py:290
  44.6 10.3 %collective-permute-start.14 = (f32[4,128,128]{2,1,0:T(8,128)S(1)}, f32[4,128,128]{2,1,0:T(8,128)S(1)}, u32[]{:S(2)}, u32[]{:S(2)}) collective-permute-start(f32[4,128,128]{2,1,0:T(8,128)S(1)} %get-tuple-element.44.other_ref.self_ref.prior_ref), channel_id=1, source_target_pairs={{2,4},{6,8},{10,12},{14,16},{18,20},{22,24},{26,28},{30,32},{34,36... | collective-permute-start | bytes 786440 | tf_op jit(solution)/shard_map/ppermute | solution.py:291
  45.3 1.5 collective-permute-start.12
  50.7 10.2 %collective-permute-start.16 = (f32[4,128,128]{2,1,0:T(8,128)S(1)}, f32[4,128,128]{2,1,0:T(8,128)S(1)}, u32[]{:S(2)}, u32[]{:S(2)}) collective-permute-start(f32[4,128,128]{2,1,0:T(8,128)S(1)} %near4.1.rest_0_.near_ref.self_ref.other_ref.prior_ref), channel_id=1, source_target_pairs={{0,2},{4,6},{8,10},{12,14},{16,18},{20,22},{24,26},{28,30},{32,34}... | collective-permute-start | bytes 786440 | tf_op jit(solution)/shard_map/ppermute | solution.py:290
  55.0 9.9 %collective-permute-start.17 = (f32[4,128,128]{2,1,0:T(8,128)S(1)}, f32[4,128,128]{2,1,0:T(8,128)S(1)}, u32[]{:S(2)}, u32[]{:S(2)}) collective-permute-start(f32[4,128,128]{2,1,0:T(8,128)S(1)} %get-tuple-element.46.other_ref.self_ref.prior_ref), channel_id=1, source_target_pairs={{2,4},{6,8},{10,12},{14,16},{18,20},{22,24},{26,28},{30,32},{34,36... | collective-permute-start | bytes 786440 | tf_op jit(solution)/shard_map/ppermute | solution.py:291
  55.6 1.3 collective-permute-start.15
  61.0 9.9 %collective-permute-start.19 = (f32[4,128,128]{2,1,0:T(8,128)S(1)}, f32[4,128,128]{2,1,0:T(8,128)S(1)}, u32[]{:S(2)}, u32[]{:S(2)}) collective-permute-start(f32[4,128,128]{2,1,0:T(8,128)S(1)} %near5.1.rest_0_.near_ref.self_ref.other_ref.prior_ref), channel_id=1, source_target_pairs={{0,2},{4,6},{8,10},{12,14},{16,18},{20,22},{24,26},{28,30},{32,34}... | collective-permute-start | bytes 786440 | tf_op jit(solution)/shard_map/ppermute | solution.py:290
  64.9 9.9 %collective-permute-start.20 = (f32[4,128,128]{2,1,0:T(8,128)S(1)}, f32[4,128,128]{2,1,0:T(8,128)S(1)}, u32[]{:S(2)}, u32[]{:S(2)}) collective-permute-start(f32[4,128,128]{2,1,0:T(8,128)S(1)} %get-tuple-element.48.other_ref.self_ref.prior_ref), channel_id=1, source_target_pairs={{2,4},{6,8},{10,12},{14,16},{18,20},{22,24},{26,28},{30,32},{34,36... | collective-permute-start | bytes 786440 | tf_op jit(solution)/shard_map/ppermute | solution.py:291
  65.6 1.3 collective-permute-start.18
  71.0 10.0 %collective-permute-start.22 = (f32[4,128,128]{2,1,0:T(8,128)S(1)}, f32[4,128,128]{2,1,0:T(8,128)S(1)}, u32[]{:S(2)}, u32[]{:S(2)}) collective-permute-start(f32[4,128,128]{2,1,0:T(8,128)S(1)} %near6.1.rest_0_.near_ref.self_ref.other_ref), channel_id=1, source_target_pairs={{0,2},{4,6},{8,10},{12,14},{16,18},{20,22},{24,26},{28,30},{32,34}... | collective-permute-start | bytes 786440 | tf_op jit(solution)/shard_map/ppermute | solution.py:290
  75.0 7.5 %collective-permute-start.23 = (f32[4,128,128]{2,1,0:T(8,128)S(1)}, f32[4,128,128]{2,1,0:T(8,128)S(1)}, u32[]{:S(2)}, u32[]{:S(2)}) collective-permute-start(f32[4,128,128]{2,1,0:T(8,128)S(1)} %get-tuple-element.50.other_ref.self_ref), channel_id=1, source_target_pairs={{2,4},{6,8},{10,12},{14,16},{18,20},{22,24},{26,28},{30,32},{34,36... | collective-permute-start | bytes 786440 | tf_op jit(solution)/shard_map/ppermute | solution.py:291
  75.6 1.3 collective-permute-start.21
  77.5 3.6 %copy-start = (f32[128,8,128]{2,1,0:T(8,128)S(1)}, f32[128,8,128]{2,1,0:T(8,128)}, u32[]{:S(2)}) copy-start(f32[128,8,128]{2,1,0:T(8,128)} %param.15) | copy-start | bytes 1572868
  81.0 0.7 copy-start.3

commit v9 on v5

--- a/solution.py
+++ b/solution.py
@@ -171,7 +171,7 @@
         rim_ref[REACH + i] = rim(out_ref, i, first)
 
 
-def image_half(is_near, sides_ref, half_ref, receiver_ref, receiver_depth_ref, image_ref, pad_ref, row, stride):
+def image_half(is_near, sides_ref, half_ref, receiver_ref, receiver_depth_ref, image_ref, pad_ref, row, stride, keep):
     odd = sides_ref[0:1, :]
     length, depth = half_ref.shape[1:]
     width = 2 * REACH
@@ -192,6 +192,7 @@
             field = choose(odd, rising.shape, rising, falling).T
             receiver = choose(odd, low.shape, high, low)
             begin = choose(odd, start_low.shape, start_high, start_low)
+        keep(j, field)
         begin = jnp.broadcast_to(begin, levels.shape)
         product = field * jnp.where(levels >= begin, receiver, jnp.zeros_like(receiver))
         pad_ref[8 : 8 + depth, :] = product
@@ -200,29 +201,30 @@
         )
 
 
-def image_near_kernel(sides_ref, near_ref, receiver_ref, receiver_depth_ref, image_ref, pad_ref):
-    image_half(True, sides_ref, near_ref, receiver_ref, receiver_depth_ref, image_ref, pad_ref, 0, REACH)
+def image_near_kernel(sides_ref, near_ref, receiver_ref, receiver_depth_ref, image_ref, field_ref, pad_ref):
+    def keep(j, field):
+        field_ref[j] = field
+
+    image_half(True, sides_ref, near_ref, receiver_ref, receiver_depth_ref, image_ref, pad_ref, 0, REACH, keep)
 
 
 def last_kernel(
-    sides_ref, base_ref, coef_ref, halo_ref, receiver_ref, receiver_depth_ref, part_ref, far_ref, image_ref, pad_ref
+    sides_ref, base_ref, coef_ref, halo_ref, receiver_ref, receiver_depth_ref, part_ref, field_ref,
+    p_ref, image_ref, far_ref, pad_ref,
 ):
     add_halo(base_ref, coef_ref, halo_ref, far_ref)
+    odd = sides_ref[0:1, :]
     width = 2 * REACH
     depth = part_ref.shape[0] // REACH
-    image_half(False, sides_ref, far_ref, receiver_ref, receiver_depth_ref, image_ref, pad_ref, REACH, width)
+
+    def keep(j, far):
+        near = field_ref[j]
+        p_ref[pl.ds(j, depth, stride=width), :] = choose(odd, far.shape, near, far)
+        p_ref[pl.ds(REACH + j, depth, stride=width), :] = choose(odd, far.shape, far, near)
+
+    image_half(False, sides_ref, far_ref, receiver_ref, receiver_depth_ref, image_ref, pad_ref, REACH, width, keep)
     for j in range(REACH):
         image_ref[pl.ds(j, depth, stride=width), :] = part_ref[pl.ds(j, depth, stride=REACH), :]
-
-
-def final_kernel(sides_ref, near_ref, far_ref, p_ref):
-    odd = sides_ref[0:1, :]
-    width = 2 * REACH
-    depth = p_ref.shape[0] // width
-    for i in range(REACH):
-        near, far = near_ref[i], far_ref[i]
-        p_ref[pl.ds(REACH + i, depth, stride=width), :] = choose(odd, near.shape, far, near).T
-        p_ref[pl.ds(REACH - 1 - i, depth, stride=width), :] = choose(odd, near.shape, near, far).T
 
 
 def join_kernel(levels, parts_ref, image_ref):
@@ -319,25 +321,28 @@
                 outer_kernel, (half, rims), (sides, base, far_coef, far_halo, near_next), name=f"far{step}"
             )
         else:
-            part = kernel(
+            part, field = kernel(
                 image_near_kernel,
-                jax.ShapeDtypeStruct((depth * REACH, length), F32),
+                (
+                    jax.ShapeDtypeStruct((depth * REACH, length), F32),
+                    jax.ShapeDtypeStruct((REACH, depth, length), F32),
+                ),
                 (sides, near_next, receiver, receiver_depth),
                 pad,
                 "image_near",
             )
-            far_next, filtered = kernel(
+            final, filtered = kernel(
                 last_kernel,
-                (half, whole),
-                (sides, base, far_coef, far_halo, receiver, receiver_depth, part),
-                pad,
+                (whole, whole),
+                (sides, base, far_coef, far_halo, receiver, receiver_depth, part, field),
+                (pltpu.VMEM((REACH, length, depth), F32),) + pad,
                 f"far{step}",
             )
+            break
         near_prior, far_prior = near, far
         near, far = near_next, far_next
     levels = depth // size
     parts = lax.all_to_all(filtered, "gx", split_axis=0, concat_axis=0, tiled=True)
-    final = kernel(final_kernel, whole, (sides, near, far), name="final")
     image = kernel(
         functools.partial(join_kernel, levels),
         jax.ShapeDtypeStruct((levels, size * width, length), F32),

time: 178 us -> 178 us (level)
  blocking collectives: 0 us -> 92.8 us
  waiting for transfers between devices: 99.1 us -> 39.6 us
  starting transfers between devices: 61.2 us -> 28.7 us
    all_to_all x0 -> x1, blocking collectives: none -> 92.8 us  [shards(): lax.all_to_all(filtered, 'gx', split_axis=0, concat_axis=0, tiled=True)]
    all_to_all x1 -> x0, waiting for transfers between devices: 59.5 us -> none  [shards(): lax.all_to_all(filtered, 'gx', split_axis=0, concat_axis=0, tiled=True)]
    all_to_all x1 -> x0, starting transfers between devices: 32.5 us -> none  [shards(): lax.all_to_all(filtered, 'gx', split_axis=0, concat_axis=0, tiled=True)]
    pallas_call x30 -> x29, Pallas kernels: 13.5 us -> 12.7 us  [kernel(): pl.pallas_call(body, out_shape=outs, in_specs=[VM] * len(inputs), out_spe...]
  transfers between devices with their start and end apart: 25 -> 24, of which waited for: 16 -> 15; matrix products, arithmetic and copies ran while one was open for 0% -> 0% of each run, Pallas kernels for 6% -> 6%
where the time goes in v9:
time: 178 us; the launch traced here: 177 us
  blocking collectives  92.8 us (52%)
  waiting for transfers between devices  39.6 us (22%)
  starting transfers between devices  28.7 us (16%)
  Pallas kernels  12.7 us (7%)
  local copies, waits for them, and re-layouts  2.36 us (1%)
    all_to_all x1, blocking collectives, shards(): lax.all_to_all(filtered, 'gx', split_axis=0, concat_axis=0, tiled=True)  92.8 us
    ppermute x8, waiting for transfers between devices, shards(): near_halo = lax.ppermute(near, 'gx', near_pairs)  31.5 us
    ppermute x8, starting transfers between devices, shards(): near_halo = lax.ppermute(near, 'gx', near_pairs)  22 us
    pallas_call x29, Pallas kernels, kernel(): pl.pallas_call(body, out_shape=outs, in_specs=[VM] * len(inputs), out_spe...  12.7 us
    ppermute x8, waiting for transfers between devices, shards(): edge_in = lax.ppermute(edge, 'gy', rim_pairs)  8.1 us
    ppermute x8, starting transfers between devices, shards(): far_halo = lax.ppermute(far, 'gx', far_pairs)  5.55 us
  transfers between devices with their start and end apart: 24, of which 15 were waited for; matrix products, arithmetic and copies ran while one was open for 0% of the time, Pallas kernels for 6%

profile of v9, /device:TPU:46, one launch (start us, length us, event | category | flops | bytes accessed | tf_op | source)
XLA Modules:
  0.0 177.1 jit_solution(14393336020204291698)
XLA Ops:
  0.7 1.0 copy-done.1
  1.9 2.2 %collective-permute-start.1 = (f32[4,128,128]{2,1,0:T(8,128)S(1)}, f32[4,128,128]{2,1,0:T(8,128)S(1)}, u32[]{:S(2)}, u32[]{:S(2)}) collective-permute-start(f32[4,128,128]{2,1,0:T(8,128)S(1)} %open_near.1.near_ref.self_ref.other_ref.prior_ref), channel_id=1, source_target_pairs={{0,2},{4,6},{8,10},{12,14},{16,18},{20,22},{24,26},{28,30},{32,34}... | collective-permute-start | bytes 786440 | tf_op jit(solution)/shard_map/ppermute | solution.py:302
  4.3 0.8 collective-permute-start.2
  5.9 0.6 copy-done.4
  6.5 0.6 tables.1
  7.1 3.4 %collective-permute-done.1.halo_ref = f32[4,128,128]{2,1,0:T(8,128)S(1)} collective-permute-done((f32[4,128,128]{2,1,0:T(8,128)S(1)}, f32[4,128,128]{2,1,0:T(8,128)S(1)}, u32[]{:S(2)}, u32[]{:S(2)}) %collective-permute-start.1) | collective-permute-done | bytes 262176 | tf_op jit(solution)/shard_map/ppermute | solution.py:302
  10.6 0.6 near0.1.rest_5_.near_ref.self_ref.other_ref.prior_ref
  11.2 2.2 %collective-permute-start.4 = (f32[4,128,128]{2,1,0:T(8,128)S(1)}, f32[4,128,128]{2,1,0:T(8,128)S(1)}, u32[]{:S(2)}, u32[]{:S(2)}) collective-permute-start(f32[4,128,128]{2,1,0:T(8,128)S(1)} %near0.1.rest_5_.near_ref.self_ref.other_ref.prior_ref), channel_id=1, source_target_pairs={{0,2},{4,6},{8,10},{12,14},{16,18},{20,22},{24,26},{28,30},{32,34}... | collective-permute-start | bytes 786440 | tf_op jit(solution)/shard_map/ppermute | solution.py:302
  13.4 0.6 inner0.1.base_ref
  14.0 0.7 collective-permute-start.5
  14.9 1.2 collective-permute-done.3.rim_in_ref.rest_0_
  16.0 3.9 %collective-permute-done.4.halo_ref = f32[4,128,128]{2,1,0:T(8,128)S(1)} collective-permute-done((f32[4,128,128]{2,1,0:T(8,128)S(1)}, f32[4,128,128]{2,1,0:T(8,128)S(1)}, u32[]{:S(2)}, u32[]{:S(2)}) %collective-permute-start.4) | collective-permute-done | bytes 262176 | tf_op jit(solution)/shard_map/ppermute | solution.py:302
  19.9 0.6 near1.1.rest_5_.near_ref.self_ref.other_ref.prior_ref
  20.5 3.0 %collective-permute-start.7 = (f32[4,128,128]{2,1,0:T(8,128)S(1)}, f32[4,128,128]{2,1,0:T(8,128)S(1)}, u32[]{:S(2)}, u32[]{:S(2)}) collective-permute-start(f32[4,128,128]{2,1,0:T(8,128)S(1)} %near1.1.rest_5_.near_ref.self_ref.other_ref.prior_ref), channel_id=1, source_target_pairs={{0,2},{4,6},{8,10},{12,14},{16,18},{20,22},{24,26},{28,30},{32,34}... | collective-permute-start | bytes 786440 | tf_op jit(solution)/shard_map/ppermute | solution.py:302
  23.4 0.5 inner1.1.base_ref
  24.1 0.7 collective-permute-start.8
  24.9 1.2 collective-permute-done.6.rim_in_ref.rest_0_
  26.1 4.0 %collective-permute-done.7.halo_ref = f32[4,128,128]{2,1,0:T(8,128)S(1)} collective-permute-done((f32[4,128,128]{2,1,0:T(8,128)S(1)}, f32[4,128,128]{2,1,0:T(8,128)S(1)}, u32[]{:S(2)}, u32[]{:S(2)}) %collective-permute-start.7) | collective-permute-done | bytes 262176 | tf_op jit(solution)/shard_map/ppermute | solution.py:302
  30.1 0.6 near2.1.rest_5_.near_ref.self_ref.other_ref.prior_ref
  30.7 3.1 %collective-permute-start.10 = (f32[4,128,128]{2,1,0:T(8,128)S(1)}, f32[4,128,128]{2,1,0:T(8,128)S(1)}, u32[]{:S(2)}, u32[]{:S(2)}) collective-permute-start(f32[4,128,128]{2,1,0:T(8,128)S(1)} %near2.1.rest_5_.near_ref.self_ref.other_ref.prior_ref), channel_id=1, source_target_pairs={{0,2},{4,6},{8,10},{12,14},{16,18},{20,22},{24,26},{28,30},{32,34}... | collective-permute-start | bytes 786440 | tf_op jit(solution)/shard_map/ppermute | solution.py:302
  34.4 0.7 collective-permute-start.11
  35.2 1.2 collective-permute-done.9.rim_in_ref.rest_0_
  36.4 4.0 %collective-permute-done.10.halo_ref = f32[4,128,128]{2,1,0:T(8,128)S(1)} collective-permute-done((f32[4,128,128]{2,1,0:T(8,128)S(1)}, f32[4,128,128]{2,1,0:T(8,128)S(1)}, u32[]{:S(2)}, u32[]{:S(2)}) %collective-permute-start.10) | collective-permute-done | bytes 262176 | tf_op jit(solution)/shard_map/ppermute | solution.py:302
  40.4 0.6 near3.1.rest_5_.near_ref.self_ref.other_ref.prior_ref
  41.0 2.9 %collective-permute-start.13 = (f32[4,128,128]{2,1,0:T(8,128)S(1)}, f32[4,128,128]{2,1,0:T(8,128)S(1)}, u32[]{:S(2)}, u32[]{:S(2)}) collective-permute-start(f32[4,128,128]{2,1,0:T(8,128)S(1)} %near3.1.rest_5_.near_ref.self_ref.other_ref.prior_ref), channel_id=1, source_target_pairs={{0,2},{4,6},{8,10},{12,14},{16,18},{20,22},{24,26},{28,30},{32,34}... | collective-permute-start | bytes 786440 | tf_op jit(solution)/shard_map/ppermute | solution.py:302
  44.6 0.7 collective-permute-start.14
  45.4 1.2 collective-permute-done.12.rim_in_ref.rest_0_
  46.6 4.0 %collective-permute-done.13.halo_ref = f32[4,128,128]{2,1,0:T(8,128)S(1)} collective-permute-done((f32[4,128,128]{2,1,0:T(8,128)S(1)}, f32[4,128,128]{2,1,0:T(8,128)S(1)}, u32[]{:S(2)}, u32[]{:S(2)}) %collective-permute-start.13) | collective-permute-done | bytes 262176 | tf_op jit(solution)/shard_map/ppermute | solution.py:302
  50.6 0.6 near4.1.rest_5_.near_ref.self_ref.other_ref.prior_ref
  51.2 3.0 %collective-permute-start.16 = (f32[4,128,128]{2,1,0:T(8,128)S(1)}, f32[4,128,128]{2,1,0:T(8,128)S(1)}, u32[]{:S(2)}, u32[]{:S(2)}) collective-permute-start(f32[4,128,128]{2,1,0:T(8,128)S(1)} %near4.1.rest_5_.near_ref.self_ref.other_ref.prior_ref), channel_id=1, source_target_pairs={{0,2},{4,6},{8,10},{12,14},{16,18},{20,22},{24,26},{28,30},{32,34}... | collective-permute-start | bytes 786440 | tf_op jit(solution)/shard_map/ppermute | solution.py:302
  54.8 0.7 collective-permute-start.17
  55.7 1.2 collective-permute-done.15.rim_in_ref.rest_0_
  56.8 4.0 %collective-permute-done.16.halo_ref = f32[4,128,128]{2,1,0:T(8,128)S(1)} collective-permute-done((f32[4,128,128]{2,1,0:T(8,128)S(1)}, f32[4,128,128]{2,1,0:T(8,128)S(1)}, u32[]{:S(2)}, u32[]{:S(2)}) %collective-permute-start.16) | collective-permute-done | bytes 262176 | tf_op jit(solution)/shard_map/ppermute | solution.py:302
  60.9 0.6 near5.1.rest_5_.near_ref.self_ref.other_ref.prior_ref
  61.5 2.7 %collective-permute-start.19 = (f32[4,128,128]{2,1,0:T(8,128)S(1)}, f32[4,128,128]{2,1,0:T(8,128)S(1)}, u32[]{:S(2)}, u32[]{:S(2)}) collective-permute-start(f32[4,128,128]{2,1,0:T(8,128)S(1)} %near5.1.rest_5_.near_ref.self_ref.other_ref.prior_ref), channel_id=1, source_target_pairs={{0,2},{4,6},{8,10},{12,14},{16,18},{20,22},{24,26},{28,30},{32,34}... | collective-permute-start | bytes 786440 | tf_op jit(solution)/shard_map/ppermute | solution.py:302
  64.8 0.7 collective-permute-start.20
  65.6 1.2 collective-permute-done.18.rim_in_ref.rest_0_
  66.8 4.0 %collective-permute-done.19.halo_ref = f32[4,128,128]{2,1,0:T(8,128)S(1)} collective-permute-done((f32[4,128,128]{2,1,0:T(8,128)S(1)}, f32[4,128,128]{2,1,0:T(8,128)S(1)}, u32[]{:S(2)}, u32[]{:S(2)}) %collective-permute-start.19) | collective-permute-done | bytes 262176 | tf_op jit(solution)/shard_map/ppermute | solution.py:302
  70.8 0.6 near6.1.rest_5_.near_ref.self_ref.other_ref
  71.4 2.9 %collective-permute-start.22 = (f32[4,128,128]{2,1,0:T(8,128)S(1)}, f32[4,128,128]{2,1,0:T(8,128)S(1)}, u32[]{:S(2)}, u32[]{:S(2)}) collective-permute-start(f32[4,128,128]{2,1,0:T(8,128)S(1)} %near6.1.rest_5_.near_ref.self_ref.other_ref), channel_id=1, source_target_pairs={{0,2},{4,6},{8,10},{12,14},{16,18},{20,22},{24,26},{28,30},{32,34}... | collective-permute-start | bytes 786440 | tf_op jit(solution)/shard_map/ppermute | solution.py:302
  74.9 0.7 collective-permute-start.23
  75.7 1.2 collective-permute-done.21.rim_in_ref.rest_0_
  76.9 4.0 %collective-permute-done.22.halo_ref = f32[4,128,128]{2,1,0:T(8,128)S(1)} collective-permute-done((f32[4,128,128]{2,1,0:T(8,128)S(1)}, f32[4,128,128]{2,1,0:T(8,128)S(1)}, u32[]{:S(2)}, u32[]{:S(2)}) %collective-permute-start.22) | collective-permute-done | bytes 262176 | tf_op jit(solution)/shard_map/ppermute | solution.py:302
  80.9 0.6 near7.1.rest_5_.near_ref
  81.8 0.5 inner7.1.base_ref
  82.3 1.1 far7.1
  83.5 92.8 %all_to_all.11 = f32[32,32,128]{2,1,0:T(8,128)S(1)} all-to-all(f32[32,32,128]{2,1,0:T(8,128)S(1)} %bitcast.15), channel_id=1, replica_groups=mesh['shots'=4,'gx'=32,'gy'=2] {'gx'}, dimensions={0} | all-to-all | bytes 1048576 | tf_op jit(solution)/shard_map/all_to_all | solution.py:345
  176.3 0.8 join.1
  (50 shorter events, 5.6 us)
Async XLA Ops:
  0.7 1.0 copy-start.1
  1.9 3.4 %copy-start.6 = (bf16[128,8,128]{2,1,0:T(8,128)(2,1)S(1)}, bf16[128,8,128]{2,1,0:T(8,128)(2,1)}, u32[]{:S(2)}) copy-start(bf16[128,8,128]{2,1,0:T(8,128)(2,1)} %param.10) | copy-start | bytes 786436
  1.9 8.6 %collective-permute-start.1 = (f32[4,128,128]{2,1,0:T(8,128)S(1)}, f32[4,128,128]{2,1,0:T(8,128)S(1)}, u32[]{:S(2)}, u32[]{:S(2)}) collective-permute-start(f32[4,128,128]{2,1,0:T(8,128)S(1)} %open_near.1.near_ref.self_ref.other_ref.prior_ref), channel_id=1, source_target_pairs={{0,2},{4,6},{8,10},{12,14},{16,18},{20,22},{24,26},{28,30},{32,34}... | collective-permute-start | bytes 786440 | tf_op jit(solution)/shard_map/ppermute | solution.py:302
  4.3 1.6 copy-start.2
  4.3 9.6 %collective-permute-start.2 = (f32[4,128,128]{2,1,0:T(8,128)S(1)}, f32[4,128,128]{2,1,0:T(8,128)S(1)}, u32[]{:S(2)}, u32[]{:S(2)}) collective-permute-start(f32[4,128,128]{2,1,0:T(8,128)S(1)} %get-tuple-element.29.other_ref.self_ref.rest_1_), channel_id=1, source_target_pairs={{2,4},{6,8},{10,12},{14,16},{18,20},{22,24},{26,28},{30,32},{34,36... | collective-permute-start | bytes 786440 | tf_op jit(solution)/shard_map/ppermute | solution.py:303
  5.1 0.7 copy-start.7
  5.2 2.0 %collective-permute-start = (f32[8,4,128]{2,1,0:T(4,128)S(1)}, f32[8,4,128]{2,1,0:T(4,128)S(1)}, u32[]{:S(2)}, u32[]{:S(2)}) collective-permute-start(f32[8,4,128]{2,1,0:T(4,128)S(1)} %get-tuple-element.30), channel_id=1, source_target_pairs={{0,1},{1,0},{2,3},{3,2},{4,5},{5,4},{6,7},{7,6},{8,9},{9,8},{10,11... | collective-permute-start | bytes 49160 | tf_op jit(solution)/shard_map/ppermute | solution.py:304
  5.8 0.7 copy-start.4
  5.8 0.7 copy-start.5
  11.2 8.7 %collective-permute-start.4 = (f32[4,128,128]{2,1,0:T(8,128)S(1)}, f32[4,128,128]{2,1,0:T(8,128)S(1)}, u32[]{:S(2)}, u32[]{:S(2)}) collective-permute-start(f32[4,128,128]{2,1,0:T(8,128)S(1)} %near0.1.rest_5_.near_ref.self_ref.other_ref.prior_ref), channel_id=1, source_target_pairs={{0,2},{4,6},{8,10},{12,14},{16,18},{20,22},{24,26},{28,30},{32,34}... | collective-permute-start | bytes 786440 | tf_op jit(solution)/shard_map/ppermute | solution.py:302
  14.0 10.0 %collective-permute-start.5 = (f32[4,128,128]{2,1,0:T(8,128)S(1)}, f32[4,128,128]{2,1,0:T(8,128)S(1)}, u32[]{:S(2)}, u32[]{:S(2)}) collective-permute-start(f32[4,128,128]{2,1,0:T(8,128)S(1)} %get-tuple-element.38.other_ref.self_ref.rest_1_), channel_id=1, source_target_pairs={{2,4},{6,8},{10,12},{14,16},{18,20},{22,24},{26,28},{30,32},{34,36... | collective-permute-start | bytes 786440 | tf_op jit(solution)/shard_map/ppermute | solution.py:303
  14.7 1.3 collective-permute-start.3
  20.5 9.6 %collective-permute-start.7 = (f32[4,128,128]{2,1,0:T(8,128)S(1)}, f32[4,128,128]{2,1,0:T(8,128)S(1)}, u32[]{:S(2)}, u32[]{:S(2)}) collective-permute-start(f32[4,128,128]{2,1,0:T(8,128)S(1)} %near1.1.rest_5_.near_ref.self_ref.other_ref.prior_ref), channel_id=1, source_target_pairs={{0,2},{4,6},{8,10},{12,14},{16,18},{20,22},{24,26},{28,30},{32,34}... | collective-permute-start | bytes 786440 | tf_op jit(solution)/shard_map/ppermute | solution.py:302
  24.1 10.2 %collective-permute-start.8 = (f32[4,128,128]{2,1,0:T(8,128)S(1)}, f32[4,128,128]{2,1,0:T(8,128)S(1)}, u32[]{:S(2)}, u32[]{:S(2)}) collective-permute-start(f32[4,128,128]{2,1,0:T(8,128)S(1)} %get-tuple-element.40.other_ref.self_ref.rest_1_), channel_id=1, source_target_pairs={{2,4},{6,8},{10,12},{14,16},{18,20},{22,24},{26,28},{30,32},{34,36... | collective-permute-start | bytes 786440 | tf_op jit(solution)/shard_map/ppermute | solution.py:303
  24.8 1.3 collective-permute-start.6
  30.7 9.7 %collective-permute-start.10 = (f32[4,128,128]{2,1,0:T(8,128)S(1)}, f32[4,128,128]{2,1,0:T(8,128)S(1)}, u32[]{:S(2)}, u32[]{:S(2)}) collective-permute-start(f32[4,128,128]{2,1,0:T(8,128)S(1)} %near2.1.rest_5_.near_ref.self_ref.other_ref.prior_ref), channel_id=1, source_target_pairs={{0,2},{4,6},{8,10},{12,14},{16,18},{20,22},{24,26},{28,30},{32,34}... | collective-permute-start | bytes 786440 | tf_op jit(solution)/shard_map/ppermute | solution.py:302
  34.4 10.1 %collective-permute-start.11 = (f32[4,128,128]{2,1,0:T(8,128)S(1)}, f32[4,128,128]{2,1,0:T(8,128)S(1)}, u32[]{:S(2)}, u32[]{:S(2)}) collective-permute-start(f32[4,128,128]{2,1,0:T(8,128)S(1)} %get-tuple-element.42.other_ref.self_ref.rest_1_), channel_id=1, source_target_pairs={{2,4},{6,8},{10,12},{14,16},{18,20},{22,24},{26,28},{30,32},{34,36... | collective-permute-start | bytes 786440 | tf_op jit(solution)/shard_map/ppermute | solution.py:303
  35.1 1.3 collective-permute-start.9
  41.0 9.6 %collective-permute-start.13 = (f32[4,128,128]{2,1,0:T(8,128)S(1)}, f32[4,128,128]{2,1,0:T(8,128)S(1)}, u32[]{:S(2)}, u32[]{:S(2)}) collective-permute-start(f32[4,128,128]{2,1,0:T(8,128)S(1)} %near3.1.rest_5_.near_ref.self_ref.other_ref.prior_ref), channel_id=1, source_target_pairs={{0,2},{4,6},{8,10},{12,14},{16,18},{20,22},{24,26},{28,30},{32,34}... | collective-permute-start | bytes 786440 | tf_op jit(solution)/shard_map/ppermute | solution.py:302
  44.6 10.2 %collective-permute-start.14 = (f32[4,128,128]{2,1,0:T(8,128)S(1)}, f32[4,128,128]{2,1,0:T(8,128)S(1)}, u32[]{:S(2)}, u32[]{:S(2)}) collective-permute-start(f32[4,128,128]{2,1,0:T(8,128)S(1)} %get-tuple-element.44.other_ref.self_ref.rest_1_), channel_id=1, source_target_pairs={{2,4},{6,8},{10,12},{14,16},{18,20},{22,24},{26,28},{30,32},{34,36... | collective-permute-start | bytes 786440 | tf_op jit(solution)/shard_map/ppermute | solution.py:303
  45.3 1.3 collective-permute-start.12
  51.2 9.7 %collective-permute-start.16 = (f32[4,128,128]{2,1,0:T(8,128)S(1)}, f32[4,128,128]{2,1,0:T(8,128)S(1)}, u32[]{:S(2)}, u32[]{:S(2)}) collective-permute-start(f32[4,128,128]{2,1,0:T(8,128)S(1)} %near4.1.rest_5_.near_ref.self_ref.other_ref.prior_ref), channel_id=1, source_target_pairs={{0,2},{4,6},{8,10},{12,14},{16,18},{20,22},{24,26},{28,30},{32,34}... | collective-permute-start | bytes 786440 | tf_op jit(solution)/shard_map/ppermute | solution.py:302
  54.8 9.9 %collective-permute-start.17 = (f32[4,128,128]{2,1,0:T(8,128)S(1)}, f32[4,128,128]{2,1,0:T(8,128)S(1)}, u32[]{:S(2)}, u32[]{:S(2)}) collective-permute-start(f32[4,128,128]{2,1,0:T(8,128)S(1)} %get-tuple-element.46.other_ref.self_ref.rest_1_), channel_id=1, source_target_pairs={{2,4},{6,8},{10,12},{14,16},{18,20},{22,24},{26,28},{30,32},{34,36... | collective-permute-start | bytes 786440 | tf_op jit(solution)/shard_map/ppermute | solution.py:303
  55.5 1.3 collective-permute-start.15
  61.5 9.4 %collective-permute-start.19 = (f32[4,128,128]{2,1,0:T(8,128)S(1)}, f32[4,128,128]{2,1,0:T(8,128)S(1)}, u32[]{:S(2)}, u32[]{:S(2)}) collective-permute-start(f32[4,128,128]{2,1,0:T(8,128)S(1)} %near5.1.rest_5_.near_ref.self_ref.other_ref.prior_ref), channel_id=1, source_target_pairs={{0,2},{4,6},{8,10},{12,14},{16,18},{20,22},{24,26},{28,30},{32,34}... | collective-permute-start | bytes 786440 | tf_op jit(solution)/shard_map/ppermute | solution.py:302
  64.8 10.0 %collective-permute-start.20 = (f32[4,128,128]{2,1,0:T(8,128)S(1)}, f32[4,128,128]{2,1,0:T(8,128)S(1)}, u32[]{:S(2)}, u32[]{:S(2)}) collective-permute-start(f32[4,128,128]{2,1,0:T(8,128)S(1)} %get-tuple-element.48.other_ref.self_ref.rest_1_), channel_id=1, source_target_pairs={{2,4},{6,8},{10,12},{14,16},{18,20},{22,24},{26,28},{30,32},{34,36... | collective-permute-start | bytes 786440 | tf_op jit(solution)/shard_map/ppermute | solution.py:303
  65.5 1.3 collective-permute-start.18
  71.4 9.5 %collective-permute-start.22 = (f32[4,128,128]{2,1,0:T(8,128)S(1)}, f32[4,128,128]{2,1,0:T(8,128)S(1)}, u32[]{:S(2)}, u32[]{:S(2)}) collective-permute-start(f32[4,128,128]{2,1,0:T(8,128)S(1)} %near6.1.rest_5_.near_ref.self_ref.other_ref), channel_id=1, source_target_pairs={{0,2},{4,6},{8,10},{12,14},{16,18},{20,22},{24,26},{28,30},{32,34}... | collective-permute-start | bytes 786440 | tf_op jit(solution)/shard_map/ppermute | solution.py:302
  74.9 7.5 %collective-permute-start.23 = (f32[4,128,128]{2,1,0:T(8,128)S(1)}, f32[4,128,128]{2,1,0:T(8,128)S(1)}, u32[]{:S(2)}, u32[]{:S(2)}) collective-permute-start(f32[4,128,128]{2,1,0:T(8,128)S(1)} %get-tuple-element.50.other_ref.self_ref), channel_id=1, source_target_pairs={{2,4},{6,8},{10,12},{14,16},{18,20},{22,24},{26,28},{30,32},{34,36... | collective-permute-start | bytes 786440 | tf_op jit(solution)/shard_map/ppermute | solution.py:303
  75.6 5.9 %copy-start = (f32[128,8,128]{2,1,0:T(8,128)S(1)}, f32[128,8,128]{2,1,0:T(8,128)}, u32[]{:S(2)}) copy-start(f32[128,8,128]{2,1,0:T(8,128)} %param.15) | copy-start | bytes 1572868
  75.6 1.3 collective-permute-start.21
  80.9 0.7 copy-start.3
